TPU v7x, 32 devices: a whole 2x2x4 slice. The times are simulated.
32 devices in a mesh: dom: 32 (over z, y, x, core).
Axes of the slice: x: 2, y: 2, z: 4, core: 2. Of those that a mesh axis runs over, the one named last changes fastest.
Arguments:
- features: bfloat16 [32768, 256], P('dom'), may hold values from -6 to 6
- edge_source: int32 [32, 128, 128], P('dom'), may hold values from 0 to 2047, as said below
- edge_relation: int32 [32, 128, 128], P('dom'), may hold values from 0 to 7
- edge_target: int32 [32, 128, 128], P('dom'), may hold values from 0 to 1023, as said below
- block_count: int32 [32], P('dom'), may hold values from 1 to 128, as said below
- send_list: int32 [32, 32, 32], P('dom'), may hold values from 0 to 1023
- bases_first: bfloat16 [30, 256, 256], P(None, 'dom'), may hold values from -0.375 to 0.375
- self_first: bfloat16 [256, 256], P('dom'), may hold values from -0.375 to 0.375
- coef_first: float32 [8, 30], replicated, may hold values from -1 to 1
- bias_first: float32 [256], replicated, may hold values from -3 to 3
- bases_second: bfloat16 [30, 256, 256], P(None, 'dom'), may hold values from -0.375 to 0.375
- self_second: bfloat16 [256, 256], P('dom'), may hold values from -0.375 to 0.375
- coef_second: float32 [8, 30], replicated, may hold values from -1 to 1
- bias_second: float32 [256], replicated, may hold values from -3 to 3
Outputs:
- embedded: bfloat16 [32768, 256], P('dom')
Inputs may be any that keep to these rules, and one draw needn't show every extreme that they name: `edge_source`: an entry below 1024 names a row of the edge's own partition; an entry 1024 + p * 32 + s names the row that partition p sends to the edge's partition in slot s, and p is never the edge's own partition. `edge_target`: non-decreasing within each block; all targets of one block lie in one aligned window of 16 rows, from 16 * k to 16 * k + 15 for some k. `block_count`: blocks at and beyond it are ignored; some partition uses all 128.
All inputs are finite; a program needn't handle non-finite values.
Results may differ from a plain program's by a relative error of at most 0.0064.
Values may be sent and summed in bfloat16 or wider, within the bound.
No kernel may reach another device: no remote copies, remote signals or barrier semaphores. Data moves between devices by JAX's collectives and lax.ppermute only.
A program may use at most 128 MiB of HBM per device.

v0:
```python
import functools

import jax
import jax.numpy as jnp
from jax import lax
from jax.experimental import pallas as pl
from jax.experimental.pallas import tpu as pltpu
from jax.sharding import PartitionSpec as P

WIN = 16
CHUNK = 512
MIB = 1 << 20
RESIDENT_MAX = 36 * MIB
CONTRACT_LANES = (((1,), (1,)), ((), ()))


def estimate(flops, nbytes):
    return pl.CostEstimate(flops=int(flops), bytes_accessed=int(nbytes), transcendentals=0)


def params(mib, **more):
    return pltpu.CompilerParams(vmem_limit_bytes=mib * MIB, **more)


def hot(rows, lanes):
    row_ids = lax.broadcasted_iota(jnp.int32, (rows, lanes.shape[1]), 0)
    return jnp.where(row_ids == lanes, 1.0, 0.0)


def code_edges(source_ref, relation_ref, target_ref, slot_ref, code_ref, low_ref, relations):
    slot = relation_ref[...] * WIN + (target_ref[...] & (WIN - 1))
    slot_ref[...] = slot
    code_ref[...] = (source_ref[...] // CHUNK) * (WIN * relations) + slot
    low_ref[...] = source_ref[...] & (CHUNK - 1)


def link_blocks(tile_ref, count_ref, head_ref, next_ref, tiles):
    def clear(t, carry):
        head_ref[t] = -1
        return carry

    lax.fori_loop(0, tiles, clear, 0)

    def link(b, carry):
        t = tile_ref[b] // WIN
        next_ref[b] = head_ref[t]
        head_ref[t] = b
        return carry

    lax.fori_loop(0, count_ref[0], link, 0)


def pair_of(first, next_ref):
    second = jnp.where(first >= 0, next_ref[jnp.maximum(first, 0)], -1)
    after = jnp.where(second >= 0, next_ref[jnp.maximum(second, 0)], -1)
    return second, after


def pair_rows(ref, first, second):
    one = jnp.where(first >= 0, ref[pl.ds(jnp.maximum(first, 0), 1), :], -1)
    two = jnp.where(second >= 0, ref[pl.ds(jnp.maximum(second, 0), 1), :], -1)
    return jnp.concatenate([one, two], axis=1)


def pair_counts(first, second, slot_ref, code_ref, low_ref, rows, slots):
    left = hot(rows, pair_rows(code_ref, first, second)).astype(jnp.bfloat16)
    right = hot(CHUNK, pair_rows(low_ref, first, second)).astype(jnp.bfloat16)
    counts = lax.dot_general(left, right, CONTRACT_LANES, preferred_element_type=jnp.float32)
    degree = jnp.sum(hot(slots, pair_rows(slot_ref, first, second)), axis=1, keepdims=True)
    return counts, degree


def put_counts(counts, local_ref, remote_ref, row, slots, locals_):
    for piece in range(counts.shape[0] // slots):
        part = counts[piece * slots : (piece + 1) * slots].astype(jnp.bfloat16)
        if piece < locals_:
            local_ref[pl.ds(row, slots), pl.ds(piece * CHUNK, CHUNK)] = part
        else:
            remote_ref[pl.ds(row, slots), pl.ds((piece - locals_) * CHUNK, CHUNK)] = part


def build_resident(
    tile_ref, count_ref, source_ref, relation_ref, target_ref,
    local_ref, remote_ref, degree_ref,
    head_ref, next_ref, slot_ref, code_ref, low_ref, sum_ref,
    *, tiles, relations, locals_, pieces, unroll,
):
    slots = WIN * relations
    rows = pieces * slots
    code_edges(source_ref, relation_ref, target_ref, slot_ref, code_ref, low_ref, relations)
    link_blocks(tile_ref, count_ref, head_ref, next_ref, tiles)

    def base(i, carry):
        for u in range(unroll):
            t = i * unroll + u
            first = head_ref[t]
            second, after = pair_of(first, next_ref)
            counts, degree = pair_counts(first, second, slot_ref, code_ref, low_ref, rows, slots)
            row = pl.multiple_of(t * slots, slots)
            put_counts(counts, local_ref, remote_ref, row, slots, locals_)
            degree_ref[pl.ds(row, slots), :] = degree
            head_ref[t] = after
        return carry

    lax.fori_loop(0, tiles // unroll, base, 0)

    def rest(t, carry):
        @pl.when(head_ref[t] >= 0)
        def _():
            row = pl.multiple_of(t * slots, slots)
            for piece in range(pieces):
                ref, at = (local_ref, piece) if piece < locals_ else (remote_ref, piece - locals_)
                sum_ref[pl.ds(piece * slots, slots), :] = ref[
                    pl.ds(row, slots), pl.ds(at * CHUNK, CHUNK)
                ].astype(jnp.float32)

            def step(first):
                second, after = pair_of(first, next_ref)
                counts, degree = pair_counts(first, second, slot_ref, code_ref, low_ref, rows, slots)
                sum_ref[...] += counts
                degree_ref[pl.ds(row, slots), :] += degree
                return after

            lax.while_loop(lambda first: first >= 0, step, head_ref[t])
            put_counts(sum_ref[...], local_ref, remote_ref, row, slots, locals_)

        return carry

    lax.fori_loop(0, tiles, rest, 0)


def build_streamed(
    tile_ref, count_ref, source_ref, relation_ref, target_ref,
    local_ref, remote_ref, degree_ref,
    head_ref, next_ref, slot_ref, code_ref, low_ref, sum_ref,
    *, tiles, relations, locals_, pieces, unroll,
):
    slots = WIN * relations
    rows = pieces * slots
    t = pl.program_id(0)

    @pl.when(t == 0)
    def _():
        code_edges(source_ref, relation_ref, target_ref, slot_ref, code_ref, low_ref, relations)
        link_blocks(tile_ref, count_ref, head_ref, next_ref, tiles)

    sum_ref[...] = jnp.zeros_like(sum_ref)
    degree_ref[...] = jnp.zeros_like(degree_ref)

    def step(first):
        second, after = pair_of(first, next_ref)
        counts, degree = pair_counts(first, second, slot_ref, code_ref, low_ref, rows, slots)
        sum_ref[...] += counts
        degree_ref[...] += degree
        return after

    lax.while_loop(lambda first: first >= 0, step, head_ref[t])
    put_counts(sum_ref[...], local_ref, remote_ref, 0, slots, locals_)


def build(tile_of, count, source, relation, target, *, node_rows, relations, remote_rows, resident):
    blocks, width = source.shape
    tiles, slots = node_rows // WIN, WIN * relations
    locals_, remotes = node_rows // CHUNK, remote_rows // CHUNK
    pieces = locals_ + remotes
    smem = pl.BlockSpec(memory_space=pltpu.SMEM)
    settings = dict(tiles=tiles, relations=relations, locals_=locals_, pieces=pieces, unroll=2)
    shapes = [
        ((tiles * slots, node_rows), jnp.bfloat16),
        ((tiles * slots, remote_rows), jnp.bfloat16),
        ((tiles * slots, 1), jnp.float32),
    ]
    scratch = [
        pltpu.SMEM((tiles,), jnp.int32),
        pltpu.SMEM((blocks,), jnp.int32),
        pltpu.VMEM((blocks, width), jnp.int32),
        pltpu.VMEM((blocks, width), jnp.int32),
        pltpu.VMEM((blocks, width), jnp.int32),
        pltpu.VMEM((pieces * slots, CHUNK), jnp.float32),
    ]
    cost = estimate(
        2 * (tiles + blocks // 4) * pieces * slots * CHUNK * 2 * width,
        2 * tiles * slots * pieces * CHUNK,
    )
    args = (tile_of, count, source, relation, target)
    if resident:
        vmem = pl.BlockSpec(memory_space=pltpu.VMEM)
        return pl.pallas_call(
            functools.partial(build_resident, **settings),
            out_shape=[pltpu.VMEM(s, d) for s, d in shapes],
            in_specs=[smem, smem, vmem, vmem, vmem],
            out_specs=[vmem, vmem, vmem],
            scratch_shapes=scratch,
            compiler_params=params(12),
            cost_estimate=cost,
            name="build",
        )(*args)
    whole = pl.BlockSpec((blocks, width), lambda t: (0, 0))
    return pl.pallas_call(
        functools.partial(build_streamed, **settings),
        grid=(tiles,),
        out_shape=[jax.ShapeDtypeStruct(s, d) for s, d in shapes],
        in_specs=[smem, smem, whole, whole, whole],
        out_specs=[pl.BlockSpec((slots, s[1]), lambda t: (t, 0)) for s, _ in shapes],
        scratch_shapes=scratch,
        compiler_params=params(40),
        cost_estimate=cost,
        name="build",
    )(*args)


def apply_local_body(counts_ref, table_ref, pooled_ref, *, group):
    def step(i, carry):
        rows = pl.ds(pl.multiple_of(i * group, group), group)
        pooled_ref[rows, :] = jnp.dot(
            counts_ref[rows, :], table_ref[...], preferred_element_type=jnp.float32
        )
        return carry

    lax.fori_loop(0, counts_ref.shape[0] // group, step, 0)


def apply_local(counts, table, *, resident, group=512):
    rows, depth = counts.shape
    width = table.shape[1]
    cost = estimate(2 * rows * depth * width, 2 * rows * depth)
    if resident:
        vmem = pl.BlockSpec(memory_space=pltpu.VMEM)
        return pl.pallas_call(
            functools.partial(apply_local_body, group=group),
            out_shape=pltpu.VMEM((rows, width), jnp.float32),
            in_specs=[vmem, vmem],
            out_specs=vmem,
            compiler_params=params(6),
            cost_estimate=cost,
            name="local",
        )(counts, table)
    return pl.pallas_call(
        functools.partial(apply_local_body, group=group),
        grid=(rows // group,),
        out_shape=jax.ShapeDtypeStruct((rows, width), jnp.float32),
        in_specs=[
            pl.BlockSpec((group, depth), lambda i: (i, 0)),
            pl.BlockSpec((depth, width), lambda i: (0, 0)),
        ],
        out_specs=pl.BlockSpec((group, width), lambda i: (i, 0)),
        compiler_params=params(40),
        cost_estimate=cost,
        name="local",
    )(counts, table)


def apply_remote_body(
    counts_ref, table_ref, pooled_ref, degree_ref, mean_ref, *, group, relations
):
    slots = WIN * relations
    width = table_ref.shape[1]

    def step(i, carry):
        rows = pl.ds(pl.multiple_of(i * group, group), group)
        total = pooled_ref[rows, :] + jnp.dot(
            counts_ref[rows, :], table_ref[...], preferred_element_type=jnp.float32
        )
        mean = (total * (1.0 / jnp.maximum(degree_ref[rows, :], 1.0))).astype(jnp.bfloat16)
        for tile in range(group // slots):
            at = i * (group // slots) + tile
            for relation in range(relations):
                start = tile * slots + relation * WIN
                mean_ref[
                    pl.ds(pl.multiple_of(at * WIN, WIN), WIN), pl.ds(relation * width, width)
                ] = mean[start : start + WIN]
        return carry

    lax.fori_loop(0, counts_ref.shape[0] // group, step, 0)


def apply_remote(counts, table, pooled, degree, *, relations, resident, group=512):
    rows, depth = counts.shape
    width = table.shape[1]
    nodes = rows // relations
    body = functools.partial(apply_remote_body, group=group, relations=relations)
    cost = estimate(2 * rows * depth * width, 2 * rows * depth)
    if resident:
        vmem = pl.BlockSpec(memory_space=pltpu.VMEM)
        return pl.pallas_call(
            body,
            out_shape=pltpu.VMEM((nodes, relations * width), jnp.bfloat16),
            in_specs=[vmem] * 4,
            out_specs=vmem,
            compiler_params=params(6),
            cost_estimate=cost,
            name="remote",
        )(counts, table, pooled, degree)
    return pl.pallas_call(
        body,
        grid=(rows // group,),
        out_shape=jax.ShapeDtypeStruct((nodes, relations * width), jnp.bfloat16),
        in_specs=[
            pl.BlockSpec((group, depth), lambda i: (i, 0)),
            pl.BlockSpec((depth, width), lambda i: (0, 0)),
            pl.BlockSpec((group, width), lambda i: (i, 0)),
            pl.BlockSpec((group, 1), lambda i: (i, 0)),
        ],
        out_specs=pl.BlockSpec((group // relations, relations * width), lambda i: (i, 0)),
        compiler_params=params(40),
        cost_estimate=cost,
        name="remote",
    )(counts, table, pooled, degree)


def dense_sum(side_ref, mean_ref, own_ref, mine_ref, other_ref, bias_ref):
    half = other_ref.shape[0]
    mine_at = pl.multiple_of(side_ref[0] * half, half)
    other_at = pl.multiple_of((1 - side_ref[0]) * half, half)
    total = jnp.dot(
        mean_ref[:, pl.ds(mine_at, half)], mine_ref[:half], preferred_element_type=jnp.float32
    )
    total += jnp.dot(
        mean_ref[:, pl.ds(other_at, half)], other_ref[...], preferred_element_type=jnp.float32
    )
    total += jnp.dot(own_ref[...], mine_ref[half:], preferred_element_type=jnp.float32)
    return total + bias_ref[...]


def dense_first_body(
    side_ref, mean_ref, own_ref, mine_ref, other_ref, bias_ref, send_ref, hidden_ref, out_ref
):
    total = dense_sum(side_ref, mean_ref, own_ref, mine_ref, other_ref, bias_ref)
    hidden_ref[...] = jnp.maximum(total, 0.0).astype(jnp.bfloat16)
    pick_body(send_ref, hidden_ref, out_ref)


def dense_second_body(side_ref, mean_ref, own_ref, mine_ref, other_ref, bias_ref, out_ref):
    total = dense_sum(side_ref, mean_ref, own_ref, mine_ref, other_ref, bias_ref)
    out_ref[...] = total.astype(jnp.bfloat16)


def pick_body(send_ref, rows_ref, out_ref):
    depth = rows_ref.shape[0]
    piece = 256

    def step(i, carry):
        rows = pl.ds(pl.multiple_of(i * piece, piece), piece)
        lanes = lax.broadcasted_iota(jnp.int32, (piece, depth), 1)
        chosen = jnp.where(send_ref[rows, :] == lanes, 1.0, 0.0).astype(jnp.bfloat16)
        out_ref[rows, :] = jnp.dot(
            chosen, rows_ref[...], preferred_element_type=jnp.float32
        ).astype(jnp.bfloat16)
        return carry

    lax.fori_loop(0, send_ref.shape[0] // piece, step, 0)


def pick(send, rows):
    vmem = pl.BlockSpec(memory_space=pltpu.VMEM)
    return pl.pallas_call(
        pick_body,
        out_shape=jax.ShapeDtypeStruct((send.shape[0], rows.shape[1]), rows.dtype),
        in_specs=[vmem, vmem],
        out_specs=vmem,
        compiler_params=params(16),
        cost_estimate=estimate(2 * send.shape[0] * rows.shape[0] * rows.shape[1], 0),
        name="pick",
    )(send, rows)


def dense(side, mean, own, mine, other, bias, send=None):
    nodes, width = own.shape
    vmem = pl.BlockSpec(memory_space=pltpu.VMEM)
    smem = pl.BlockSpec(memory_space=pltpu.SMEM)
    cost = estimate(2 * nodes * mean.shape[1] * width, 0)
    shape = jax.ShapeDtypeStruct((nodes, width), jnp.bfloat16)
    if send is None:
        return pl.pallas_call(
            dense_second_body,
            out_shape=shape,
            in_specs=[smem] + [vmem] * 5,
            out_specs=vmem,
            compiler_params=params(14),
            cost_estimate=cost,
            name="dense",
        )(side, mean, own, mine, other, bias)
    picked = jax.ShapeDtypeStruct((send.shape[0], width), jnp.bfloat16)
    return pl.pallas_call(
        dense_first_body,
        out_shape=[shape, picked],
        in_specs=[smem] + [vmem] * 6,
        out_specs=[vmem, vmem],
        compiler_params=params(16),
        cost_estimate=cost,
        name="dense",
    )(side, mean, own, mine, other, bias, send)


def weight_halves(bases, self_weight, coef):
    relations, width = coef.shape[0], bases.shape[2]
    mixed = jnp.einsum(
        "rb,bij->rij", coef, bases.astype(jnp.float32), precision=lax.Precision.HIGHEST
    ).astype(jnp.bfloat16)
    half = relations // 2
    halves = [
        jnp.concatenate([mixed[:half], self_weight[None]], axis=0),
        jnp.concatenate([mixed[half:], self_weight[None]], axis=0),
    ]
    return jnp.stack([h.reshape(-1, width) for h in halves])


def exchange(picked, halves, devices):
    width = picked.shape[1]
    rows = picked.reshape(devices, -1, width)
    weights = jnp.broadcast_to(halves[None], (devices // 2,) + halves.shape)
    outgoing = jnp.concatenate([rows, weights.reshape(devices, -1, width)], axis=1)
    return lax.all_to_all(outgoing, "dom", split_axis=0, concat_axis=0, tiled=True)


def split(incoming, slot, relations):
    devices, _, width = incoming.shape
    table = incoming[:, :slot].reshape(-1, width)
    mine = incoming[:, slot:].reshape(devices, relations // 2 + 1, -1, width)
    mine = jnp.swapaxes(mine, 0, 1).reshape(-1, width)
    swap = [(i, i ^ 1) for i in range(devices)]
    other = lax.ppermute(mine[: mine.shape[0] - width], "dom", swap)
    return table, mine, other


def shards(
    features,
    edge_source,
    edge_relation,
    edge_target,
    block_count,
    send_list,
    bases_first,
    self_first,
    coef_first,
    bias_first,
    bases_second,
    self_second,
    coef_second,
    bias_second,
):
    node_rows = features.shape[0]
    relations = coef_first.shape[0]
    devices, slot = send_list.shape[1:]
    remote_rows = devices * slot
    resident = 2 * node_rows * relations * (node_rows + remote_rows) <= RESIDENT_MAX
    side = (lax.axis_index("dom") & 1).astype(jnp.int32).reshape(1)
    send = send_list.reshape(-1, 1)
    halves_first = weight_halves(bases_first, self_first, coef_first)
    incoming = exchange(pick(send, features), halves_first, devices)
    halves_second = weight_halves(bases_second, self_second, coef_second)
    local, remote, degree = build(
        edge_target[0, :, 0],
        block_count,
        edge_source[0],
        edge_relation[0],
        edge_target[0],
        node_rows=node_rows,
        relations=relations,
        remote_rows=remote_rows,
        resident=resident,
    )
    pooled = apply_local(local, features, resident=resident)
    table, mine, other = split(incoming, slot, relations)
    mean = apply_remote(remote, table, pooled, degree, relations=relations, resident=resident)
    hidden, picked = dense(side, mean, features, mine, other, bias_first[None], send)
    incoming = exchange(picked, halves_second, devices)
    pooled = apply_local(local, hidden, resident=resident)
    table, mine, other = split(incoming, slot, relations)
    mean = apply_remote(remote, table, pooled, degree, relations=relations, resident=resident)
    return dense(side, mean, hidden, mine, other, bias_second[None])


def solution(mesh):
    placed = (
        P("dom", None),
        P("dom", None, None),
        P("dom", None, None),
        P("dom", None, None),
        P("dom"),
        P("dom", None, None),
        P(None, "dom", None),
        P("dom", None),
        P(),
        P(),
        P(None, "dom", None),
        P("dom", None),
        P(),
        P(),
    )
    return jax.shard_map(
        shards, mesh=mesh, in_specs=placed, out_specs=P("dom", None), check_vma=False
    )
```

profile of v0, /device:TPU:0, one launch (start us, length us, event | category | flops | bytes accessed | tf_op | source)
XLA Modules:
  0.0 156.6 jit_solution(14214400923708058416)
XLA Ops:
  0.0 0.9 copy-done
  0.9 0.9 convolution_convert_fusion.1
  1.8 0.7 copy.19
  2.5 1.2 reshape.54.send_ref
  3.8 1.0 copy-done.12
  4.9 1.6 %pick.1 = bf16[1024,256]{1,0:T(8,128)(2,1)S(1)} custom-call(s32[1024,1]{1,0:T(8,128)S(1)} %reshape.54.send_ref, bf16[1024,256]{1,0:T(8,128)(2,1)S(1)} %copy-done.12), custom_call_target="tpu_custom_call" | custom-call | flops 536870912 | tf_op jit(solution)/shard_map/pick/pallas_call | solution.py:356
  6.6 1.1 pad_maximum_fusion
  7.7 7.3 %all-to-all-start = ((bf16[32,72,256]{2,1,0:T(8,128)(2,1)}), bf16[32,72,256]{2,1,0:T(8,128)(2,1)S(1)}, u32[]{:S(2)}, u32[]{:S(2)}) async-start(bf16[32,72,256]{2,1,0:T(8,128)(2,1)} %pad_maximum_fusion), calls=%async_computation | async-start | bytes 2359296 | tf_op jit(solution)/shard_map/all_to_all | solution.py:413
  15.7 0.2 convolution_convert_fusion
  16.0 0.1 slice_reduce_fusion.tile_ref
  16.1 27.8 %build.1 = (bf16[8192,1024]{1,0:T(8,128)(2,1)S(1)}, bf16[8192,1024]{1,0:T(8,128)(2,1)S(1)}, f32[8192,1]{1,0:T(8,128)S(1)}) custom-call(s32[128]{0:T(128)S(1)} %slice_reduce_fusion.tile_ref, s32[1]{0:T(128)S(6)} %copy.41.count_ref, s32[128,128]{1,0:T(8,128)S(1)} %bitcast.51, s32[128,128]{1,0:T(8,128)S(1)} %bitcast.52, s32[128,128]{1,0:T(8,128)S(1)} %bitcast.48), custom_call_target="tpu_custom_call" | custom-call | flops 12884901888 | bytes 33554432 | tf_op jit(solution)/shard_map/build/pallas_call | solution.py:188
  43.9 5.7 %copy-done.2 = bf16[8192,1024]{1,0:T(8,128)(2,1)} copy-done((bf16[8192,1024]{1,0:T(8,128)(2,1)}, bf16[8192,1024]{1,0:T(8,128)(2,1)S(1)}, u32[]{:S(2)}) %copy-start.2) | copy-done | bytes 16777240
  49.7 5.7 %copy-done.4 = bf16[8192,1024]{1,0:T(8,128)(2,1)} copy-done((bf16[8192,1024]{1,0:T(8,128)(2,1)}, bf16[8192,1024]{1,0:T(8,128)(2,1)S(1)}, u32[]{:S(2)}) %copy-start.4) | copy-done | bytes 16777240
  55.4 2.0 %copy-done.9 = f32[8192,1]{1,0:T(8,128)} copy-done((f32[8192,1]{1,0:T(8,128)}, f32[8192,1]{1,0:T(8,128)S(1)}, u32[]{:S(2)}) %copy-start.9) | copy-done | bytes 32792
  57.4 5.8 %copy-done.5 = bf16[8192,1024]{1,0:T(8,128)(2,1)S(1)} copy-done((bf16[8192,1024]{1,0:T(8,128)(2,1)S(1)}, bf16[8192,1024]{1,0:T(8,128)(2,1)}, u32[]{:S(2)}) %copy-start.5) | copy-done | bytes 16777240
  63.2 7.0 %local.2.pooled_ref = f32[8192,256]{1,0:T(8,128)S(1)} custom-call(bf16[8192,1024]{1,0:T(8,128)(2,1)S(1)} %copy-done.5, bf16[1024,256]{1,0:T(8,128)(2,1)S(1)} %copy-done.13), custom_call_target="tpu_custom_call" | custom-call | flops 4294967296 | bytes 16777216 | tf_op jit(solution)/shard_map/local/pallas_call | solution.py:229
  70.2 3.2 %copy-done.7 = f32[8192,256]{1,0:T(8,128)} copy-done((f32[8192,256]{1,0:T(8,128)}, f32[8192,256]{1,0:T(8,128)S(1)}, u32[]{:S(2)}) %copy-start.7) | copy-done | bytes 8388632
  73.5 0.1 slice.56
  73.5 0.8 copy.24
  74.5 5.8 %copy-done.3 = bf16[8192,1024]{1,0:T(8,128)(2,1)S(1)} copy-done((bf16[8192,1024]{1,0:T(8,128)(2,1)S(1)}, bf16[8192,1024]{1,0:T(8,128)(2,1)}, u32[]{:S(2)}) %copy-start.3) | copy-done | bytes 16777240
  80.3 3.4 %copy-done.8 = f32[8192,256]{1,0:T(8,128)S(1)} copy-done((f32[8192,256]{1,0:T(8,128)S(1)}, f32[8192,256]{1,0:T(8,128)}, u32[]{:S(2)}) %copy-start.8) | copy-done | bytes 8388632
  83.7 2.2 %copy-done.10 = f32[8192,1]{1,0:T(8,128)S(1)} copy-done((f32[8192,1]{1,0:T(8,128)S(1)}, f32[8192,1]{1,0:T(8,128)}, u32[]{:S(2)}) %copy-start.10) | copy-done | bytes 32792
  85.9 7.0 %remote.2.mean_ref = bf16[1024,2048]{1,0:T(8,128)(2,1)S(1)} custom-call(bf16[8192,1024]{1,0:T(8,128)(2,1)S(1)} %copy-done.3, bf16[1024,256]{1,0:T(8,128)(2,1)S(1)} %bitcast.45, f32[8192,256]{1,0:T(8,128)S(1)} %copy-done.8, f32[8192,1]{1,0:T(8,128)S(1)} %copy-done.10), custom_call_target="tpu_custom_call" | custom-call | flops 4294967296 | bytes 16777216 | tf_op jit(solution)/shard_map/remote/pallas_call | solution.py:285
  92.9 3.0 %dense.2 = (bf16[1024,256]{1,0:T(8,128)(2,1)S(1)}, bf16[1024,256]{1,0:T(8,128)(2,1)S(1)}) custom-call(s32[1]{0:T(128)} %bitcast.side_ref, bf16[1024,2048]{1,0:T(8,128)(2,1)S(1)} %remote.2.mean_ref, bf16[1024,256]{1,0:T(8,128)(2,1)S(1)} %copy-done.13, bf16[1280,256]{1,0:T(8,128)(2,1)S(1)} %bitcast.42, bf16[1024,256]{1,0:T(8,128)(2,1)S(1)} %collective-permute-done.other_ref, ...), custom_call_target="tpu_custom_call" | custom-call | flops 1073741824 | tf_op jit(solution)/shard_map/dense/pallas_call | solution.py:384
  96.0 0.1 pad_maximum_fusion.1
  96.1 37.8 %all_to_all.10 = bf16[32,72,256]{2,1,0:T(8,128)(2,1)S(1)} all-to-all(bf16[32,72,256]{2,1,0:T(8,128)(2,1)S(1)} %pad_maximum_fusion.1), channel_id=1, replica_groups=mesh['dom'=32] {'dom'}, dimensions={0} | all-to-all | bytes 2359296 | tf_op jit(solution)/shard_map/all_to_all | solution.py:413
  134.0 0.1 collective-permute-start.1
  134.1 5.9 %copy-done.6 = bf16[8192,1024]{1,0:T(8,128)(2,1)S(1)} copy-done((bf16[8192,1024]{1,0:T(8,128)(2,1)S(1)}, bf16[8192,1024]{1,0:T(8,128)(2,1)}, u32[]{:S(2)}) %copy-start.6) | copy-done | bytes 16777240
  140.0 7.1 %local.3.pooled_ref = f32[8192,256]{1,0:T(8,128)S(1)} custom-call(bf16[8192,1024]{1,0:T(8,128)(2,1)S(1)} %copy-done.6, bf16[1024,256]{1,0:T(8,128)(2,1)S(1)} %get-tuple-element.14.table_ref.own_ref), custom_call_target="tpu_custom_call" | custom-call | flops 4294967296 | bytes 16777216 | tf_op jit(solution)/shard_map/local/pallas_call | solution.py:229
  147.2 0.1 slice.59
  147.3 7.0 %remote.3.mean_ref = bf16[1024,2048]{1,0:T(8,128)(2,1)S(1)} custom-call(bf16[8192,1024]{1,0:T(8,128)(2,1)S(1)} %bitcast.41, bf16[1024,256]{1,0:T(8,128)(2,1)S(1)} %bitcast.44, f32[8192,256]{1,0:T(8,128)S(1)} %local.3.pooled_ref, f32[8192,1]{1,0:T(8,128)S(1)} %copy-done.11), custom_call_target="tpu_custom_call" | custom-call | flops 4294967296 | bytes 16777216 | tf_op jit(solution)/shard_map/remote/pallas_call | solution.py:285
  154.4 2.2 %dense.3 = bf16[1024,256]{1,0:T(8,128)(2,1)} custom-call(s32[1]{0:T(128)} %bitcast.side_ref, bf16[1024,2048]{1,0:T(8,128)(2,1)S(1)} %remote.3.mean_ref, bf16[1024,256]{1,0:T(8,128)(2,1)S(1)} %get-tuple-element.14.table_ref.own_ref, bf16[1280,256]{1,0:T(8,128)(2,1)S(1)} %bitcast.43, bf16[1024,256]{1,0:T(8,128)(2,1)S(1)} %collective-permute-done.1.other_ref, ...), custom_call_target="tpu_custom_call" | custom-call | flops 1073741824 | tf_op jit(solution)/shard_map/dense/pallas_call | solution.py:374
  (64 shorter events, 0.7 us)
Async XLA Ops:
  0.0 0.9 copy-start
  3.8 1.0 copy-start.12
  6.5 9.2 %copy-start.20 = (bf16[8,256]{1,0:T(8,128)(2,1)S(1)}, bf16[8,256]{1,0:T(8,128)(2,1)}, u32[]{:S(2)}) copy-start(bf16[8,256]{1,0:T(8,128)(2,1)} %param.25) | copy-start | bytes 12292
  6.5 9.2 %copy-start.19 = (bf16[30,8,256]{2,1,0:T(8,128)(2,1)S(1)}, bf16[30,8,256]{2,1,0:T(8,128)(2,1)}, u32[]{:S(2)}) copy-start(bf16[30,8,256]{2,1,0:T(8,128)(2,1)} %param.24) | copy-start | bytes 368644
  6.5 9.2 %copy-start.21 = (f32[8,30]{1,0:T(8,128)S(1)}, f32[8,30]{1,0:T(8,128)}, u32[]{:S(2)}) copy-start(f32[8,30]{1,0:T(8,128)} %param.26) | copy-start | bytes 2884
  6.5 9.4 %copy-start.14 = (s32[1,128,128]{2,1,0:T(8,128)S(1)}, s32[1,128,128]{2,1,0:T(8,128)}, u32[]{:S(2)}) copy-start(s32[1,128,128]{2,1,0:T(8,128)} %param.17) | copy-start | bytes 196612
  6.5 9.5 %copy-start.17 = (s32[1,128,128]{2,1,0:T(8,128)S(1)}, s32[1,128,128]{2,1,0:T(8,128)}, u32[]{:S(2)}) copy-start(s32[1,128,128]{2,1,0:T(8,128)} %param.15) | copy-start | bytes 196612
  6.6 9.5 %copy-start.18 = (s32[1,128,128]{2,1,0:T(8,128)S(1)}, s32[1,128,128]{2,1,0:T(8,128)}, u32[]{:S(2)}) copy-start(s32[1,128,128]{2,1,0:T(8,128)} %param.16) | copy-start | bytes 196612
  7.7 65.7 %all-to-all-start = ((bf16[32,72,256]{2,1,0:T(8,128)(2,1)}), bf16[32,72,256]{2,1,0:T(8,128)(2,1)S(1)}, u32[]{:S(2)}, u32[]{:S(2)}) async-start(bf16[32,72,256]{2,1,0:T(8,128)(2,1)} %pad_maximum_fusion), calls=%async_computation | async-start | bytes 2359296 | tf_op jit(solution)/shard_map/all_to_all | solution.py:413
  16.1 41.3 %copy-start.13 = (bf16[1024,256]{1,0:T(8,128)(2,1)S(1)}, bf16[1024,256]{1,0:T(8,128)(2,1)}, u32[]{:S(2)}) copy-start(bf16[1024,256]{1,0:T(8,128)(2,1)} %own_ref.1) | copy-start | bytes 1572868
  43.9 5.7 %copy-start.2 = (bf16[8192,1024]{1,0:T(8,128)(2,1)}, bf16[8192,1024]{1,0:T(8,128)(2,1)S(1)}, u32[]{:S(2)}) copy-start(bf16[8192,1024]{1,0:T(8,128)(2,1)S(1)} %get-tuple-element.10.counts_ref) | copy-start | bytes 50331652
  49.7 5.7 %copy-start.4 = (bf16[8192,1024]{1,0:T(8,128)(2,1)}, bf16[8192,1024]{1,0:T(8,128)(2,1)S(1)}, u32[]{:S(2)}) copy-start(bf16[8192,1024]{1,0:T(8,128)(2,1)S(1)} %get-tuple-element.11.counts_ref) | copy-start | bytes 50331652
  55.4 2.0 %copy-start.9 = (f32[8192,1]{1,0:T(8,128)}, f32[8192,1]{1,0:T(8,128)S(1)}, u32[]{:S(2)}) copy-start(f32[8192,1]{1,0:T(8,128)S(1)} %get-tuple-element.12.degree_ref) | copy-start | bytes 98308
  57.4 5.8 %copy-start.5 = (bf16[8192,1024]{1,0:T(8,128)(2,1)S(1)}, bf16[8192,1024]{1,0:T(8,128)(2,1)}, u32[]{:S(2)}) copy-start(bf16[8192,1024]{1,0:T(8,128)(2,1)} %copy-done.4) | copy-start | bytes 50331652
  70.2 3.3 %copy-start.7 = (f32[8192,256]{1,0:T(8,128)}, f32[8192,256]{1,0:T(8,128)S(1)}, u32[]{:S(2)}) copy-start(f32[8192,256]{1,0:T(8,128)S(1)} %local.2.pooled_ref) | copy-start | bytes 25165828
  74.4 18.6 %collective-permute-start = (bf16[1024,256]{1,0:T(8,128)(2,1)}, bf16[1024,256]{1,0:T(8,128)(2,1)S(1)}, u32[]{:S(2)}, u32[]{:S(2)}) collective-permute-start(bf16[1024,256]{1,0:T(8,128)(2,1)} %bitcast.15), channel_id=1, source_target_pairs={{0,1},{1,0},{2,3},{3,2},{4,5},{5,4},{6,7},{7,6},{8,9},{9,8},{10,11... | collective-permute-start | bytes 1572872 | tf_op jit(solution)/shard_map/ppermute | solution.py:422
  74.5 5.8 %copy-start.3 = (bf16[8192,1024]{1,0:T(8,128)(2,1)S(1)}, bf16[8192,1024]{1,0:T(8,128)(2,1)}, u32[]{:S(2)}) copy-start(bf16[8192,1024]{1,0:T(8,128)(2,1)} %copy-done.2) | copy-start | bytes 50331652
  80.3 3.4 %copy-start.8 = (f32[8192,256]{1,0:T(8,128)S(1)}, f32[8192,256]{1,0:T(8,128)}, u32[]{:S(2)}) copy-start(f32[8192,256]{1,0:T(8,128)} %copy-done.7) | copy-start | bytes 25165828
  83.7 2.2 %copy-start.10 = (f32[8192,1]{1,0:T(8,128)S(1)}, f32[8192,1]{1,0:T(8,128)}, u32[]{:S(2)}) copy-start(f32[8192,1]{1,0:T(8,128)} %copy-done.9) | copy-start | bytes 98308
  85.9 7.1 %copy-start.15 = (f32[256]{0:T(256)S(1)}, f32[256]{0:T(256)}, u32[]{:S(2)}) copy-start(f32[256]{0:T(256)} %param.23) | copy-start | bytes 3076
  133.9 13.4 %slice-start = ((s8[16777216]{0:T(1024)(128)(4,1)}), s8[4194304]{0:T(1024)(128)(4,1)S(1)}, s32[]{:S(2)}) async-start(s8[16777216]{0:T(1024)(128)(4,1)} %bitcast.40), calls=%async_computation.2 | async-start | bytes 8388608
  134.0 20.4 %collective-permute-start.1 = (bf16[1024,256]{1,0:T(8,128)(2,1)S(1)}, bf16[1024,256]{1,0:T(8,128)(2,1)S(1)}, u32[]{:S(2)}, u32[]{:S(2)}) collective-permute-start(bf16[1024,256]{1,0:T(8,128)(2,1)S(1)} %bitcast.55), channel_id=1, source_target_pairs={{0,1},{1,0},{2,3},{3,2},{4,5},{5,4},{6,7},{7,6},{8,9},{9,8},{10,11... | collective-permute-start | bytes 1572872 | tf_op jit(solution)/shard_map/ppermute | solution.py:422
  134.1 5.9 %copy-start.6 = (bf16[8192,1024]{1,0:T(8,128)(2,1)S(1)}, bf16[8192,1024]{1,0:T(8,128)(2,1)}, u32[]{:S(2)}) copy-start(bf16[8192,1024]{1,0:T(8,128)(2,1)} %copy-done.4) | copy-start | bytes 50331652
  140.0 7.2 %slice-start.1 = ((s8[16777216]{0:T(1024)(128)(4,1)}), s8[4194304]{0:T(1024)(128)(4,1)S(1)}, s32[]{:S(2)}) async-start(s8[16777216]{0:T(1024)(128)(4,1)} %bitcast.40), calls=%async_computation.3 | async-start | bytes 8388608
  140.0 7.3 %slice-start.2 = ((s8[16777216]{0:T(1024)(128)(4,1)}), s8[4194304]{0:T(1024)(128)(4,1)S(1)}, s32[]{:S(2)}) async-start(s8[16777216]{0:T(1024)(128)(4,1)} %bitcast.40), calls=%async_computation.4 | async-start | bytes 8388608
  140.0 7.3 %slice-start.3 = ((s8[16777216]{0:T(1024)(128)(4,1)}), s8[4194304]{0:T(1024)(128)(4,1)S(1)}, s32[]{:S(2)}) async-start(s8[16777216]{0:T(1024)(128)(4,1)} %bitcast.40), calls=%async_computation.5 | async-start | bytes 8388608
  140.0 7.3 %copy-start.11 = (f32[8192,1]{1,0:T(8,128)S(1)}, f32[8192,1]{1,0:T(8,128)}, u32[]{:S(2)}) copy-start(f32[8192,1]{1,0:T(8,128)} %copy-done.9) | copy-start | bytes 98308
  147.3 7.1 %copy-start.16 = (f32[256]{0:T(256)S(1)}, f32[256]{0:T(256)}, u32[]{:S(2)}) copy-start(f32[256]{0:T(256)} %param.27) | copy-start | bytes 3076
  154.4 2.2 %copy-start.1 = (bf16[30,8,256]{2,1,0:T(8,128)(2,1)S(1)}, bf16[30,8,256]{2,1,0:T(8,128)(2,1)}, u32[]{:S(2)}) copy-start(bf16[30,8,256]{2,1,0:T(8,128)(2,1)} %param.20) | copy-start | bytes 368644
where the time goes:
time: 157 us
  Pallas kernels  62.8 us (40%)
  local copies, waits for them, and re-layouts  45.2 us (29%)
  blocking collectives  37.8 us (24%)
  starting transfers between devices  7.4 us (5%)
    unnamed x52, local copies, waits for them, and re-layouts  41.7 us
    all_to_all x1, blocking collectives, exchange(): lax.all_to_all(outgoing, 'dom', split_axis=0, concat_axis=0, tiled=True)  37.8 us
    pallas_call x1, Pallas kernels, build(): pl.pallas_call(functools.partial(build_resident, **settings), out_shape=[...  27.8 us
    pallas_call x2, Pallas kernels, apply_local(): pl.pallas_call(functools.partial(apply_local_body, group=group), out_shap...  14.1 us
    pallas_call x2, Pallas kernels, apply_remote(): pl.pallas_call(body, out_shape=pltpu.VMEM((nodes, relations * width), jnp...  14.1 us
    all_to_all x1, starting transfers between devices, exchange(): lax.all_to_all(outgoing, 'dom', split_axis=0, concat_axis=0, tiled=True)  7.32 us
  transfers between devices with their start and end apart: 3, of which 0 were waited for; matrix products, arithmetic and copies ran while one was open for 0% of the time, Pallas kernels for 36%

commit v1 on v0

v1 whole, which is shorter than its diff:
```python
import functools

import jax
import jax.numpy as jnp
from jax import lax
from jax.experimental import pallas as pl
from jax.experimental.pallas import tpu as pltpu
from jax.sharding import PartitionSpec as P

WIN = 16
CHUNK = 512
GROUP = 8
MIB = 1 << 20
WHOLE_MAX = 36 * MIB
CONTRACT_LANES = (((1,), (1,)), ((), ()))


def estimate(flops, nbytes):
    return pl.CostEstimate(flops=int(flops), bytes_accessed=int(nbytes), transcendentals=0)


def params(mib, **more):
    return pltpu.CompilerParams(vmem_limit_bytes=mib * MIB, **more)


def hot(rows, lanes):
    row_ids = lax.broadcasted_iota(jnp.int32, (rows, lanes.shape[1]), 0)
    return jnp.where(row_ids == lanes, 1.0, 0.0)


def code_edges(source_ref, relation_ref, target_ref, slot_ref, code_ref, low_ref, relations):
    slot = relation_ref[...] * WIN + (target_ref[...] & (WIN - 1))
    slot_ref[...] = slot
    code_ref[...] = (source_ref[...] // CHUNK) * (WIN * relations) + slot
    low_ref[...] = source_ref[...] & (CHUNK - 1)


def link_blocks(tile_ref, count_ref, head_ref, next_ref, tiles):
    def clear(t, carry):
        head_ref[t] = -1
        return carry

    lax.fori_loop(0, tiles, clear, 0)

    def link(b, carry):
        t = tile_ref[b] // WIN
        next_ref[b] = head_ref[t]
        head_ref[t] = b
        return carry

    lax.fori_loop(0, count_ref[0], link, 0)


def pair_of(first, next_ref):
    second = jnp.where(first >= 0, next_ref[jnp.maximum(first, 0)], -1)
    after = jnp.where(second >= 0, next_ref[jnp.maximum(second, 0)], -1)
    return second, after


def pair_rows(ref, first, second):
    one = jnp.where(first >= 0, ref[pl.ds(jnp.maximum(first, 0), 1), :], -1)
    two = jnp.where(second >= 0, ref[pl.ds(jnp.maximum(second, 0), 1), :], -1)
    return jnp.concatenate([one, two], axis=1)


def pair_counts(first, second, slot_ref, code_ref, low_ref, rows, slots):
    left = hot(rows, pair_rows(code_ref, first, second)).astype(jnp.bfloat16)
    right = hot(CHUNK, pair_rows(low_ref, first, second)).astype(jnp.bfloat16)
    counts = lax.dot_general(left, right, CONTRACT_LANES, preferred_element_type=jnp.float32)
    degree = jnp.sum(hot(slots, pair_rows(slot_ref, first, second)), axis=1, keepdims=True)
    return counts, degree


def put_counts(counts, local_ref, remote_ref, row, slots, locals_):
    for piece in range(counts.shape[0] // slots):
        part = counts[piece * slots : (piece + 1) * slots].astype(jnp.bfloat16)
        if piece < locals_:
            local_ref[pl.ds(row, slots), pl.ds(piece * CHUNK, CHUNK)] = part
        else:
            remote_ref[pl.ds(row, slots), pl.ds((piece - locals_) * CHUNK, CHUNK)] = part


def build_streamed(
    tile_ref, count_ref, source_ref, relation_ref, target_ref,
    local_ref, remote_ref, degree_ref,
    head_ref, next_ref, slot_ref, code_ref, low_ref, sum_ref,
    *, tiles, relations, locals_, pieces,
):
    slots = WIN * relations
    rows = pieces * slots
    t = pl.program_id(0)

    @pl.when(t == 0)
    def _():
        code_edges(source_ref, relation_ref, target_ref, slot_ref, code_ref, low_ref, relations)
        link_blocks(tile_ref, count_ref, head_ref, next_ref, tiles)

    sum_ref[...] = jnp.zeros_like(sum_ref)
    degree_ref[...] = jnp.zeros_like(degree_ref)

    def step(first):
        second, after = pair_of(first, next_ref)
        counts, degree = pair_counts(first, second, slot_ref, code_ref, low_ref, rows, slots)
        sum_ref[...] += counts
        degree_ref[...] += degree
        return after

    lax.while_loop(lambda first: first >= 0, step, head_ref[t])
    put_counts(sum_ref[...], local_ref, remote_ref, 0, slots, locals_)


def build_streamed_call(tile_of, count, source, relation, target, *, node_rows, relations, remote_rows):
    blocks, width = source.shape
    tiles, slots = node_rows // WIN, WIN * relations
    locals_, remotes = node_rows // CHUNK, remote_rows // CHUNK
    pieces = locals_ + remotes
    smem = pl.BlockSpec(memory_space=pltpu.SMEM)
    shapes = [
        ((tiles * slots, node_rows), jnp.bfloat16),
        ((tiles * slots, remote_rows), jnp.bfloat16),
        ((tiles * slots, 1), jnp.float32),
    ]
    whole = pl.BlockSpec((blocks, width), lambda t: (0, 0))
    return pl.pallas_call(
        functools.partial(
            build_streamed, tiles=tiles, relations=relations, locals_=locals_, pieces=pieces
        ),
        grid=(tiles,),
        out_shape=[jax.ShapeDtypeStruct(s, d) for s, d in shapes],
        in_specs=[smem, smem, whole, whole, whole],
        out_specs=[pl.BlockSpec((slots, s[1]), lambda t: (t, 0)) for s, _ in shapes],
        scratch_shapes=[
            pltpu.SMEM((tiles,), jnp.int32),
            pltpu.SMEM((blocks,), jnp.int32),
            pltpu.VMEM((blocks, width), jnp.int32),
            pltpu.VMEM((blocks, width), jnp.int32),
            pltpu.VMEM((blocks, width), jnp.int32),
            pltpu.VMEM((pieces * slots, CHUNK), jnp.float32),
        ],
        compiler_params=params(40),
        cost_estimate=estimate(
            4 * (tiles + blocks // 4) * pieces * slots * CHUNK * width,
            2 * tiles * slots * pieces * CHUNK,
        ),
        name="build",
    )(tile_of, count, source, relation, target)


def local_streamed_body(counts_ref, table_ref, pooled_ref):
    pooled_ref[...] = jnp.dot(
        counts_ref[...], table_ref[...], preferred_element_type=jnp.float32
    )


def local_streamed(counts, table, *, group):
    rows, depth = counts.shape
    width = table.shape[1]
    return pl.pallas_call(
        local_streamed_body,
        grid=(rows // group,),
        out_shape=jax.ShapeDtypeStruct((rows, width), jnp.float32),
        in_specs=[
            pl.BlockSpec((group, depth), lambda i: (i, 0)),
            pl.BlockSpec((depth, width), lambda i: (0, 0)),
        ],
        out_specs=pl.BlockSpec((group, width), lambda i: (i, 0)),
        compiler_params=params(40),
        cost_estimate=estimate(2 * rows * depth * width, 2 * rows * depth),
        name="local",
    )(counts, table)


def put_means(mean, mean_ref, first_tile, relations):
    slots = WIN * relations
    width = mean.shape[1]
    for tile in range(mean.shape[0] // slots):
        at = pl.multiple_of((first_tile + tile) * WIN, WIN)
        for relation in range(relations):
            start = tile * slots + relation * WIN
            mean_ref[pl.ds(at, WIN), pl.ds(relation * width, width)] = mean[start : start + WIN]


def remote_streamed_body(counts_ref, table_ref, pooled_ref, degree_ref, mean_ref, *, relations):
    total = pooled_ref[...] + jnp.dot(
        counts_ref[...], table_ref[...], preferred_element_type=jnp.float32
    )
    mean = total * (1.0 / jnp.maximum(degree_ref[...], 1.0))
    put_means(mean.astype(jnp.bfloat16), mean_ref, 0, relations)


def remote_streamed(counts, table, pooled, degree, *, relations, group):
    rows, depth = counts.shape
    width = table.shape[1]
    return pl.pallas_call(
        functools.partial(remote_streamed_body, relations=relations),
        grid=(rows // group,),
        out_shape=jax.ShapeDtypeStruct((rows // relations, relations * width), jnp.bfloat16),
        in_specs=[
            pl.BlockSpec((group, depth), lambda i: (i, 0)),
            pl.BlockSpec((depth, width), lambda i: (0, 0)),
            pl.BlockSpec((group, width), lambda i: (i, 0)),
            pl.BlockSpec((group, 1), lambda i: (i, 0)),
        ],
        out_specs=pl.BlockSpec((group // relations, relations * width), lambda i: (i, 0)),
        compiler_params=params(40),
        cost_estimate=estimate(2 * rows * depth * width, 2 * rows * depth),
        name="remote",
    )(counts, table, pooled, degree)


def build_body(
    tile_ref, count_ref, source_ref, relation_ref, target_ref, own_ref,
    local_ref, remote_ref, pooled_ref, degree_ref,
    local_v, remote_v, pooled_v, head_ref, next_ref, list_ref, slot_ref, code_ref, low_ref, sum_ref,
    sems, *, tiles, relations, locals_, pieces,
):
    slots = WIN * relations
    rows = pieces * slots
    code_edges(source_ref, relation_ref, target_ref, slot_ref, code_ref, low_ref, relations)
    link_blocks(tile_ref, count_ref, head_ref, next_ref, tiles)
    head_ref[tiles] = -1
    counted = functools.partial(
        pair_counts, slot_ref=slot_ref, code_ref=code_ref, low_ref=low_ref, rows=rows, slots=slots
    )

    def place(t, piece):
        row = pl.multiple_of(t * slots, slots)
        ref, at = (local_v, piece) if piece < locals_ else (remote_v, piece - locals_)
        return ref, (pl.ds(row, slots), pl.ds(at * CHUNK, CHUNK))

    def part(counts, piece):
        return counts[piece * slots : (piece + 1) * slots]

    def add_degree(i, u, degree):
        lanes = lax.broadcasted_iota(jnp.int32, (slots, GROUP), 1)
        degree_ref[i] += jnp.where(lanes == u, degree, 0.0)

    def group(i, carry):
        for u in range(GROUP):
            t = i * GROUP + u
            first = head_ref[t]
            second, after = pair_of(first, next_ref)
            counts, degree = counted(first, second)
            for piece in range(pieces):
                ref, where = place(t, piece)
                ref[where] = part(counts, piece).astype(jnp.bfloat16)
            degree_ref[i, :, pl.ds(u, 1)] = degree
            head_ref[t] = after

        short = jnp.int32(0)
        for u in range(GROUP):
            t = i * GROUP + u
            first = head_ref[t]
            _, after = pair_of(first, next_ref)
            list_ref[short] = t
            short += jnp.where((first >= 0) & (after < 0), 1, 0)
        list_ref[short] = tiles

        def add_two(j, carry):
            for k in range(2):
                t = list_ref[2 * j + k]
                first = head_ref[t]
                second, _ = pair_of(first, next_ref)
                counts, degree = counted(first, second)
                for piece in range(pieces):
                    ref, where = place(t, piece)
                    total = ref[where].astype(jnp.float32) + part(counts, piece)
                    ref[where] = total.astype(jnp.bfloat16)
                add_degree(i, t - i * GROUP, degree)
            return carry

        lax.fori_loop(0, (short + 1) // 2, add_two, 0)

        def long(u, carry):
            t = i * GROUP + u
            first = head_ref[t]
            _, after = pair_of(first, next_ref)

            @pl.when(after >= 0)
            def _():
                for piece in range(pieces):
                    ref, where = place(t, piece)
                    sum_ref[pl.ds(piece * slots, slots), :] = ref[where].astype(jnp.float32)

                def step(first):
                    second, after = pair_of(first, next_ref)
                    counts, degree = counted(first, second)
                    sum_ref[...] += counts
                    add_degree(i, u, degree)
                    return after

                lax.while_loop(lambda first: first >= 0, step, first)
                for piece in range(pieces):
                    ref, where = place(t, piece)
                    ref[where] = sum_ref[pl.ds(piece * slots, slots), :].astype(jnp.bfloat16)

            return carry

        lax.fori_loop(0, GROUP, long, 0)
        some = pl.ds(pl.multiple_of(i * GROUP * slots, GROUP * slots), GROUP * slots)
        pooled_v[some, :] = jnp.dot(
            local_v[some, :], own_ref[...], preferred_element_type=jnp.float32
        )
        pltpu.make_async_copy(local_v.at[some], local_ref.at[some], sems.at[0]).start()
        pltpu.make_async_copy(remote_v.at[some], remote_ref.at[some], sems.at[1]).start()
        pltpu.make_async_copy(pooled_v.at[some], pooled_ref.at[some], sems.at[2]).start()
        return carry

    lax.fori_loop(0, tiles // GROUP, group, 0)
    every = pl.ds(0, tiles * slots)
    pltpu.make_async_copy(local_v.at[every], local_ref, sems.at[0]).wait()
    pltpu.make_async_copy(remote_v.at[every], remote_ref, sems.at[1]).wait()
    pltpu.make_async_copy(pooled_v, pooled_ref, sems.at[2]).wait()


def build(tile_of, count, source, relation, target, own, *, relations, remote_rows):
    blocks, block_width = source.shape
    node_rows, width = own.shape
    tiles, slots = node_rows // WIN, WIN * relations
    rows = tiles * slots
    locals_, remotes = node_rows // CHUNK, remote_rows // CHUNK
    pieces = locals_ + remotes
    vmem = pl.BlockSpec(memory_space=pltpu.VMEM)
    smem = pl.BlockSpec(memory_space=pltpu.SMEM)
    hbm = pl.BlockSpec(memory_space=pltpu.HBM)
    return pl.pallas_call(
        functools.partial(
            build_body, tiles=tiles, relations=relations, locals_=locals_, pieces=pieces
        ),
        out_shape=[
            jax.ShapeDtypeStruct((rows, node_rows), jnp.bfloat16),
            jax.ShapeDtypeStruct((rows, remote_rows), jnp.bfloat16),
            jax.ShapeDtypeStruct((rows, width), jnp.float32),
            jax.ShapeDtypeStruct((tiles // GROUP, slots, GROUP), jnp.float32),
        ],
        in_specs=[smem, smem, vmem, vmem, vmem, vmem],
        out_specs=[hbm, hbm, hbm, vmem],
        scratch_shapes=[
            pltpu.VMEM((rows + slots, node_rows), jnp.bfloat16),
            pltpu.VMEM((rows + slots, remote_rows), jnp.bfloat16),
            pltpu.VMEM((rows, width), jnp.float32),
            pltpu.SMEM((tiles + 1,), jnp.int32),
            pltpu.SMEM((blocks,), jnp.int32),
            pltpu.SMEM((GROUP + 1,), jnp.int32),
            pltpu.VMEM((blocks, block_width), jnp.int32),
            pltpu.VMEM((blocks, block_width), jnp.int32),
            pltpu.VMEM((blocks, block_width), jnp.int32),
            pltpu.VMEM((pieces * slots, CHUNK), jnp.float32),
            pltpu.SemaphoreType.DMA((3,)),
        ],
        compiler_params=params(58),
        cost_estimate=estimate(
            4 * (tiles + blocks // 4) * pieces * slots * CHUNK * block_width
            + 2 * rows * node_rows * width,
            2 * rows * pieces * CHUNK,
        ),
        name="build",
    )(tile_of, count, source, relation, target, own)


def pool_groups(counts_ref, counts_v, sems, table_ref, degree_ref, mean_ref, relations, extra=None):
    size = GROUP * WIN * relations
    groups = counts_ref.shape[0] // size

    def copies(i):
        some = pl.ds(pl.multiple_of(i * size, size), size)
        found = [pltpu.make_async_copy(counts_ref.at[some], counts_v.at[some], sems.at[0, i])]
        if extra is not None:
            found.append(pltpu.make_async_copy(extra[0].at[some], extra[1].at[some], sems.at[1, i]))
        return found

    def begin(i, carry):
        for copy in copies(i):
            copy.start()
        return carry

    def step(i, carry):
        for copy in copies(i):
            copy.wait()
        some = pl.ds(pl.multiple_of(i * size, size), size)
        total = jnp.dot(counts_v[some, :], table_ref[...], preferred_element_type=jnp.float32)
        if extra is not None:
            total += extra[1][some, :]
        share = 1.0 / jnp.maximum(degree_ref[i], 1.0)
        slots = WIN * relations
        for u in range(GROUP):
            mean = total[u * slots : (u + 1) * slots] * share[:, u : u + 1]
            put_means(mean.astype(jnp.bfloat16), mean_ref, i * GROUP + u, relations)
        return carry

    lax.fori_loop(0, groups, begin, 0)
    lax.fori_loop(0, groups, step, 0)


def pool_body(counts_ref, pooled_ref, table_ref, degree_ref, mean_ref, counts_v, pooled_v, sems, *, relations):
    pool_groups(
        counts_ref, counts_v, sems, table_ref, degree_ref, mean_ref, relations,
        extra=(pooled_ref, pooled_v),
    )


def pool(counts, pooled, table, degree, *, relations):
    rows, depth = counts.shape
    width = table.shape[1]
    vmem = pl.BlockSpec(memory_space=pltpu.VMEM)
    hbm = pl.BlockSpec(memory_space=pltpu.HBM)
    return pl.pallas_call(
        functools.partial(pool_body, relations=relations),
        out_shape=jax.ShapeDtypeStruct((rows // relations, relations * width), jnp.bfloat16),
        in_specs=[hbm, hbm, vmem, vmem],
        out_specs=vmem,
        scratch_shapes=[
            pltpu.VMEM(counts.shape, counts.dtype),
            pltpu.VMEM(pooled.shape, pooled.dtype),
            pltpu.SemaphoreType.DMA((2, degree.shape[0])),
        ],
        compiler_params=params(44),
        cost_estimate=estimate(2 * rows * depth * width, 2 * rows * depth),
        name="pool",
    )(counts, pooled, table, degree)


def part_body(
    side_ref, counts_ref, table_ref, degree_ref, mine_ref, other_ref, extra_ref,
    out_ref, counts_v, mean_v, sems, *, relations, last,
):
    pool_groups(counts_ref, counts_v, sems, table_ref, degree_ref, mean_v, relations)
    total = dense_sum(side_ref, mean_v, None if last else table_ref, mine_ref, other_ref, extra_ref)
    out_ref[...] = total.astype(out_ref.dtype)


def part(side, counts, table, degree, mine, other, extra, *, relations, last):
    rows, depth = counts.shape
    width = table.shape[1]
    nodes = rows // relations
    vmem = pl.BlockSpec(memory_space=pltpu.VMEM)
    smem = pl.BlockSpec(memory_space=pltpu.SMEM)
    hbm = pl.BlockSpec(memory_space=pltpu.HBM)
    return pl.pallas_call(
        functools.partial(part_body, relations=relations, last=last),
        out_shape=jax.ShapeDtypeStruct((nodes, width), jnp.bfloat16 if last else jnp.float32),
        in_specs=[smem, hbm, vmem, vmem, vmem, vmem, vmem],
        out_specs=vmem,
        scratch_shapes=[
            pltpu.VMEM(counts.shape, counts.dtype),
            pltpu.VMEM((nodes, relations * width), jnp.bfloat16),
            pltpu.SemaphoreType.DMA((1, degree.shape[0])),
        ],
        compiler_params=params(44),
        cost_estimate=estimate(
            2 * rows * depth * width + 2 * nodes * relations * width * width, 2 * rows * depth
        ),
        name="last" if last else "first",
    )(side, counts, table, degree, mine, other, extra)


def dense_sum(side_ref, mean_ref, own_ref, mine_ref, other_ref, bias_ref):
    half = other_ref.shape[0]
    mine_at = pl.multiple_of(side_ref[0] * half, half)
    other_at = pl.multiple_of((1 - side_ref[0]) * half, half)
    total = jnp.dot(
        mean_ref[:, pl.ds(mine_at, half)], mine_ref[:half], preferred_element_type=jnp.float32
    )
    total += jnp.dot(
        mean_ref[:, pl.ds(other_at, half)], other_ref[...], preferred_element_type=jnp.float32
    )
    if own_ref is not None:
        total += jnp.dot(own_ref[...], mine_ref[half:], preferred_element_type=jnp.float32)
    return total + bias_ref[...]


def dense_first_body(
    side_ref, mean_ref, own_ref, mine_ref, other_ref, bias_ref, send_ref, hidden_ref, out_ref
):
    total = dense_sum(side_ref, mean_ref, own_ref, mine_ref, other_ref, bias_ref)
    hidden_ref[...] = jnp.maximum(total, 0.0).astype(jnp.bfloat16)
    pick_body(send_ref, hidden_ref, out_ref)


def dense_second_body(side_ref, mean_ref, own_ref, mine_ref, other_ref, bias_ref, out_ref):
    total = dense_sum(side_ref, mean_ref, own_ref, mine_ref, other_ref, bias_ref)
    out_ref[...] = total.astype(jnp.bfloat16)


def pick_body(send_ref, rows_ref, out_ref):
    depth = rows_ref.shape[0]
    piece = 256

    def step(i, carry):
        rows = pl.ds(pl.multiple_of(i * piece, piece), piece)
        lanes = lax.broadcasted_iota(jnp.int32, (piece, depth), 1)
        chosen = jnp.where(send_ref[rows, :] == lanes, 1.0, 0.0).astype(jnp.bfloat16)
        out_ref[rows, :] = jnp.dot(
            chosen, rows_ref[...], preferred_element_type=jnp.float32
        ).astype(jnp.bfloat16)
        return carry

    lax.fori_loop(0, send_ref.shape[0] // piece, step, 0)


def pick(send, rows):
    vmem = pl.BlockSpec(memory_space=pltpu.VMEM)
    return pl.pallas_call(
        pick_body,
        out_shape=jax.ShapeDtypeStruct((send.shape[0], rows.shape[1]), rows.dtype),
        in_specs=[vmem, vmem],
        out_specs=vmem,
        compiler_params=params(16),
        cost_estimate=estimate(2 * send.shape[0] * rows.shape[0] * rows.shape[1], 0),
        name="pick",
    )(send, rows)


def dense(side, mean, own, mine, other, bias, send=None):
    nodes, width = own.shape
    vmem = pl.BlockSpec(memory_space=pltpu.VMEM)
    smem = pl.BlockSpec(memory_space=pltpu.SMEM)
    cost = estimate(2 * nodes * mean.shape[1] * width, 0)
    shape = jax.ShapeDtypeStruct((nodes, width), jnp.bfloat16)
    if send is None:
        return pl.pallas_call(
            dense_second_body,
            out_shape=shape,
            in_specs=[smem] + [vmem] * 5,
            out_specs=vmem,
            compiler_params=params(14),
            cost_estimate=cost,
            name="dense",
        )(side, mean, own, mine, other, bias)
    picked = jax.ShapeDtypeStruct((send.shape[0], width), jnp.bfloat16)
    return pl.pallas_call(
        dense_first_body,
        out_shape=[shape, picked],
        in_specs=[smem] + [vmem] * 6,
        out_specs=[vmem, vmem],
        compiler_params=params(16),
        cost_estimate=cost,
        name="dense",
    )(side, mean, own, mine, other, bias, send)


def weight_halves(bases, self_weight, coef):
    relations, width = coef.shape[0], bases.shape[2]
    mixed = jnp.einsum(
        "rb,bij->rij", coef, bases.astype(jnp.float32), precision=lax.Precision.HIGHEST
    ).astype(jnp.bfloat16)
    half = relations // 2
    halves = [
        jnp.concatenate([mixed[:half], self_weight[None]], axis=0),
        jnp.concatenate([mixed[half:], self_weight[None]], axis=0),
    ]
    return jnp.stack([h.reshape(-1, width) for h in halves])


def exchange(picked, weights, devices):
    rows = picked.reshape(devices, -1, picked.shape[1])
    if weights:
        halves = jnp.concatenate(weights, axis=1)
        halves = jnp.broadcast_to(halves[None], (devices // 2,) + halves.shape)
        rows = jnp.concatenate([rows, halves.reshape(devices, -1, rows.shape[2])], axis=1)
    return lax.all_to_all(rows, "dom", split_axis=0, concat_axis=0, tiled=True)


def join_weights(received, relations):
    devices, _, width = received.shape
    mine = received.reshape(devices, relations // 2 + 1, -1, width)
    mine = jnp.swapaxes(mine, 0, 1).reshape(-1, width)
    swap = [(i, i ^ 1) for i in range(devices)]
    return mine, lax.ppermute(mine[: mine.shape[0] - width], "dom", swap)


def shards(
    features,
    edge_source,
    edge_relation,
    edge_target,
    block_count,
    send_list,
    bases_first,
    self_first,
    coef_first,
    bias_first,
    bases_second,
    self_second,
    coef_second,
    bias_second,
):
    node_rows, width = features.shape
    relations = coef_first.shape[0]
    devices, slot = send_list.shape[1:]
    remote_rows = devices * slot
    side = (lax.axis_index("dom") & 1).astype(jnp.int32).reshape(1)
    send = send_list.reshape(-1, 1)
    halves = [
        weight_halves(bases_first, self_first, coef_first),
        weight_halves(bases_second, self_second, coef_second),
    ]
    incoming = exchange(pick(send, features), halves, devices)
    edges = (edge_target[0, :, 0], block_count, edge_source[0], edge_relation[0], edge_target[0])
    fits = 2 * node_rows * relations * (node_rows + remote_rows) <= WHOLE_MAX
    if fits:
        local, remote, pooled, degree = build(
            *edges, features, relations=relations, remote_rows=remote_rows
        )
    else:
        local, remote, degree = build_streamed_call(
            *edges, node_rows=node_rows, relations=relations, remote_rows=remote_rows
        )
        pooled = local_streamed(local, features, group=512)
    table = incoming[:, :slot].reshape(-1, width)
    rest = halves[0].shape[1]
    mine, other = join_weights(incoming[:, slot : slot + rest], relations)
    mine_next, other_next = join_weights(incoming[:, slot + rest :], relations)
    if fits:
        mean = pool(remote, pooled, table, degree, relations=relations)
    else:
        mean = remote_streamed(remote, table, pooled, degree, relations=relations, group=512)
    hidden, picked = dense(side, mean, features, mine, other, bias_first[None], send)
    table = exchange(picked, [], devices).reshape(-1, width)
    if fits:
        settings = dict(relations=relations)
        partial = part(
            side, local, hidden, degree, mine_next, other_next, bias_second[None], last=False, **settings
        )
        return part(
            side, remote, table, degree, mine_next, other_next, partial, last=True, **settings
        )
    pooled = local_streamed(local, hidden, group=512)
    mean = remote_streamed(remote, table, pooled, degree, relations=relations, group=512)
    return dense(side, mean, hidden, mine_next, other_next, bias_second[None])


def solution(mesh):
    placed = (
        P("dom", None),
        P("dom", None, None),
        P("dom", None, None),
        P("dom", None, None),
        P("dom"),
        P("dom", None, None),
        P(None, "dom", None),
        P("dom", None),
        P(),
        P(),
        P(None, "dom", None),
        P("dom", None),
        P(),
        P(),
    )
    return jax.shard_map(
        shards, mesh=mesh, in_specs=placed, out_specs=P("dom", None), check_vma=False
    )
```

time: 157 us -> 142 us (0.904)
  waiting for transfers between devices: 0.01 us -> 46.4 us
  blocking collectives: 37.8 us -> 0 us
  local copies, waits for them, and re-layouts: 45.2 us -> 13.9 us
  starting transfers between devices: 7.4 us -> 12.5 us
    all_to_all x1 -> x2, waiting for transfers between devices: 0.01 us -> 46.4 us  [exchange(): return lax.all_to_all(rows, 'dom', split_axis=0, concat_axis=0, tiled=True)]
    unnamed x52 -> x22, local copies, waits for them, and re-layouts: 41.7 us -> 3.8 us
    all_to_all x1 -> x0, blocking collectives: 37.8 us -> none  [exchange(): lax.all_to_all(outgoing, 'dom', split_axis=0, concat_axis=0, tiled=True)]
    all_to_all x1 -> x2, starting transfers between devices: 7.32 us -> 12.5 us  [exchange(): return lax.all_to_all(rows, 'dom', split_axis=0, concat_axis=0, tiled=True)]
    transpose x4 -> x3, local copies, waits for them, and re-layouts: 0.17 us -> 3.64 us  [join_weights(): mine = jnp.swapaxes(mine, 0, 1).reshape(-1, width)]
    slice x6 -> x5, local copies, waits for them, and re-layouts: 1.08 us -> 2.99 us  [the longest x4 1.91 us: join_weights(): return (mine, lax.ppermute(mine[:mine.shape[0] - width], 'dom', swap))]
    pallas_call x6 -> x4, Pallas kernels: 58.2 us -> 58.7 us  [the longest x1 31.5 us: build(): pl.pallas_call(functools.partial(build_body, tiles=tiles, relations=relat...]
  transfers between devices with their start and end apart: 3 -> 4, of which waited for: 0 -> 2; matrix products, arithmetic and copies ran while one was open for 0% -> 3% of each run, Pallas kernels for 36% -> 38%
where the time goes in v1:
time: 142 us; the launch traced here: 141 us
  Pallas kernels  64.1 us (45%)
  waiting for transfers between devices  46.4 us (33%)
  local copies, waits for them, and re-layouts  13.9 us (10%)
  starting transfers between devices  12.5 us (9%)
  matrix products  1.94 us (1%)
  other arithmetic  1.46 us (1%)
    all_to_all x2, waiting for transfers between devices, exchange(): return lax.all_to_all(rows, 'dom', split_axis=0, concat_axis=0, tiled=True)  46.4 us
    pallas_call x1, Pallas kernels, build(): pl.pallas_call(functools.partial(build_body, tiles=tiles, relations=relat...  31.5 us
    pallas_call x2, Pallas kernels, part(): pl.pallas_call(functools.partial(part_body, relations=relations, last=las...  18.2 us
    all_to_all x2, starting transfers between devices, exchange(): return lax.all_to_all(rows, 'dom', split_axis=0, concat_axis=0, tiled=True)  12.5 us
    pallas_call x1, Pallas kernels, pool(): pl.pallas_call(functools.partial(pool_body, relations=relations), out_sha...  9.08 us
    unnamed x22, local copies, waits for them, and re-layouts  3.8 us
    pallas_call x1, Pallas kernels, dense(): pl.pallas_call(dense_first_body, out_shape=[shape, picked], in_specs=[sme...  3.78 us
    transpose x3, local copies, waits for them, and re-layouts, join_weights(): mine = jnp.swapaxes(mine, 0, 1).reshape(-1, width)  3.64 us
  transfers between devices with their start and end apart: 4, of which 2 were waited for; matrix products, arithmetic and copies ran while one was open for 3% of the time, Pallas kernels for 38%

profile of v1, /device:TPU:0, one launch (start us, length us, event | category | flops | bytes accessed | tf_op | source)
XLA Modules:
  0.0 141.2 jit_solution(18126771033763766289)
XLA Ops:
  0.0 0.9 copy-done
  0.9 0.9 convolution_convert_fusion
  1.8 0.7 copy.24
  2.5 1.1 convolution_convert_fusion.1
  3.6 0.7 copy.19
  4.3 1.2 reshape.49.send_ref
  5.7 0.0 copy-start.4
  5.7 1.0 copy-done.4
  6.7 1.6 %pick.1 = bf16[1024,256]{1,0:T(8,128)(2,1)S(1)} custom-call(s32[1024,1]{1,0:T(8,128)S(1)} %reshape.49.send_ref, bf16[1024,256]{1,0:T(8,128)(2,1)S(1)} %copy-done.4), custom_call_target="tpu_custom_call" | custom-call | flops 536870912 | tf_op jit(solution)/shard_map/pick/pallas_call | solution.py:503
  8.3 0.1 broadcast_in_dim.22
  8.4 1.4 pad_maximum_fusion
  9.8 7.4 %all-to-all-start = ((bf16[32,112,256]{2,1,0:T(8,128)(2,1)}), bf16[32,112,256]{2,1,0:T(8,128)(2,1)}, u32[]{:S(2)}, u32[]{:S(2)}) async-start(bf16[32,112,256]{2,1,0:T(8,128)(2,1)} %pad_maximum_fusion), calls=%async_computation | async-start | bytes 3670016 | tf_op jit(solution)/shard_map/all_to_all | solution.py:561
  17.9 0.7 slice_reduce_fusion.tile_ref
  18.6 41.8 %all-to-all-done = bf16[32,112,256]{2,1,0:T(8,128)(2,1)} async-done(((bf16[32,112,256]{2,1,0:T(8,128)(2,1)}), bf16[32,112,256]{2,1,0:T(8,128)(2,1)}, u32[]{:S(2)}, u32[]{:S(2)}) %all-to-all-start) | async-done | bytes 1835040 | tf_op jit(solution)/shard_map/all_to_all | solution.py:561
  60.4 1.4 slice_bitcast_fusion
  61.8 0.1 slice.54
  61.8 1.0 copy.29
  62.8 31.5 %build.1 = (bf16[8192,1024]{1,0:T(8,128)(2,1)}, bf16[8192,1024]{1,0:T(8,128)(2,1)}, f32[8192,256]{1,0:T(8,128)}, f32[8,128,8]{2,1,0:T(8,128)}) custom-call(s32[128]{0:T(128)} %slice_reduce_fusion.tile_ref, s32[1]{0:T(128)S(6)} %copy.41.count_ref, s32[128,128]{1,0:T(8,128)} %bitcast.51, s32[128,128]{1,0:T(8,128)} %bitcast.52, s32[128,128]{1,0:T(8,128)} %bitcast.48, ...), custom_call_target="tpu_custom_call" | custom-call | flops 17179869184 | bytes 33554432 | tf_op jit(solution)/shard_map/build/pallas_call | solution.py:326
  94.3 1.1 copy.28
  95.4 0.1 slice.56
  95.5 0.8 copy.32
  96.3 1.1 slice.52
  97.4 0.0 copy-start.7
  97.5 9.1 %pool.1.mean_ref = bf16[1024,2048]{1,0:T(8,128)(2,1)S(1)} custom-call(bf16[8192,1024]{1,0:T(8,128)(2,1)} %get-tuple-element.11.counts_ref, f32[8192,256]{1,0:T(8,128)} %get-tuple-element.12.pooled_ref, bf16[1024,256]{1,0:T(8,128)(2,1)S(1)} %bitcast.43, f32[8,128,8]{2,1,0:T(8,128)S(1)} %copy-done.1), custom_call_target="tpu_custom_call" | custom-call | flops 4294967296 | bytes 16777216 | tf_op jit(solution)/shard_map/pool/pallas_call | solution.py:407
  106.6 3.8 %dense.1 = (bf16[1024,256]{1,0:T(8,128)(2,1)S(1)}, bf16[1024,256]{1,0:T(8,128)(2,1)}) custom-call(s32[1]{0:T(128)} %bitcast.side_ref, bf16[1024,2048]{1,0:T(8,128)(2,1)S(1)} %pool.1.mean_ref, bf16[1024,256]{1,0:T(8,128)(2,1)S(1)} %copy-done.5, bf16[1280,256]{1,0:T(8,128)(2,1)S(1)} %bitcast.41, bf16[1024,256]{1,0:T(8,128)(2,1)S(1)} %collective-permute-done.other_ref, ...), custom_call_target="tpu_custom_call" | custom-call | flops 1073741824 | tf_op jit(solution)/shard_map/dense/pallas_call | solution.py:531
  110.4 0.8 copy-done.2
  111.1 5.0 %all-to-all-start.1 = ((bf16[32,32,256]{2,1,0:T(8,128)(2,1)}), bf16[32,32,256]{2,1,0:T(8,128)(2,1)S(1)}, u32[]{:S(2)}, u32[]{:S(2)}) async-start(bf16[32,32,256]{2,1,0:T(8,128)(2,1)} %bitcast.21), calls=%async_computation.1 | async-start | bytes 1048576 | tf_op jit(solution)/shard_map/all_to_all | solution.py:561
  116.2 1.1 copy.31
  117.3 1.0 copy-done.3
  118.4 8.7 %first.1.extra_ref = f32[1024,256]{1,0:T(8,128)S(1)} custom-call(s32[1]{0:T(128)} %bitcast.side_ref, bf16[8192,1024]{1,0:T(8,128)(2,1)} %get-tuple-element.15.counts_ref, bf16[1024,256]{1,0:T(8,128)(2,1)S(1)} %copy-done.3, f32[8,128,8]{2,1,0:T(8,128)S(1)} %copy-done.1, bf16[1280,256]{1,0:T(8,128)(2,1)S(1)} %bitcast.39, ...), custom_call_target="tpu_custom_call" | custom-call | flops 5368709120 | bytes 16777216 | tf_op jit(solution)/shard_map/first/pallas_call | solution.py:439
  127.1 4.7 %all-to-all-done.1 = bf16[32,32,256]{2,1,0:T(8,128)(2,1)S(1)} async-done(((bf16[32,32,256]{2,1,0:T(8,128)(2,1)}), bf16[32,32,256]{2,1,0:T(8,128)(2,1)S(1)}, u32[]{:S(2)}, u32[]{:S(2)}) %all-to-all-start.1) | async-done | bytes 524320 | tf_op jit(solution)/shard_map/all_to_all | solution.py:561
  131.8 9.4 %last.1 = bf16[1024,256]{1,0:T(8,128)(2,1)} custom-call(s32[1]{0:T(128)} %bitcast.side_ref, bf16[8192,1024]{1,0:T(8,128)(2,1)} %get-tuple-element.11.counts_ref, bf16[1024,256]{1,0:T(8,128)(2,1)S(1)} %bitcast.42, f32[8,128,8]{2,1,0:T(8,128)S(1)} %copy-done.1, bf16[1280,256]{1,0:T(8,128)(2,1)S(1)} %bitcast.40, ...), custom_call_target="tpu_custom_call" | custom-call | flops 5368709120 | bytes 16777216 | tf_op jit(solution)/shard_map/last/pallas_call | solution.py:439
  (27 shorter events, 0.2 us)
Async XLA Ops:
  0.0 0.9 copy-start
  5.7 1.0 copy-start.4
  9.8 8.1 %copy-start.10 = (s32[1,128,128]{2,1,0:T(8,128)S(1)}, s32[1,128,128]{2,1,0:T(8,128)}, u32[]{:S(2)}) copy-start(s32[1,128,128]{2,1,0:T(8,128)} %param.17) | copy-start | bytes 196612
  9.8 50.5 %all-to-all-start = ((bf16[32,112,256]{2,1,0:T(8,128)(2,1)}), bf16[32,112,256]{2,1,0:T(8,128)(2,1)}, u32[]{:S(2)}, u32[]{:S(2)}) async-start(bf16[32,112,256]{2,1,0:T(8,128)(2,1)} %pad_maximum_fusion), calls=%async_computation | async-start | bytes 3670016 | tf_op jit(solution)/shard_map/all_to_all | solution.py:561
  61.7 32.5 %copy-start.9 = (bf16[5,32,8,256]{3,2,0,1:T(8,128)(2,1)}, bf16[5,32,8,256]{3,2,0,1:T(8,128)(2,1)S(1)}, u32[]{:S(2)}) copy-start(bf16[5,32,8,256]{3,2,0,1:T(8,128)(2,1)S(1)} %get-tuple-element.18) | copy-start | bytes 1966084
  61.8 33.7 %copy-start.8 = (bf16[5,32,8,256]{3,2,0,1:T(8,128)(2,1)}, bf16[5,32,8,256]{3,2,0,1:T(8,128)(2,1)S(1)}, u32[]{:S(2)}) copy-start(bf16[5,32,8,256]{3,2,0,1:T(8,128)(2,1)S(1)} %get-tuple-element.17) | copy-start | bytes 1966084
  62.8 43.8 %collective-permute-start = (bf16[1024,256]{1,0:T(8,128)(2,1)}, bf16[1024,256]{1,0:T(8,128)(2,1)S(1)}, u32[]{:S(2)}, u32[]{:S(2)}) collective-permute-start(bf16[1024,256]{1,0:T(8,128)(2,1)} %bitcast.19), channel_id=1, source_target_pairs={{0,1},{1,0},{2,3},{3,2},{4,5},{5,4},{6,7},{7,6},{8,9},{9,8},{10,11... | collective-permute-start | bytes 1572872 | tf_op jit(solution)/shard_map/ppermute | solution.py:569
  95.4 2.0 %copy-start.1 = (f32[8,128,8]{2,1,0:T(8,128)S(1)}, f32[8,128,8]{2,1,0:T(8,128)}, u32[]{:S(2)}) copy-start(f32[8,128,8]{2,1,0:T(8,128)} %get-tuple-element.13.degree_ref) | copy-start | bytes 98308
  96.3 21.0 %collective-permute-start.1 = (bf16[1024,256]{1,0:T(8,128)(2,1)}, bf16[1024,256]{1,0:T(8,128)(2,1)S(1)}, u32[]{:S(2)}, u32[]{:S(2)}) collective-permute-start(bf16[1024,256]{1,0:T(8,128)(2,1)} %bitcast.27), channel_id=1, source_target_pairs={{0,1},{1,0},{2,3},{3,2},{4,5},{5,4},{6,7},{7,6},{8,9},{9,8},{10,11... | collective-permute-start | bytes 1572872 | tf_op jit(solution)/shard_map/ppermute | solution.py:569
  97.4 9.1 %copy-start.5 = (bf16[1024,256]{1,0:T(8,128)(2,1)S(1)}, bf16[1024,256]{1,0:T(8,128)(2,1)}, u32[]{:S(2)}) copy-start(bf16[1024,256]{1,0:T(8,128)(2,1)} %own_ref.3) | copy-start | bytes 1572868
  97.4 9.1 %copy-start.7 = (f32[256]{0:T(256)S(1)}, f32[256]{0:T(256)}, u32[]{:S(2)}) copy-start(f32[256]{0:T(256)} %param.23) | copy-start | bytes 3076
  110.4 0.8 copy-start.2
  111.1 6.2 %copy-start.6 = (f32[256]{0:T(256)S(1)}, f32[256]{0:T(256)}, u32[]{:S(2)}) copy-start(f32[256]{0:T(256)} %param.27) | copy-start | bytes 3076
  111.1 20.6 %all-to-all-start.1 = ((bf16[32,32,256]{2,1,0:T(8,128)(2,1)}), bf16[32,32,256]{2,1,0:T(8,128)(2,1)S(1)}, u32[]{:S(2)}, u32[]{:S(2)}) async-start(bf16[32,32,256]{2,1,0:T(8,128)(2,1)} %bitcast.21), calls=%async_computation.1 | async-start | bytes 1048576 | tf_op jit(solution)/shard_map/all_to_all | solution.py:561
  117.3 1.0 copy-start.3

commit v2 on v1

--- a/solution.py
+++ b/solution.py
@@ -358,7 +358,9 @@
     )(tile_of, count, source, relation, target, own)
 
 
-def pool_groups(counts_ref, counts_v, sems, table_ref, degree_ref, mean_ref, relations, extra=None):
+def pool_groups(
+    counts_ref, counts_v, sems, table_ref, degree_ref, mean_ref, relations, ready=None, extra=None
+):
     size = GROUP * WIN * relations
     groups = counts_ref.shape[0] // size
 
@@ -389,57 +391,199 @@
         return carry
 
     lax.fori_loop(0, groups, begin, 0)
+    if ready is not None:
+        ready()
     lax.fori_loop(0, groups, step, 0)
 
 
-def pool_body(counts_ref, pooled_ref, table_ref, degree_ref, mean_ref, counts_v, pooled_v, sems, *, relations):
+def copy_table(incoming_ref, table_ref, slot):
+    for device in range(incoming_ref.shape[0]):
+        table_ref[device * slot : (device + 1) * slot, :] = incoming_ref[device, :slot, :]
+
+
+def pool_body(
+    counts_ref, pooled_ref, incoming_ref, degree_ref, mean_ref,
+    counts_v, pooled_v, table_v, sems, *, relations, slot,
+):
+    def ready():
+        copy_table(incoming_ref, table_v, slot)
+
     pool_groups(
-        counts_ref, counts_v, sems, table_ref, degree_ref, mean_ref, relations,
+        counts_ref, counts_v, sems, table_v, degree_ref, mean_ref, relations, ready,
         extra=(pooled_ref, pooled_v),
     )
 
 
-def pool(counts, pooled, table, degree, *, relations):
+def pool(counts, pooled, incoming, degree, *, relations, slot):
     rows, depth = counts.shape
-    width = table.shape[1]
+    width = incoming.shape[2]
     vmem = pl.BlockSpec(memory_space=pltpu.VMEM)
     hbm = pl.BlockSpec(memory_space=pltpu.HBM)
     return pl.pallas_call(
-        functools.partial(pool_body, relations=relations),
+        functools.partial(pool_body, relations=relations, slot=slot),
         out_shape=jax.ShapeDtypeStruct((rows // relations, relations * width), jnp.bfloat16),
         in_specs=[hbm, hbm, vmem, vmem],
         out_specs=vmem,
         scratch_shapes=[
             pltpu.VMEM(counts.shape, counts.dtype),
             pltpu.VMEM(pooled.shape, pooled.dtype),
+            pltpu.VMEM((depth, width), jnp.bfloat16),
             pltpu.SemaphoreType.DMA((2, degree.shape[0])),
         ],
         compiler_params=params(44),
         cost_estimate=estimate(2 * rows * depth * width, 2 * rows * depth),
         name="pool",
-    )(counts, pooled, table, degree)
-
-
-def part_body(
-    side_ref, counts_ref, table_ref, degree_ref, mine_ref, other_ref, extra_ref,
-    out_ref, counts_v, mean_v, sems, *, relations, last,
+    )(counts, pooled, incoming, degree)
+
+
+def pick_rows(send_ref, rows_ref, emit):
+    devices, slot = send_ref.shape
+    depth = rows_ref.shape[0]
+    columns = send_ref[...].astype(jnp.float32).T.astype(jnp.int32)
+    lanes = lax.broadcasted_iota(jnp.int32, (slot, depth), 1)
+    step = 8
+    for start in range(0, devices, step):
+        chosen = jnp.concatenate(
+            [
+                jnp.where(columns[:, device : device + 1] == lanes, 1.0, 0.0).astype(jnp.bfloat16)
+                for device in range(start, start + step)
+            ],
+            axis=0,
+        )
+        picked = jnp.dot(chosen, rows_ref[...], preferred_element_type=jnp.float32)
+        for k in range(step):
+            emit(start + k, picked[k * slot : (k + 1) * slot].astype(jnp.bfloat16))
+
+
+def middle_body(
+    side_ref, mean_ref, own_ref, incoming_ref, swapped_ref, bias_ref, send_ref,
+    hidden_ref, out_ref, self_ref, weights_v, *, relations, slot,
+):
+    width = own_ref.shape[1]
+    half = relations // 2
+    devices = incoming_ref.shape[0]
+    piece = width // devices
+    block = (half + 1) * width
+    for device in range(devices):
+        for m in range(half + 1):
+            at = m * width + device * piece
+            weights_v[at : at + piece, :] = incoming_ref[
+                device, slot + m * piece : slot + (m + 1) * piece, :
+            ]
+            weights_v[block + at : block + at + piece, :] = swapped_ref[
+                device, m * piece : (m + 1) * piece, :
+            ]
+    side = side_ref[0]
+    mine_at = pl.multiple_of(side * (half * width), width)
+    other_at = pl.multiple_of((1 - side) * (half * width), width)
+    own_at = pl.multiple_of(half * width + side * block, width)
+    next_at = pl.multiple_of(half * width + (1 - side) * block, width)
+    self_ref[...] = weights_v[pl.ds(next_at, width), :]
+    total = jnp.dot(
+        mean_ref[:, pl.ds(mine_at, half * width)],
+        weights_v[: half * width, :],
+        preferred_element_type=jnp.float32,
+    )
+    total += jnp.dot(
+        mean_ref[:, pl.ds(other_at, half * width)],
+        weights_v[block : block + half * width, :],
+        preferred_element_type=jnp.float32,
+    )
+    total += jnp.dot(
+        own_ref[...], weights_v[pl.ds(own_at, width), :], preferred_element_type=jnp.float32
+    )
+    hidden_ref[...] = jnp.maximum(total + bias_ref[...], 0.0).astype(jnp.bfloat16)
+
+    def emit(device, picked):
+        out_ref[device, :, :] = picked
+
+    pick_rows(send_ref, hidden_ref, emit)
+
+
+def middle(side, mean, own, incoming, swapped, bias, send, *, relations):
+    nodes, width = own.shape
+    devices, slot = send.shape
+    vmem = pl.BlockSpec(memory_space=pltpu.VMEM)
+    smem = pl.BlockSpec(memory_space=pltpu.SMEM)
+    return pl.pallas_call(
+        functools.partial(middle_body, relations=relations, slot=slot),
+        out_shape=[
+            jax.ShapeDtypeStruct((nodes, width), jnp.bfloat16),
+            jax.ShapeDtypeStruct((devices, slot, width), jnp.bfloat16),
+            jax.ShapeDtypeStruct((width, width), jnp.bfloat16),
+        ],
+        in_specs=[smem] + [vmem] * 6,
+        out_specs=[vmem] * 3,
+        scratch_shapes=[pltpu.VMEM(((relations + 2) * width, width), jnp.bfloat16)],
+        compiler_params=params(20),
+        cost_estimate=estimate(2 * nodes * mean.shape[1] * width, 0),
+        name="middle",
+    )(side, mean, own, incoming, swapped, bias, send)
+
+
+def first_body(
+    class_ref, counts_ref, own_ref, degree_ref, self_ref, bias_ref, *refs, relations
+):
+    pieces, (out_ref, weights_ref, counts_v, mean_v, sems) = refs[:relations], refs[relations:]
+    width = own_ref.shape[1]
+
+    def ready():
+        for k, piece in enumerate(pieces):
+            at = pl.multiple_of((class_ref[0] ^ k) * width, width)
+            weights_ref[pl.ds(at, width), :] = piece[...]
+
+    pool_groups(counts_ref, counts_v, sems, own_ref, degree_ref, mean_v, relations, ready)
+    total = jnp.dot(mean_v[...], weights_ref[...], preferred_element_type=jnp.float32)
+    total += jnp.dot(own_ref[...], self_ref[...], preferred_element_type=jnp.float32)
+    out_ref[...] = total + bias_ref[...]
+
+
+def first(class_, counts, own, degree, self_weight, bias, pieces, *, relations):
+    rows, depth = counts.shape
+    nodes, width = own.shape
+    vmem = pl.BlockSpec(memory_space=pltpu.VMEM)
+    smem = pl.BlockSpec(memory_space=pltpu.SMEM)
+    hbm = pl.BlockSpec(memory_space=pltpu.HBM)
+    return pl.pallas_call(
+        functools.partial(first_body, relations=relations),
+        out_shape=[
+            jax.ShapeDtypeStruct((nodes, width), jnp.float32),
+            jax.ShapeDtypeStruct((relations * width, width), jnp.bfloat16),
+        ],
+        in_specs=[smem, hbm] + [vmem] * (4 + relations),
+        out_specs=[vmem, vmem],
+        scratch_shapes=[
+            pltpu.VMEM(counts.shape, counts.dtype),
+            pltpu.VMEM((nodes, relations * width), jnp.bfloat16),
+            pltpu.SemaphoreType.DMA((1, degree.shape[0])),
+        ],
+        compiler_params=params(44),
+        cost_estimate=estimate(
+            2 * rows * depth * width + 2 * nodes * relations * width * width, 2 * rows * depth
+        ),
+        name="first",
+    )(class_, counts, own, degree, self_weight, bias, *pieces)
+
+
+def last_body(
+    counts_ref, table_ref, degree_ref, weights_ref, partial_ref, out_ref,
+    counts_v, mean_v, sems, *, relations,
 ):
     pool_groups(counts_ref, counts_v, sems, table_ref, degree_ref, mean_v, relations)
-    total = dense_sum(side_ref, mean_v, None if last else table_ref, mine_ref, other_ref, extra_ref)
-    out_ref[...] = total.astype(out_ref.dtype)
-
-
-def part(side, counts, table, degree, mine, other, extra, *, relations, last):
+    total = jnp.dot(mean_v[...], weights_ref[...], preferred_element_type=jnp.float32)
+    out_ref[...] = (total + partial_ref[...]).astype(out_ref.dtype)
+
+
+def last(counts, table, degree, weights, partial, *, relations):
     rows, depth = counts.shape
     width = table.shape[1]
     nodes = rows // relations
     vmem = pl.BlockSpec(memory_space=pltpu.VMEM)
-    smem = pl.BlockSpec(memory_space=pltpu.SMEM)
     hbm = pl.BlockSpec(memory_space=pltpu.HBM)
     return pl.pallas_call(
-        functools.partial(part_body, relations=relations, last=last),
-        out_shape=jax.ShapeDtypeStruct((nodes, width), jnp.bfloat16 if last else jnp.float32),
-        in_specs=[smem, hbm, vmem, vmem, vmem, vmem, vmem],
+        functools.partial(last_body, relations=relations),
+        out_shape=jax.ShapeDtypeStruct((nodes, width), jnp.bfloat16),
+        in_specs=[hbm] + [vmem] * 4,
         out_specs=vmem,
         scratch_shapes=[
             pltpu.VMEM(counts.shape, counts.dtype),
@@ -450,123 +594,132 @@
         cost_estimate=estimate(
             2 * rows * depth * width + 2 * nodes * relations * width * width, 2 * rows * depth
         ),
-        name="last" if last else "first",
-    )(side, counts, table, degree, mine, other, extra)
-
-
-def dense_sum(side_ref, mean_ref, own_ref, mine_ref, other_ref, bias_ref):
-    half = other_ref.shape[0]
-    mine_at = pl.multiple_of(side_ref[0] * half, half)
-    other_at = pl.multiple_of((1 - side_ref[0]) * half, half)
-    total = jnp.dot(
-        mean_ref[:, pl.ds(mine_at, half)], mine_ref[:half], preferred_element_type=jnp.float32
-    )
-    total += jnp.dot(
-        mean_ref[:, pl.ds(other_at, half)], other_ref[...], preferred_element_type=jnp.float32
-    )
-    if own_ref is not None:
-        total += jnp.dot(own_ref[...], mine_ref[half:], preferred_element_type=jnp.float32)
-    return total + bias_ref[...]
-
-
-def dense_first_body(
-    side_ref, mean_ref, own_ref, mine_ref, other_ref, bias_ref, send_ref, hidden_ref, out_ref
-):
-    total = dense_sum(side_ref, mean_ref, own_ref, mine_ref, other_ref, bias_ref)
-    hidden_ref[...] = jnp.maximum(total, 0.0).astype(jnp.bfloat16)
-    pick_body(send_ref, hidden_ref, out_ref)
-
-
-def dense_second_body(side_ref, mean_ref, own_ref, mine_ref, other_ref, bias_ref, out_ref):
-    total = dense_sum(side_ref, mean_ref, own_ref, mine_ref, other_ref, bias_ref)
-    out_ref[...] = total.astype(jnp.bfloat16)
-
-
-def pick_body(send_ref, rows_ref, out_ref):
-    depth = rows_ref.shape[0]
-    piece = 256
-
-    def step(i, carry):
-        rows = pl.ds(pl.multiple_of(i * piece, piece), piece)
-        lanes = lax.broadcasted_iota(jnp.int32, (piece, depth), 1)
-        chosen = jnp.where(send_ref[rows, :] == lanes, 1.0, 0.0).astype(jnp.bfloat16)
-        out_ref[rows, :] = jnp.dot(
-            chosen, rows_ref[...], preferred_element_type=jnp.float32
-        ).astype(jnp.bfloat16)
-        return carry
-
-    lax.fori_loop(0, send_ref.shape[0] // piece, step, 0)
-
-
-def pick(send, rows):
+        name="last",
+    )(counts, table, degree, weights, partial)
+
+
+def pack_body(
+    coef_first_ref, coef_second_ref, features_ref, send_ref, bases_first_ref, self_first_ref,
+    bases_second_ref, self_second_ref, out_ref,
+):
+    relations, bases = coef_first_ref.shape
+    devices, slot = send_ref.shape
+    piece = self_first_ref.shape[0]
+    half = relations // 2
+
+    def mix(coef_ref, bases_ref):
+        mixed = []
+        for relation in range(relations):
+            total = coef_ref[relation, 0] * bases_ref[0].astype(jnp.float32)
+            for base in range(1, bases):
+                total += coef_ref[relation, base] * bases_ref[base].astype(jnp.float32)
+            mixed.append(total.astype(jnp.bfloat16))
+        return mixed
+
+    first = mix(coef_first_ref, bases_first_ref)
+    second = mix(coef_second_ref, bases_second_ref)
+    own = [self_first_ref[...], self_second_ref[...]]
+    for device in range(devices):
+        side = device % 2
+        rows = first[side * half : (side + 1) * half] + [own[side], second[device % relations]]
+        for k, value in enumerate(rows):
+            at = slot + k * piece
+            out_ref[device, at : at + piece, :] = value
+
+    def emit(device, picked):
+        out_ref[device, :slot, :] = picked
+
+    pick_rows(send_ref, features_ref, emit)
+
+
+def pack(features, send, bases_first, self_first, coef_first, bases_second, self_second, coef_second):
+    devices, slot = send.shape
+    relations = coef_first.shape[0]
+    piece, width = self_first.shape
     vmem = pl.BlockSpec(memory_space=pltpu.VMEM)
-    return pl.pallas_call(
-        pick_body,
-        out_shape=jax.ShapeDtypeStruct((send.shape[0], rows.shape[1]), rows.dtype),
-        in_specs=[vmem, vmem],
+    smem = pl.BlockSpec(memory_space=pltpu.SMEM)
+    return pl.pallas_call(
+        pack_body,
+        out_shape=jax.ShapeDtypeStruct(
+            (devices, slot + (relations // 2 + 2) * piece, width), jnp.bfloat16
+        ),
+        in_specs=[smem, smem] + [vmem] * 6,
+        out_specs=vmem,
+        compiler_params=params(24),
+        cost_estimate=estimate(2 * devices * slot * features.size, 0),
+        name="pack",
+    )(coef_first, coef_second, features, send, bases_first, self_first, bases_second, self_second)
+
+
+def dense_body(mean_ref, own_ref, weights_ref, bias_ref, out_ref, *, last):
+    depth = mean_ref.shape[1]
+    total = jnp.dot(mean_ref[...], weights_ref[:depth], preferred_element_type=jnp.float32)
+    total += jnp.dot(own_ref[...], weights_ref[depth:], preferred_element_type=jnp.float32)
+    total += bias_ref[...]
+    out_ref[...] = (total if last else jnp.maximum(total, 0.0)).astype(jnp.bfloat16)
+
+
+def dense(mean, own, weights, bias, *, last):
+    nodes, width = own.shape
+    vmem = pl.BlockSpec(memory_space=pltpu.VMEM)
+    return pl.pallas_call(
+        functools.partial(dense_body, last=last),
+        out_shape=jax.ShapeDtypeStruct((nodes, width), jnp.bfloat16),
+        in_specs=[vmem] * 4,
         out_specs=vmem,
         compiler_params=params(16),
-        cost_estimate=estimate(2 * send.shape[0] * rows.shape[0] * rows.shape[1], 0),
-        name="pick",
-    )(send, rows)
-
-
-def dense(side, mean, own, mine, other, bias, send=None):
-    nodes, width = own.shape
-    vmem = pl.BlockSpec(memory_space=pltpu.VMEM)
-    smem = pl.BlockSpec(memory_space=pltpu.SMEM)
-    cost = estimate(2 * nodes * mean.shape[1] * width, 0)
-    shape = jax.ShapeDtypeStruct((nodes, width), jnp.bfloat16)
-    if send is None:
-        return pl.pallas_call(
-            dense_second_body,
-            out_shape=shape,
-            in_specs=[smem] + [vmem] * 5,
-            out_specs=vmem,
-            compiler_params=params(14),
-            cost_estimate=cost,
-            name="dense",
-        )(side, mean, own, mine, other, bias)
-    picked = jax.ShapeDtypeStruct((send.shape[0], width), jnp.bfloat16)
-    return pl.pallas_call(
-        dense_first_body,
-        out_shape=[shape, picked],
-        in_specs=[smem] + [vmem] * 6,
-        out_specs=[vmem, vmem],
-        compiler_params=params(16),
-        cost_estimate=cost,
+        cost_estimate=estimate(2 * nodes * mean.shape[1] * width, 0),
         name="dense",
-    )(side, mean, own, mine, other, bias, send)
-
-
-def weight_halves(bases, self_weight, coef):
-    relations, width = coef.shape[0], bases.shape[2]
+    )(mean, own, weights, bias)
+
+
+def mix_weights(bases, self_weight, coef):
     mixed = jnp.einsum(
         "rb,bij->rij", coef, bases.astype(jnp.float32), precision=lax.Precision.HIGHEST
     ).astype(jnp.bfloat16)
+    return jnp.concatenate([mixed, self_weight[None]], axis=0)
+
+
+def general_layers(
+    features, edges, send, weights_first, weights_second, bias_first, bias_second, relations
+):
+    node_rows, width = features.shape
+    devices, slot = send.shape
     half = relations // 2
-    halves = [
-        jnp.concatenate([mixed[:half], self_weight[None]], axis=0),
-        jnp.concatenate([mixed[half:], self_weight[None]], axis=0),
-    ]
-    return jnp.stack([h.reshape(-1, width) for h in halves])
-
-
-def exchange(picked, weights, devices):
-    rows = picked.reshape(devices, -1, picked.shape[1])
-    if weights:
-        halves = jnp.concatenate(weights, axis=1)
-        halves = jnp.broadcast_to(halves[None], (devices // 2,) + halves.shape)
-        rows = jnp.concatenate([rows, halves.reshape(devices, -1, rows.shape[2])], axis=1)
-    return lax.all_to_all(rows, "dom", split_axis=0, concat_axis=0, tiled=True)
-
-
-def join_weights(received, relations):
-    devices, _, width = received.shape
-    mine = received.reshape(devices, relations // 2 + 1, -1, width)
-    mine = jnp.swapaxes(mine, 0, 1).reshape(-1, width)
     swap = [(i, i ^ 1) for i in range(devices)]
-    return mine, lax.ppermute(mine[: mine.shape[0] - width], "dom", swap)
+    side = lax.axis_index("dom") & 1
+
+    def send_all(rows, weights):
+        rows = rows[send]
+        halves = [
+            jnp.concatenate([weights[:half], weights[relations:]], axis=0).reshape(-1, width),
+            jnp.concatenate([weights[half:relations], weights[relations:]], axis=0).reshape(-1, width),
+        ]
+        halves = jnp.broadcast_to(jnp.stack(halves)[None], (devices // 2, 2) + halves[0].shape)
+        rows = jnp.concatenate([rows, halves.reshape(devices, -1, width)], axis=1)
+        return lax.all_to_all(rows, "dom", split_axis=0, concat_axis=0, tiled=True)
+
+    def take_all(incoming):
+        mine = jnp.swapaxes(incoming[:, slot:].reshape(devices, half + 1, -1, width), 0, 1)
+        mine = mine.reshape(-1, width)
+        other = lax.ppermute(mine[: half * width], "dom", swap)
+        mine, own = mine[: half * width], mine[half * width :]
+        low, high = jnp.where(side == 0, mine, other), jnp.where(side == 0, other, mine)
+        return incoming[:, :slot].reshape(-1, width), jnp.concatenate([low, high, own], axis=0)
+
+    local, remote, degree = build_streamed_call(
+        *edges, node_rows=node_rows, relations=relations, remote_rows=devices * slot
+    )
+
+    def layer(rows, weights, bias, last):
+        incoming = send_all(rows, weights)
+        pooled = local_streamed(local, rows, group=512)
+        table, full = take_all(incoming)
+        mean = remote_streamed(remote, table, pooled, degree, relations=relations, group=512)
+        return dense(mean, rows, full, bias[None], last=last)
+
+    hidden = layer(features, weights_first, bias_first, False)
+    return layer(hidden, weights_second, bias_second, True)
 
 
 def shards(
@@ -589,45 +742,53 @@
     relations = coef_first.shape[0]
     devices, slot = send_list.shape[1:]
     remote_rows = devices * slot
-    side = (lax.axis_index("dom") & 1).astype(jnp.int32).reshape(1)
-    send = send_list.reshape(-1, 1)
-    halves = [
-        weight_halves(bases_first, self_first, coef_first),
-        weight_halves(bases_second, self_second, coef_second),
-    ]
-    incoming = exchange(pick(send, features), halves, devices)
+    send = send_list[0]
     edges = (edge_target[0, :, 0], block_count, edge_source[0], edge_relation[0], edge_target[0])
-    fits = 2 * node_rows * relations * (node_rows + remote_rows) <= WHOLE_MAX
-    if fits:
-        local, remote, pooled, degree = build(
-            *edges, features, relations=relations, remote_rows=remote_rows
+    if 2 * node_rows * relations * (node_rows + remote_rows) > WHOLE_MAX:
+        return general_layers(
+            features,
+            edges,
+            send,
+            mix_weights(bases_first, self_first, coef_first),
+            mix_weights(bases_second, self_second, coef_second),
+            bias_first,
+            bias_second,
+            relations,
         )
-    else:
-        local, remote, degree = build_streamed_call(
-            *edges, node_rows=node_rows, relations=relations, remote_rows=remote_rows
-        )
-        pooled = local_streamed(local, features, group=512)
-    table = incoming[:, :slot].reshape(-1, width)
-    rest = halves[0].shape[1]
-    mine, other = join_weights(incoming[:, slot : slot + rest], relations)
-    mine_next, other_next = join_weights(incoming[:, slot + rest :], relations)
-    if fits:
-        mean = pool(remote, pooled, table, degree, relations=relations)
-    else:
-        mean = remote_streamed(remote, table, pooled, degree, relations=relations, group=512)
-    hidden, picked = dense(side, mean, features, mine, other, bias_first[None], send)
-    table = exchange(picked, [], devices).reshape(-1, width)
-    if fits:
-        settings = dict(relations=relations)
-        partial = part(
-            side, local, hidden, degree, mine_next, other_next, bias_second[None], last=False, **settings
-        )
-        return part(
-            side, remote, table, degree, mine_next, other_next, partial, last=True, **settings
-        )
-    pooled = local_streamed(local, hidden, group=512)
-    mean = remote_streamed(remote, table, pooled, degree, relations=relations, group=512)
-    return dense(side, mean, hidden, mine_next, other_next, bias_second[None])
+    here = lax.axis_index("dom").astype(jnp.int32).reshape(1)
+    side, class_ = here & 1, here & (relations - 1)
+    outgoing = pack(
+        features, send, bases_first, self_first, coef_first, bases_second, self_second, coef_second
+    )
+    incoming = lax.all_to_all(outgoing, "dom", split_axis=0, concat_axis=0, tiled=True)
+    local, remote, pooled, degree = build(
+        *edges, features, relations=relations, remote_rows=remote_rows
+    )
+    incoming, degree = lax.optimization_barrier((incoming, degree))
+
+    def from_peer(array, mask):
+        return lax.ppermute(array, "dom", [(i, i ^ mask) for i in range(devices)])
+
+    next_at = slot + (relations // 2 + 1) * self_first.shape[0]
+    swapped = from_peer(incoming[:, slot:next_at], 1)
+    pieces = {0: incoming[:, next_at:].reshape(width, width)}
+    mask = relations // 2
+    while mask:
+        pieces.update({k | mask: from_peer(piece, mask) for k, piece in sorted(pieces.items())})
+        mask //= 2
+    pieces = [pieces[k] for k in range(relations)]
+    mean = pool(remote, pooled, incoming, degree, relations=relations, slot=slot)
+    hidden, picked, self_next = middle(
+        side, mean, features, incoming, swapped, bias_first[None], send, relations=relations
+    )
+    table = lax.all_to_all(picked, "dom", split_axis=0, concat_axis=0, tiled=True)
+    partial, weights = first(
+        class_, local, hidden, degree, self_next, bias_second[None], pieces, relations=relations
+    )
+    table, partial = lax.optimization_barrier((table, partial))
+    return last(
+        remote, table.reshape(-1, width), degree, weights, partial, relations=relations
+    )
 
 
 def solution(mesh):

time: 142 us -> 116 us (0.82)
  waiting for transfers between devices: 46.4 us -> 11.5 us
  starting transfers between devices: 12.5 us -> 20.4 us
  local copies, waits for them, and re-layouts: 13.9 us -> 19.2 us
  matrix products: 1.94 us -> 0 us
  other arithmetic: 1.46 us -> 0 us
    all_to_all x2, waiting for transfers between devices: 46.4 us -> 1.38 us  [the longest x1 1.37 us: shards(): lax.all_to_all(outgoing, 'dom', split_axis=0, concat_axis=0, tiled=True)]
    unnamed x22 -> x58, local copies, waits for them, and re-layouts: 3.8 us -> 18.5 us
    ppermute x2 -> x8, waiting for transfers between devices: 0.01 us -> 10.2 us  [from_peer(): return lax.ppermute(array, 'dom', [(i, i ^ mask) for i in range(devices)])]
    ppermute x2 -> x8, starting transfers between devices: 0.01 us -> 6.86 us  [from_peer(): return lax.ppermute(array, 'dom', [(i, i ^ mask) for i in range(devices)])]
    transpose x3 -> x0, local copies, waits for them, and re-layouts: 3.64 us -> none  [join_weights(): mine = jnp.swapaxes(mine, 0, 1).reshape(-1, width)]
    slice x7 -> x1, local copies, waits for them, and re-layouts: 3.02 us -> 0.04 us  [shards(): swapped = from_peer(incoming[:, slot:next_at], 1)]
    pallas_call x1, Pallas kernels: 31.5 us -> 29.3 us  [build(): pl.pallas_call(functools.partial(build_body, tiles=tiles, relations=relat...]
    dot_general x2 -> x0, matrix products: 1.94 us -> none  [weight_halves(): jnp.einsum('rb,bij->rij', coef, bases.astype(jnp.float32), precision=lax....]
  transfers between devices with their start and end apart: 4 -> 10, of which waited for: 2 -> 3; matrix products, arithmetic and copies ran while one was open for 3% -> 1% of each run, Pallas kernels for 38% -> 41%
where the time goes in v2:
time: 116 us; the launch traced here: 115 us
  Pallas kernels  63.2 us (54%)
  starting transfers between devices  20.4 us (18%)
  local copies, waits for them, and re-layouts  19.2 us (17%)
  waiting for transfers between devices  11.5 us (10%)
    pallas_call x1, Pallas kernels, build(): pl.pallas_call(functools.partial(build_body, tiles=tiles, relations=relat...  29.3 us
    unnamed x58, local copies, waits for them, and re-layouts  18.5 us
    ppermute x8, waiting for transfers between devices, from_peer(): return lax.ppermute(array, 'dom', [(i, i ^ mask) for i in range(devices)])  10.2 us
    pallas_call x1, Pallas kernels, last(): pl.pallas_call(functools.partial(last_body, relations=relations), out_sha...  9.38 us
    pallas_call x1, Pallas kernels, pool(): pl.pallas_call(functools.partial(pool_body, relations=relations, slot=slo...  9.07 us
    pallas_call x1, Pallas kernels, first(): pl.pallas_call(functools.partial(first_body, relations=relations), out_sh...  8.73 us
    all_to_all x1, starting transfers between devices, shards(): lax.all_to_all(outgoing, 'dom', split_axis=0, concat_axis=0, tiled=True)  7.33 us
    ppermute x8, starting transfers between devices, from_peer(): return lax.ppermute(array, 'dom', [(i, i ^ mask) for i in range(devices)])  6.86 us
  transfers between devices with their start and end apart: 10, of which 3 were waited for; matrix products, arithmetic and copies ran while one was open for 1% of the time, Pallas kernels for 41%

profile of v2, /device:TPU:0, one launch (start us, length us, event | category | flops | bytes accessed | tf_op | source)
XLA Modules:
  0.0 115.2 jit_solution(16253649587344477732)
XLA Ops:
  0.0 1.0 copy-done.2
  1.0 0.9 copy-done.4
  1.9 0.9 copy-done.5
  2.8 0.7 copy-done.6
  3.6 0.7 copy-done.8
  4.3 0.7 copy-done.9
  4.9 0.7 copy-done.10
  5.6 0.7 copy-done.11
  6.3 2.9 %pack.1 = bf16[32,80,256]{2,1,0:T(8,128)(2,1)} custom-call(f32[8,30]{1,0:T(8,128)S(1)} %copy-done.8, f32[8,30]{1,0:T(8,128)S(1)} %copy-done.9, bf16[1024,256]{1,0:T(8,128)(2,1)S(1)} %copy-done.2, s32[32,32]{1,0:T(8,128)S(1)} %bitcast.12, bf16[30,8,256]{2,1,0:T(8,128)(2,1)S(1)} %copy-done.4, bf16[8,256]{1,0:T(8,128)(2,1)S(1)} %copy-done.10, ...), custom_call_target="tpu_custom_call" | custom-call | flops 536870912 | tf_op jit(solution)/shard_map/pack/pallas_call | solution.py:641
  9.2 7.3 %all-to-all-start = ((bf16[32,80,256]{2,1,0:T(8,128)(2,1)}), bf16[32,80,256]{2,1,0:T(8,128)(2,1)S(1)}, u32[]{:S(2)}, u32[]{:S(2)}) async-start(bf16[32,80,256]{2,1,0:T(8,128)(2,1)} %pack.1), calls=%async_computation | async-start | bytes 2621440 | tf_op jit(solution)/shard_map/all_to_all | solution.py:763
  17.8 29.3 %build.1 = (bf16[8192,1024]{1,0:T(8,128)(2,1)}, bf16[8192,1024]{1,0:T(8,128)(2,1)}, f32[8192,256]{1,0:T(8,128)}, f32[8,128,8]{2,1,0:T(8,128)}) custom-call(s32[128]{0:T(128)} %slice_reduce_fusion.tile_ref, s32[1]{0:T(128)S(6)} %copy.15.count_ref, s32[128,128]{1,0:T(8,128)} %bitcast.17, s32[128,128]{1,0:T(8,128)} %bitcast.18, s32[128,128]{1,0:T(8,128)} %bitcast.16, ...), custom_call_target="tpu_custom_call" | custom-call | flops 17179869184 | bytes 33554432 | tf_op jit(solution)/shard_map/build/pallas_call | solution.py:326
  47.1 1.4 %all-to-all-done.incoming_ref = bf16[32,80,256]{2,1,0:T(8,128)(2,1)S(1)} async-done(((bf16[32,80,256]{2,1,0:T(8,128)(2,1)}), bf16[32,80,256]{2,1,0:T(8,128)(2,1)S(1)}, u32[]{:S(2)}, u32[]{:S(2)}) %all-to-all-start) | async-done | bytes 1310752 | tf_op jit(solution)/shard_map/all_to_all | solution.py:763
  48.6 1.4 %collective-permute-start = (bf16[32,40,256]{2,1,0:T(8,128)(2,1)S(1)}, bf16[32,40,256]{2,1,0:T(8,128)(2,1)S(1)}, u32[]{:S(2)}, u32[]{:S(2)}) collective-permute-start(bf16[32,40,256]{2,1,0:T(8,128)(2,1)S(1)} %slice.10), channel_id=1, source_target_pairs={{0,1},{1,0},{2,3},{3,2},{4,5},{5,4},{6,7},{7,6},{8,9},{9,8},{10,11... | collective-permute-start | bytes 1966088 | tf_op jit(solution)/shard_map/ppermute | solution.py:770
  50.0 1.0 copy-done
  51.0 9.1 %pool.1.mean_ref = bf16[1024,2048]{1,0:T(8,128)(2,1)S(1)} custom-call(bf16[8192,1024]{1,0:T(8,128)(2,1)} %get-tuple-element.18.counts_ref, f32[8192,256]{1,0:T(8,128)} %get-tuple-element.19.pooled_ref, bf16[32,80,256]{2,1,0:T(8,128)(2,1)S(1)} %all-to-all-done.incoming_ref, f32[8,128,8]{2,1,0:T(8,128)S(1)} %copy-done), custom_call_target="tpu_custom_call" | custom-call | flops 4294967296 | bytes 16777216 | tf_op jit(solution)/shard_map/pool/pallas_call | solution.py:422
  60.2 3.8 %middle.1 = (bf16[1024,256]{1,0:T(8,128)(2,1)S(1)}, bf16[32,32,256]{2,1,0:T(8,128)(2,1)}, bf16[256,256]{1,0:T(8,128)(2,1)S(1)}) custom-call(s32[1]{0:T(128)} %bitcast.3.side_ref, bf16[1024,2048]{1,0:T(8,128)(2,1)S(1)} %pool.1.mean_ref, bf16[1024,256]{1,0:T(8,128)(2,1)S(1)} %copy-done.3, bf16[32,80,256]{2,1,0:T(8,128)(2,1)S(1)} %all-to-all-done.incoming_ref, ...), custom_call_target="tpu_custom_call" | custom-call | flops 1073741824 | tf_op jit(solution)/shard_map/middle/pallas_call | solution.py:508
  64.0 0.8 copy-done.13
  65.5 6.2 %all-to-all-start.1 = ((bf16[32,32,256]{2,1,0:T(8,128)(2,1)}), bf16[32,32,256]{2,1,0:T(8,128)(2,1)S(1)}, u32[]{:S(2)}, u32[]{:S(2)}) async-start(bf16[32,32,256]{2,1,0:T(8,128)(2,1)} %get-tuple-element.23), calls=%async_computation.1 | async-start | bytes 1048576 | tf_op jit(solution)/shard_map/all_to_all | solution.py:784
  71.7 1.8 %collective-permute-start.4 = (bf16[256,256]{1,0:T(8,128)(2,1)S(1)}, bf16[256,256]{1,0:T(8,128)(2,1)S(1)}, u32[]{:S(2)}, u32[]{:S(2)}) collective-permute-start(bf16[256,256]{1,0:T(8,128)(2,1)S(1)} %slice_bitcast_fusion.refs_0_), channel_id=1, source_target_pairs={{0,4},{1,5},{2,6},{3,7},{4,0},{5,1},{6,2},{7,3},{8,12},{9,13},{10,... | collective-permute-start | bytes 393224 | tf_op jit(solution)/shard_map/ppermute | solution.py:770
  73.5 1.5 %collective-permute-start.2 = (bf16[256,256]{1,0:T(8,128)(2,1)S(1)}, bf16[256,256]{1,0:T(8,128)(2,1)S(1)}, u32[]{:S(2)}, u32[]{:S(2)}) collective-permute-start(bf16[256,256]{1,0:T(8,128)(2,1)S(1)} %slice_bitcast_fusion.refs_0_), channel_id=1, source_target_pairs={{0,2},{1,3},{2,0},{3,1},{4,6},{5,7},{6,4},{7,5},{8,10},{9,11},{10,... | collective-permute-start | bytes 393224 | tf_op jit(solution)/shard_map/ppermute | solution.py:770
  75.0 6.4 %collective-permute-done.4.refs_4_ = bf16[256,256]{1,0:T(8,128)(2,1)S(1)} collective-permute-done((bf16[256,256]{1,0:T(8,128)(2,1)S(1)}, bf16[256,256]{1,0:T(8,128)(2,1)S(1)}, u32[]{:S(2)}, u32[]{:S(2)}) %collective-permute-start.4) | collective-permute-done | bytes 131104 | tf_op jit(solution)/shard_map/ppermute | solution.py:770
  81.4 1.6 %collective-permute-start.6 = (bf16[256,256]{1,0:T(8,128)(2,1)S(1)}, bf16[256,256]{1,0:T(8,128)(2,1)S(1)}, u32[]{:S(2)}, u32[]{:S(2)}) collective-permute-start(bf16[256,256]{1,0:T(8,128)(2,1)S(1)} %collective-permute-done.4.refs_4_), channel_id=1, source_target_pairs={{0,2},{1,3},{2,0},{3,1},{4,6},{5,7},{6,4},{7,5},{8,10},{9,11},{10,... | collective-permute-start | bytes 393224 | tf_op jit(solution)/shard_map/ppermute | solution.py:770
  83.5 3.8 %collective-permute-done.6.refs_6_ = bf16[256,256]{1,0:T(8,128)(2,1)S(1)} collective-permute-done((bf16[256,256]{1,0:T(8,128)(2,1)S(1)}, bf16[256,256]{1,0:T(8,128)(2,1)S(1)}, u32[]{:S(2)}, u32[]{:S(2)}) %collective-permute-start.6) | collective-permute-done | bytes 131104 | tf_op jit(solution)/shard_map/ppermute | solution.py:770
  90.6 1.0 copy-done.14
  91.6 0.9 copy-done.16
  92.5 0.9 copy-done.18
  93.4 0.9 copy-done.20
  94.3 0.9 copy-done.22
  95.2 0.9 copy-done.24
  96.1 0.9 copy-done.26
  97.0 8.7 %first.1 = (f32[1024,256]{1,0:T(8,128)S(1)}, bf16[2048,256]{1,0:T(8,128)(2,1)S(1)}) custom-call(s32[1]{0:T(128)} %bitcast.6.class_ref, bf16[8192,1024]{1,0:T(8,128)(2,1)} %get-tuple-element.24.counts_ref, bf16[1024,256]{1,0:T(8,128)(2,1)S(1)} %copy-done.14, f32[8,128,8]{2,1,0:T(8,128)S(1)} %copy-done.1, bf16[256,256]{1,0:T(8,128)(2,1)S(1)} %copy-done.16, ...), custom_call_target="tpu_custom_call" | custom-call | flops 5368709120 | bytes 16777216 | tf_op jit(solution)/shard_map/first/pallas_call | solution.py:547
  105.8 9.4 %last.1 = bf16[1024,256]{1,0:T(8,128)(2,1)} custom-call(bf16[8192,1024]{1,0:T(8,128)(2,1)} %get-tuple-element.18.counts_ref, bf16[1024,256]{1,0:T(8,128)(2,1)S(1)} %bitcast.11, f32[8,128,8]{2,1,0:T(8,128)S(1)} %copy-done.1, bf16[2048,256]{1,0:T(8,128)(2,1)S(1)} %get-tuple-element.29.weights_ref, f32[1024,256]{1,0:T(8,128)S(1)} %get-tuple-element.30.partial_ref), custom_call_target="tpu_custom_call" | custom-call | flops 5368709120 | bytes 16777216 | tf_op jit(solution)/shard_map/last/pallas_call | solution.py:583
  (55 shorter events, 5.1 us)
Async XLA Ops:
  0.0 1.0 copy-start.2
  1.0 0.9 copy-start.4
  1.9 0.9 copy-start.5
  2.8 0.7 copy-start.6
  3.6 0.7 copy-start.8
  4.3 0.7 copy-start.9
  5.6 0.7 copy-start.11
  6.3 10.9 %copy-start.28 = (s32[1,128,128]{2,1,0:T(8,128)S(1)}, s32[1,128,128]{2,1,0:T(8,128)}, u32[]{:S(2)}) copy-start(s32[1,128,128]{2,1,0:T(8,128)} %param.17) | copy-start | bytes 196612
  9.2 39.3 %all-to-all-start = ((bf16[32,80,256]{2,1,0:T(8,128)(2,1)}), bf16[32,80,256]{2,1,0:T(8,128)(2,1)S(1)}, u32[]{:S(2)}, u32[]{:S(2)}) async-start(bf16[32,80,256]{2,1,0:T(8,128)(2,1)} %pack.1), calls=%async_computation | async-start | bytes 2621440 | tf_op jit(solution)/shard_map/all_to_all | solution.py:763
  48.6 11.6 %collective-permute-start = (bf16[32,40,256]{2,1,0:T(8,128)(2,1)S(1)}, bf16[32,40,256]{2,1,0:T(8,128)(2,1)S(1)}, u32[]{:S(2)}, u32[]{:S(2)}) collective-permute-start(bf16[32,40,256]{2,1,0:T(8,128)(2,1)S(1)} %slice.10), channel_id=1, source_target_pairs={{0,1},{1,0},{2,3},{3,2},{4,5},{5,4},{6,7},{7,6},{8,9},{9,8},{10,11... | collective-permute-start | bytes 1966088 | tf_op jit(solution)/shard_map/ppermute | solution.py:770
  50.0 1.0 copy-start
  51.0 9.1 %copy-start.3 = (bf16[1024,256]{1,0:T(8,128)(2,1)S(1)}, bf16[1024,256]{1,0:T(8,128)(2,1)}, u32[]{:S(2)}) copy-start(bf16[1024,256]{1,0:T(8,128)(2,1)} %own_ref.3) | copy-start | bytes 1572868
  51.0 9.1 %copy-start.7 = (s32[1,32,32]{2,1,0:T(8,128)S(1)}, s32[1,32,32]{2,1,0:T(8,128)}, u32[]{:S(2)}) copy-start(s32[1,32,32]{2,1,0:T(8,128)} %param.19) | copy-start | bytes 12292
  51.0 9.1 %copy-start.12 = (f32[256]{0:T(256)S(1)}, f32[256]{0:T(256)}, u32[]{:S(2)}) copy-start(f32[256]{0:T(256)} %param.23) | copy-start | bytes 3076
  60.1 30.4 %copy-start.1 = (f32[8,128,8]{2,1,0:T(8,128)S(1)}, f32[8,128,8]{2,1,0:T(8,128)}, u32[]{:S(2)}) copy-start(f32[8,128,8]{2,1,0:T(8,128)} %get-tuple-element.22.degree_ref) | copy-start | bytes 98308
  60.1 30.4 %copy-start.27 = (f32[256]{0:T(256)S(1)}, f32[256]{0:T(256)}, u32[]{:S(2)}) copy-start(f32[256]{0:T(256)} %param.27) | copy-start | bytes 3076
  64.0 0.8 copy-start.13
  65.5 40.3 %all-to-all-start.1 = ((bf16[32,32,256]{2,1,0:T(8,128)(2,1)}), bf16[32,32,256]{2,1,0:T(8,128)(2,1)S(1)}, u32[]{:S(2)}, u32[]{:S(2)}) async-start(bf16[32,32,256]{2,1,0:T(8,128)(2,1)} %get-tuple-element.23), calls=%async_computation.1 | async-start | bytes 1048576 | tf_op jit(solution)/shard_map/all_to_all | solution.py:784
  71.7 9.7 %collective-permute-start.4 = (bf16[256,256]{1,0:T(8,128)(2,1)S(1)}, bf16[256,256]{1,0:T(8,128)(2,1)S(1)}, u32[]{:S(2)}, u32[]{:S(2)}) collective-permute-start(bf16[256,256]{1,0:T(8,128)(2,1)S(1)} %slice_bitcast_fusion.refs_0_), channel_id=1, source_target_pairs={{0,4},{1,5},{2,6},{3,7},{4,0},{5,1},{6,2},{7,3},{8,12},{9,13},{10,... | collective-permute-start | bytes 393224 | tf_op jit(solution)/shard_map/ppermute | solution.py:770
  73.5 10.0 %collective-permute-start.2 = (bf16[256,256]{1,0:T(8,128)(2,1)S(1)}, bf16[256,256]{1,0:T(8,128)(2,1)S(1)}, u32[]{:S(2)}, u32[]{:S(2)}) collective-permute-start(bf16[256,256]{1,0:T(8,128)(2,1)S(1)} %slice_bitcast_fusion.refs_0_), channel_id=1, source_target_pairs={{0,2},{1,3},{2,0},{3,1},{4,6},{5,7},{6,4},{7,5},{8,10},{9,11},{10,... | collective-permute-start | bytes 393224 | tf_op jit(solution)/shard_map/ppermute | solution.py:770
  81.4 5.9 %collective-permute-start.6 = (bf16[256,256]{1,0:T(8,128)(2,1)S(1)}, bf16[256,256]{1,0:T(8,128)(2,1)S(1)}, u32[]{:S(2)}, u32[]{:S(2)}) collective-permute-start(bf16[256,256]{1,0:T(8,128)(2,1)S(1)} %collective-permute-done.4.refs_4_), channel_id=1, source_target_pairs={{0,2},{1,3},{2,0},{3,1},{4,6},{5,7},{6,4},{7,5},{8,10},{9,11},{10,... | collective-permute-start | bytes 393224 | tf_op jit(solution)/shard_map/ppermute | solution.py:770
  83.0 4.9 %collective-permute-start.1 = (bf16[256,256]{1,0:T(8,128)(2,1)S(1)}, bf16[256,256]{1,0:T(8,128)(2,1)S(1)}, u32[]{:S(2)}, u32[]{:S(2)}) collective-permute-start(bf16[256,256]{1,0:T(8,128)(2,1)S(1)} %slice_bitcast_fusion.refs_0_), channel_id=1, source_target_pairs={{0,1},{1,0},{2,3},{3,2},{4,5},{5,4},{6,7},{7,6},{8,9},{9,8},{10,11... | collective-permute-start | bytes 393224 | tf_op jit(solution)/shard_map/ppermute | solution.py:770
  83.0 5.6 %collective-permute-start.5 = (bf16[256,256]{1,0:T(8,128)(2,1)S(1)}, bf16[256,256]{1,0:T(8,128)(2,1)S(1)}, u32[]{:S(2)}, u32[]{:S(2)}) collective-permute-start(bf16[256,256]{1,0:T(8,128)(2,1)S(1)} %collective-permute-done.4.refs_4_), channel_id=1, source_target_pairs={{0,1},{1,0},{2,3},{3,2},{4,5},{5,4},{6,7},{7,6},{8,9},{9,8},{10,11... | collective-permute-start | bytes 393224 | tf_op jit(solution)/shard_map/ppermute | solution.py:770
  83.5 5.7 %collective-permute-start.3 = (bf16[256,256]{1,0:T(8,128)(2,1)S(1)}, bf16[256,256]{1,0:T(8,128)(2,1)S(1)}, u32[]{:S(2)}, u32[]{:S(2)}) collective-permute-start(bf16[256,256]{1,0:T(8,128)(2,1)S(1)} %collective-permute-done.2.refs_2_), channel_id=1, source_target_pairs={{0,1},{1,0},{2,3},{3,2},{4,5},{5,4},{6,7},{7,6},{8,9},{9,8},{10,11... | collective-permute-start | bytes 393224 | tf_op jit(solution)/shard_map/ppermute | solution.py:770
  87.3 2.6 %collective-permute-start.7 = (bf16[256,256]{1,0:T(8,128)(2,1)S(1)}, bf16[256,256]{1,0:T(8,128)(2,1)S(1)}, u32[]{:S(2)}, u32[]{:S(2)}) collective-permute-start(bf16[256,256]{1,0:T(8,128)(2,1)S(1)} %collective-permute-done.6.refs_6_), channel_id=1, source_target_pairs={{0,1},{1,0},{2,3},{3,2},{4,5},{5,4},{6,7},{7,6},{8,9},{9,8},{10,11... | collective-permute-start | bytes 393224 | tf_op jit(solution)/shard_map/ppermute | solution.py:770
  90.6 1.0 copy-start.14
  91.6 0.9 copy-start.16
  92.5 0.9 copy-start.18
  93.4 0.9 copy-start.20
  94.3 0.9 copy-start.22
  95.2 0.9 copy-start.24
  96.1 0.9 copy-start.26
  (7 other events, 4.6 us)

commit v3 on v2

--- a/solution.py
+++ b/solution.py
@@ -208,14 +208,39 @@
     )(counts, table, pooled, degree)
 
 
+def in_hbm(*arrays):
+    return [pltpu.with_memory_space_constraint(array, pltpu.HBM) for array in arrays]
+
+
+def start_all(sems, *pairs):
+    copies = [pltpu.make_async_copy(a, b, sems.at[i]) for i, (a, b) in enumerate(pairs)]
+    for copy in copies:
+        copy.start()
+    return copies
+
+
+def wait_all(copies):
+    for copy in copies:
+        copy.wait()
+
+
 def build_body(
-    tile_ref, count_ref, source_ref, relation_ref, target_ref, own_ref,
-    local_ref, remote_ref, pooled_ref, degree_ref,
+    tile_ref, count_ref, source_hbm, relation_hbm, target_hbm, own_hbm,
+    local_ref, remote_ref, pooled_ref, degree_hbm,
+    source_ref, relation_ref, target_ref, own_ref, degree_ref,
     local_v, remote_v, pooled_v, head_ref, next_ref, list_ref, slot_ref, code_ref, low_ref, sum_ref,
-    sems, *, tiles, relations, locals_, pieces,
+    sems, in_sems, *, tiles, relations, locals_, pieces,
 ):
     slots = WIN * relations
     rows = pieces * slots
+    inputs = start_all(
+        in_sems,
+        (source_hbm, source_ref),
+        (relation_hbm, relation_ref),
+        (target_hbm, target_ref),
+        (own_hbm, own_ref),
+    )
+    wait_all(inputs)
     code_edges(source_ref, relation_ref, target_ref, slot_ref, code_ref, low_ref, relations)
     link_blocks(tile_ref, count_ref, head_ref, next_ref, tiles)
     head_ref[tiles] = -1
@@ -311,6 +336,7 @@
     pltpu.make_async_copy(local_v.at[every], local_ref, sems.at[0]).wait()
     pltpu.make_async_copy(remote_v.at[every], remote_ref, sems.at[1]).wait()
     pltpu.make_async_copy(pooled_v, pooled_ref, sems.at[2]).wait()
+    pltpu.sync_copy(degree_ref, degree_hbm)
 
 
 def build(tile_of, count, source, relation, target, own, *, relations, remote_rows):
@@ -328,14 +354,19 @@
             build_body, tiles=tiles, relations=relations, locals_=locals_, pieces=pieces
         ),
         out_shape=[
-            jax.ShapeDtypeStruct((rows, node_rows), jnp.bfloat16),
-            jax.ShapeDtypeStruct((rows, remote_rows), jnp.bfloat16),
-            jax.ShapeDtypeStruct((rows, width), jnp.float32),
-            jax.ShapeDtypeStruct((tiles // GROUP, slots, GROUP), jnp.float32),
-        ],
-        in_specs=[smem, smem, vmem, vmem, vmem, vmem],
-        out_specs=[hbm, hbm, hbm, vmem],
+            pltpu.HBM((rows, node_rows), jnp.bfloat16),
+            pltpu.HBM((rows, remote_rows), jnp.bfloat16),
+            pltpu.HBM((rows, width), jnp.float32),
+            pltpu.HBM((tiles // GROUP, slots, GROUP), jnp.float32),
+        ],
+        in_specs=[smem, smem] + [hbm] * 4,
+        out_specs=[hbm] * 4,
         scratch_shapes=[
+            pltpu.VMEM((blocks, block_width), jnp.int32),
+            pltpu.VMEM((blocks, block_width), jnp.int32),
+            pltpu.VMEM((blocks, block_width), jnp.int32),
+            pltpu.VMEM((node_rows, width), jnp.bfloat16),
+            pltpu.VMEM((tiles // GROUP, slots, GROUP), jnp.float32),
             pltpu.VMEM((rows + slots, node_rows), jnp.bfloat16),
             pltpu.VMEM((rows + slots, remote_rows), jnp.bfloat16),
             pltpu.VMEM((rows, width), jnp.float32),
@@ -347,6 +378,7 @@
             pltpu.VMEM((blocks, block_width), jnp.int32),
             pltpu.VMEM((pieces * slots, CHUNK), jnp.float32),
             pltpu.SemaphoreType.DMA((3,)),
+            pltpu.SemaphoreType.DMA((4,)),
         ],
         compiler_params=params(58),
         cost_estimate=estimate(
@@ -355,7 +387,7 @@
             2 * rows * pieces * CHUNK,
         ),
         name="build",
-    )(tile_of, count, source, relation, target, own)
+    )(tile_of, count, *in_hbm(source, relation, target, own))
 
 
 def pool_groups(
@@ -402,14 +434,17 @@
 
 
 def pool_body(
-    counts_ref, pooled_ref, incoming_ref, degree_ref, mean_ref,
-    counts_v, pooled_v, table_v, sems, *, relations, slot,
+    counts_ref, pooled_ref, incoming_ref, degree_hbm, mean_ref,
+    counts_v, pooled_v, table_v, degree_v, sems, in_sems, *, relations, slot,
 ):
+    inputs = start_all(in_sems, (degree_hbm, degree_v))
+
     def ready():
         copy_table(incoming_ref, table_v, slot)
+        wait_all(inputs)
 
     pool_groups(
-        counts_ref, counts_v, sems, table_v, degree_ref, mean_ref, relations, ready,
+        counts_ref, counts_v, sems, table_v, degree_v, mean_ref, relations, ready,
         extra=(pooled_ref, pooled_v),
     )
 
@@ -422,21 +457,23 @@
     return pl.pallas_call(
         functools.partial(pool_body, relations=relations, slot=slot),
         out_shape=jax.ShapeDtypeStruct((rows // relations, relations * width), jnp.bfloat16),
-        in_specs=[hbm, hbm, vmem, vmem],
+        in_specs=[hbm, hbm, vmem, hbm],
         out_specs=vmem,
         scratch_shapes=[
             pltpu.VMEM(counts.shape, counts.dtype),
             pltpu.VMEM(pooled.shape, pooled.dtype),
             pltpu.VMEM((depth, width), jnp.bfloat16),
+            pltpu.VMEM(degree.shape, degree.dtype),
             pltpu.SemaphoreType.DMA((2, degree.shape[0])),
+            pltpu.SemaphoreType.DMA((1,)),
         ],
         compiler_params=params(44),
         cost_estimate=estimate(2 * rows * depth * width, 2 * rows * depth),
         name="pool",
-    )(counts, pooled, incoming, degree)
-
-
-def pick_rows(send_ref, rows_ref, emit):
+    )(*in_hbm(counts, pooled), incoming, *in_hbm(degree))
+
+
+def pick_rows(send_ref, rows_ref, emit, done):
     devices, slot = send_ref.shape
     depth = rows_ref.shape[0]
     columns = send_ref[...].astype(jnp.float32).T.astype(jnp.int32)
@@ -453,13 +490,22 @@
         picked = jnp.dot(chosen, rows_ref[...], preferred_element_type=jnp.float32)
         for k in range(step):
             emit(start + k, picked[k * slot : (k + 1) * slot].astype(jnp.bfloat16))
+        done(start, step)
+
+
+def send_out(out_v, out_ref, sems, start, count):
+    some = pl.ds(start, count)
+    pltpu.make_async_copy(out_v.at[some], out_ref.at[some], sems.at[0]).start()
 
 
 def middle_body(
-    side_ref, mean_ref, own_ref, incoming_ref, swapped_ref, bias_ref, send_ref,
-    hidden_ref, out_ref, self_ref, weights_v, *, relations, slot,
+    mean_ref, own_hbm, incoming_ref, swapped_ref, bias_hbm, send_hbm,
+    hidden_hbm, out_ref, self_hbm,
+    own_v, bias_v, send_v, hidden_v, out_v, self_v, weights_v, sems, in_sems,
+    *, relations, slot,
 ):
-    width = own_ref.shape[1]
+    inputs = start_all(in_sems, (own_hbm, own_v), (bias_hbm, bias_v), (send_hbm, send_v))
+    width = own_v.shape[1]
     half = relations // 2
     devices = incoming_ref.shape[0]
     piece = width // devices
@@ -473,12 +519,12 @@
             weights_v[block + at : block + at + piece, :] = swapped_ref[
                 device, m * piece : (m + 1) * piece, :
             ]
-    side = side_ref[0]
+    side = lax.axis_index("dom") & 1
     mine_at = pl.multiple_of(side * (half * width), width)
     other_at = pl.multiple_of((1 - side) * (half * width), width)
     own_at = pl.multiple_of(half * width + side * block, width)
     next_at = pl.multiple_of(half * width + (1 - side) * block, width)
-    self_ref[...] = weights_v[pl.ds(next_at, width), :]
+    self_v[...] = weights_v[pl.ds(next_at, width), :]
     total = jnp.dot(
         mean_ref[:, pl.ds(mine_at, half * width)],
         weights_v[: half * width, :],
@@ -489,92 +535,134 @@
         weights_v[block : block + half * width, :],
         preferred_element_type=jnp.float32,
     )
+    wait_all(inputs)
     total += jnp.dot(
-        own_ref[...], weights_v[pl.ds(own_at, width), :], preferred_element_type=jnp.float32
-    )
-    hidden_ref[...] = jnp.maximum(total + bias_ref[...], 0.0).astype(jnp.bfloat16)
+        own_v[...], weights_v[pl.ds(own_at, width), :], preferred_element_type=jnp.float32
+    )
+    hidden_v[...] = jnp.maximum(total + bias_v[...], 0.0).astype(jnp.bfloat16)
+    outputs = [
+        pltpu.make_async_copy(hidden_v, hidden_hbm, sems.at[1]),
+        pltpu.make_async_copy(self_v, self_hbm, sems.at[2]),
+    ]
+    for copy in outputs:
+        copy.start()
 
     def emit(device, picked):
-        out_ref[device, :, :] = picked
-
-    pick_rows(send_ref, hidden_ref, emit)
-
-
-def middle(side, mean, own, incoming, swapped, bias, send, *, relations):
+        out_v[device, :, :] = picked
+
+    pick_rows(send_v, hidden_v, emit, functools.partial(send_out, out_v, out_ref, sems))
+    pltpu.make_async_copy(out_v, out_ref, sems.at[0]).wait()
+    wait_all(outputs)
+
+
+def middle(mean, own, incoming, swapped, bias, send, *, relations):
     nodes, width = own.shape
     devices, slot = send.shape
     vmem = pl.BlockSpec(memory_space=pltpu.VMEM)
-    smem = pl.BlockSpec(memory_space=pltpu.SMEM)
+    hbm = pl.BlockSpec(memory_space=pltpu.HBM)
     return pl.pallas_call(
         functools.partial(middle_body, relations=relations, slot=slot),
         out_shape=[
-            jax.ShapeDtypeStruct((nodes, width), jnp.bfloat16),
-            jax.ShapeDtypeStruct((devices, slot, width), jnp.bfloat16),
-            jax.ShapeDtypeStruct((width, width), jnp.bfloat16),
-        ],
-        in_specs=[smem] + [vmem] * 6,
-        out_specs=[vmem] * 3,
-        scratch_shapes=[pltpu.VMEM(((relations + 2) * width, width), jnp.bfloat16)],
-        compiler_params=params(20),
+            pltpu.HBM((nodes, width), jnp.bfloat16),
+            pltpu.HBM((devices, slot, width), jnp.bfloat16),
+            pltpu.HBM((width, width), jnp.bfloat16),
+        ],
+        in_specs=[vmem, hbm, vmem, vmem, hbm, hbm],
+        out_specs=[hbm] * 3,
+        scratch_shapes=[
+            pltpu.VMEM(own.shape, own.dtype),
+            pltpu.VMEM(bias.shape, bias.dtype),
+            pltpu.VMEM(send.shape, send.dtype),
+            pltpu.VMEM((nodes, width), jnp.bfloat16),
+            pltpu.VMEM((devices, slot, width), jnp.bfloat16),
+            pltpu.VMEM((width, width), jnp.bfloat16),
+            pltpu.VMEM(((relations + 2) * width, width), jnp.bfloat16),
+            pltpu.SemaphoreType.DMA((3,)),
+            pltpu.SemaphoreType.DMA((3,)),
+        ],
+        compiler_params=params(24),
         cost_estimate=estimate(2 * nodes * mean.shape[1] * width, 0),
         name="middle",
-    )(side, mean, own, incoming, swapped, bias, send)
+    )(mean, *in_hbm(own), incoming, swapped, *in_hbm(bias, send))
+
+
+def weight_copies(pieces, weights_v, relations):
+    width = weights_v.shape[1]
+    class_ = lax.axis_index("dom") & (relations - 1)
+    return [
+        (piece, weights_v.at[pl.ds(pl.multiple_of((class_ ^ k) * width, width), width)])
+        for k, piece in enumerate(pieces)
+    ]
 
 
 def first_body(
-    class_ref, counts_ref, own_ref, degree_ref, self_ref, bias_ref, *refs, relations
+    counts_ref, own_hbm, degree_hbm, self_hbm, bias_hbm, *refs, relations
 ):
-    pieces, (out_ref, weights_ref, counts_v, mean_v, sems) = refs[:relations], refs[relations:]
-    width = own_ref.shape[1]
-
-    def ready():
-        for k, piece in enumerate(pieces):
-            at = pl.multiple_of((class_ref[0] ^ k) * width, width)
-            weights_ref[pl.ds(at, width), :] = piece[...]
-
-    pool_groups(counts_ref, counts_v, sems, own_ref, degree_ref, mean_v, relations, ready)
-    total = jnp.dot(mean_v[...], weights_ref[...], preferred_element_type=jnp.float32)
-    total += jnp.dot(own_ref[...], self_ref[...], preferred_element_type=jnp.float32)
-    out_ref[...] = total + bias_ref[...]
-
-
-def first(class_, counts, own, degree, self_weight, bias, pieces, *, relations):
+    pieces, refs = refs[:relations], refs[relations:]
+    out_hbm, own_v, degree_v, self_v, bias_v, out_v, weights_v, counts_v, mean_v, sems, in_sems = refs
+    inputs = start_all(
+        in_sems,
+        (own_hbm, own_v),
+        (degree_hbm, degree_v),
+        (self_hbm, self_v),
+        (bias_hbm, bias_v),
+        *weight_copies(pieces, weights_v, relations),
+    )
+    pool_groups(
+        counts_ref, counts_v, sems, own_v, degree_v, mean_v, relations, lambda: wait_all(inputs)
+    )
+    total = jnp.dot(mean_v[...], weights_v[...], preferred_element_type=jnp.float32)
+    total += jnp.dot(own_v[...], self_v[...], preferred_element_type=jnp.float32)
+    out_v[...] = total + bias_v[...]
+    pltpu.sync_copy(out_v, out_hbm)
+
+
+def first(counts, own, degree, self_weight, bias, pieces, *, relations):
     rows, depth = counts.shape
     nodes, width = own.shape
-    vmem = pl.BlockSpec(memory_space=pltpu.VMEM)
-    smem = pl.BlockSpec(memory_space=pltpu.SMEM)
     hbm = pl.BlockSpec(memory_space=pltpu.HBM)
     return pl.pallas_call(
         functools.partial(first_body, relations=relations),
-        out_shape=[
-            jax.ShapeDtypeStruct((nodes, width), jnp.float32),
-            jax.ShapeDtypeStruct((relations * width, width), jnp.bfloat16),
-        ],
-        in_specs=[smem, hbm] + [vmem] * (4 + relations),
-        out_specs=[vmem, vmem],
+        out_shape=pltpu.HBM((nodes, width), jnp.float32),
+        in_specs=[hbm] * (5 + relations),
+        out_specs=hbm,
         scratch_shapes=[
+            pltpu.VMEM(own.shape, own.dtype),
+            pltpu.VMEM(degree.shape, degree.dtype),
+            pltpu.VMEM(self_weight.shape, self_weight.dtype),
+            pltpu.VMEM(bias.shape, bias.dtype),
+            pltpu.VMEM((nodes, width), jnp.float32),
+            pltpu.VMEM((relations * width, width), jnp.bfloat16),
             pltpu.VMEM(counts.shape, counts.dtype),
             pltpu.VMEM((nodes, relations * width), jnp.bfloat16),
             pltpu.SemaphoreType.DMA((1, degree.shape[0])),
+            pltpu.SemaphoreType.DMA((4 + relations,)),
         ],
         compiler_params=params(44),
         cost_estimate=estimate(
             2 * rows * depth * width + 2 * nodes * relations * width * width, 2 * rows * depth
         ),
         name="first",
-    )(class_, counts, own, degree, self_weight, bias, *pieces)
-
-
-def last_body(
-    counts_ref, table_ref, degree_ref, weights_ref, partial_ref, out_ref,
-    counts_v, mean_v, sems, *, relations,
-):
-    pool_groups(counts_ref, counts_v, sems, table_ref, degree_ref, mean_v, relations)
-    total = jnp.dot(mean_v[...], weights_ref[...], preferred_element_type=jnp.float32)
-    out_ref[...] = (total + partial_ref[...]).astype(out_ref.dtype)
-
-
-def last(counts, table, degree, weights, partial, *, relations):
+    )(*in_hbm(counts, own, degree, self_weight, bias, *pieces))
+
+
+def last_body(counts_ref, table_ref, degree_hbm, partial_hbm, *refs, relations):
+    pieces, refs = refs[:relations], refs[relations:]
+    out_ref, degree_v, partial_v, weights_v, counts_v, mean_v, sems, in_sems = refs
+    inputs = start_all(
+        in_sems,
+        (degree_hbm, degree_v),
+        (partial_hbm, partial_v),
+        *weight_copies(pieces, weights_v, relations),
+    )
+    pool_groups(
+        counts_ref, counts_v, sems, table_ref, degree_v, mean_v, relations, lambda: wait_all(inputs)
+    )
+    total = jnp.dot(mean_v[...], weights_v[...], preferred_element_type=jnp.float32)
+    out_ref[...] = (total + partial_v[...]).astype(out_ref.dtype)
+
+
+def last(counts, table, degree, partial, pieces, *, relations):
     rows, depth = counts.shape
     width = table.shape[1]
     nodes = rows // relations
@@ -583,29 +671,36 @@
     return pl.pallas_call(
         functools.partial(last_body, relations=relations),
         out_shape=jax.ShapeDtypeStruct((nodes, width), jnp.bfloat16),
-        in_specs=[hbm] + [vmem] * 4,
+        in_specs=[hbm, vmem] + [hbm] * (2 + relations),
         out_specs=vmem,
         scratch_shapes=[
+            pltpu.VMEM(degree.shape, degree.dtype),
+            pltpu.VMEM(partial.shape, partial.dtype),
+            pltpu.VMEM((relations * width, width), jnp.bfloat16),
             pltpu.VMEM(counts.shape, counts.dtype),
             pltpu.VMEM((nodes, relations * width), jnp.bfloat16),
             pltpu.SemaphoreType.DMA((1, degree.shape[0])),
+            pltpu.SemaphoreType.DMA((2 + relations,)),
         ],
         compiler_params=params(44),
         cost_estimate=estimate(
             2 * rows * depth * width + 2 * nodes * relations * width * width, 2 * rows * depth
         ),
         name="last",
-    )(counts, table, degree, weights, partial)
-
-
-def pack_body(
-    coef_first_ref, coef_second_ref, features_ref, send_ref, bases_first_ref, self_first_ref,
-    bases_second_ref, self_second_ref, out_ref,
-):
-    relations, bases = coef_first_ref.shape
-    devices, slot = send_ref.shape
-    piece = self_first_ref.shape[0]
+    )(*in_hbm(counts), table, *in_hbm(degree, partial, *pieces))
+
+
+def pack_body(*refs):
+    inputs_hbm, out_ref, inputs_v, (out_v, sems, in_sems) = refs[:8], refs[8], refs[9:17], refs[17:]
+    inputs = start_all(in_sems, *zip(inputs_hbm, inputs_v))
+    coef_first, coef_second, bases_first, bases_second, self_first, self_second, features, send = (
+        inputs_v
+    )
+    relations, bases = coef_first.shape
+    devices, slot = send.shape
+    piece = self_first.shape[0]
     half = relations // 2
+    wait_all(inputs)
 
     def mix(coef_ref, bases_ref):
         mixed = []
@@ -616,39 +711,48 @@
             mixed.append(total.astype(jnp.bfloat16))
         return mixed
 
-    first = mix(coef_first_ref, bases_first_ref)
-    second = mix(coef_second_ref, bases_second_ref)
-    own = [self_first_ref[...], self_second_ref[...]]
+    first = mix(coef_first, bases_first)
+    second = mix(coef_second, bases_second)
+    own = [self_first[...], self_second[...]]
     for device in range(devices):
         side = device % 2
         rows = first[side * half : (side + 1) * half] + [own[side], second[device % relations]]
         for k, value in enumerate(rows):
             at = slot + k * piece
-            out_ref[device, at : at + piece, :] = value
+            out_v[device, at : at + piece, :] = value
 
     def emit(device, picked):
-        out_ref[device, :slot, :] = picked
-
-    pick_rows(send_ref, features_ref, emit)
+        out_v[device, :slot, :] = picked
+
+    pick_rows(send, features, emit, functools.partial(send_out, out_v, out_ref, sems))
+    pltpu.make_async_copy(out_v, out_ref, sems.at[0]).wait()
 
 
 def pack(features, send, bases_first, self_first, coef_first, bases_second, self_second, coef_second):
     devices, slot = send.shape
     relations = coef_first.shape[0]
     piece, width = self_first.shape
-    vmem = pl.BlockSpec(memory_space=pltpu.VMEM)
-    smem = pl.BlockSpec(memory_space=pltpu.SMEM)
+    hbm = pl.BlockSpec(memory_space=pltpu.HBM)
+    shape = (devices, slot + (relations // 2 + 2) * piece, width)
+    args = (
+        coef_first, coef_second, bases_first, bases_second, self_first, self_second, features, send,
+    )
     return pl.pallas_call(
         pack_body,
-        out_shape=jax.ShapeDtypeStruct(
-            (devices, slot + (relations // 2 + 2) * piece, width), jnp.bfloat16
-        ),
-        in_specs=[smem, smem] + [vmem] * 6,
-        out_specs=vmem,
+        out_shape=pltpu.HBM(shape, jnp.bfloat16),
+        in_specs=[hbm] * 8,
+        out_specs=hbm,
+        scratch_shapes=[
+            *[pltpu.SMEM(a.shape, a.dtype) for a in args[:2]],
+            *[pltpu.VMEM(a.shape, a.dtype) for a in args[2:]],
+            pltpu.VMEM(shape, jnp.bfloat16),
+            pltpu.SemaphoreType.DMA((1,)),
+            pltpu.SemaphoreType.DMA((8,)),
+        ],
         compiler_params=params(24),
         cost_estimate=estimate(2 * devices * slot * features.size, 0),
         name="pack",
-    )(coef_first, coef_second, features, send, bases_first, self_first, bases_second, self_second)
+    )(*in_hbm(*args))
 
 
 def dense_body(mean_ref, own_ref, weights_ref, bias_ref, out_ref, *, last):
@@ -755,8 +859,6 @@
             bias_second,
             relations,
         )
-    here = lax.axis_index("dom").astype(jnp.int32).reshape(1)
-    side, class_ = here & 1, here & (relations - 1)
     outgoing = pack(
         features, send, bases_first, self_first, coef_first, bases_second, self_second, coef_second
     )
@@ -772,23 +874,31 @@
     next_at = slot + (relations // 2 + 1) * self_first.shape[0]
     swapped = from_peer(incoming[:, slot:next_at], 1)
     pieces = {0: incoming[:, next_at:].reshape(width, width)}
+
+    def widen(mask):
+        pieces.update({k | mask: from_peer(piece, mask) for k, piece in sorted(pieces.items())})
+
     mask = relations // 2
-    while mask:
-        pieces.update({k | mask: from_peer(piece, mask) for k, piece in sorted(pieces.items())})
+    widen(mask)
+    mean = pool(remote, pooled, incoming, degree, relations=relations, slot=slot)
+    pieces, mean = lax.optimization_barrier((pieces, mean))
+    while mask > 2:
         mask //= 2
+        widen(mask)
+    hidden, picked, self_next = middle(
+        mean, features, incoming, swapped, bias_first[None], send, relations=relations
+    )
+    pieces, picked = lax.optimization_barrier((pieces, picked))
+    while mask > 1:
+        mask //= 2
+        widen(mask)
     pieces = [pieces[k] for k in range(relations)]
-    mean = pool(remote, pooled, incoming, degree, relations=relations, slot=slot)
-    hidden, picked, self_next = middle(
-        side, mean, features, incoming, swapped, bias_first[None], send, relations=relations
-    )
     table = lax.all_to_all(picked, "dom", split_axis=0, concat_axis=0, tiled=True)
-    partial, weights = first(
-        class_, local, hidden, degree, self_next, bias_second[None], pieces, relations=relations
+    partial = first(
+        local, hidden, degree, self_next, bias_second[None], pieces, relations=relations
     )
     table, partial = lax.optimization_barrier((table, partial))
-    return last(
-        remote, table.reshape(-1, width), degree, weights, partial, relations=relations
-    )
+    return last(remote, table.reshape(-1, width), degree, partial, pieces, relations=relations)
 
 
 def solution(mesh):

time: 116 us -> 94.4 us (0.81)
  local copies, waits for them, and re-layouts: 19.2 us -> 1.34 us
  waiting for transfers between devices: 11.5 us -> 5.37 us
  Pallas kernels: 63.2 us -> 68.5 us
  starting transfers between devices: 20.4 us -> 18.5 us
    unnamed x58 -> x18, local copies, waits for them, and re-layouts: 18.5 us -> 0.66 us
    ppermute x8, waiting for transfers between devices: 10.2 us -> 3.15 us  [from_peer(): return lax.ppermute(array, 'dom', [(i, i ^ mask) for i in range(devices)])]
    all_to_all x1, waiting for transfers between devices: 0.01 us -> 2.22 us  [shards(): lax.all_to_all(picked, 'dom', split_axis=0, concat_axis=0, tiled=True)]
    pallas_call x1, Pallas kernels: 8.73 us -> 10.5 us  [first(): pl.pallas_call(functools.partial(first_body, relations=relations), out_sh...]
    ppermute x8, starting transfers between devices: 6.86 us -> 5.15 us  [from_peer(): return lax.ppermute(array, 'dom', [(i, i ^ mask) for i in range(devices)])]
    pallas_call x1, Pallas kernels: 29.3 us -> 30.7 us  [build(): pl.pallas_call(functools.partial(build_body, tiles=tiles, relations=relat...]
    all_to_all x1, waiting for transfers between devices: 1.37 us -> 0.01 us  [shards(): lax.all_to_all(outgoing, 'dom', split_axis=0, concat_axis=0, tiled=True)]
  transfers between devices with their start and end apart: 10 -> 10, of which waited for: 3 -> 6; matrix products, arithmetic and copies ran while one was open for 1% -> 1% of each run, Pallas kernels for 41% -> 58%
where the time goes in v3:
time: 94.4 us; the launch traced here: 94.5 us
  Pallas kernels  68.5 us (73%)
  starting transfers between devices  18.5 us (20%)
  waiting for transfers between devices  5.37 us (6%)
  local copies, waits for them, and re-layouts  1.34 us (1%)
    pallas_call x1, Pallas kernels, build(): pl.pallas_call(functools.partial(build_body, tiles=tiles, relations=relat...  30.7 us
    pallas_call x1, Pallas kernels, first(): pl.pallas_call(functools.partial(first_body, relations=relations), out_sh...  10.5 us
    pallas_call x1, Pallas kernels, last(): pl.pallas_call(functools.partial(last_body, relations=relations), out_sha...  10.3 us
    pallas_call x1, Pallas kernels, pool(): pl.pallas_call(functools.partial(pool_body, relations=relations, slot=slo...  9.18 us
    all_to_all x1, starting transfers between devices, shards(): lax.all_to_all(outgoing, 'dom', split_axis=0, concat_axis=0, tiled=True)  7.34 us
    all_to_all x1, starting transfers between devices, shards(): lax.all_to_all(picked, 'dom', split_axis=0, concat_axis=0, tiled=True)  6 us
    ppermute x8, starting transfers between devices, from_peer(): return lax.ppermute(array, 'dom', [(i, i ^ mask) for i in range(devices)])  5.15 us
    pallas_call x1, Pallas kernels, middle(): pl.pallas_call(functools.partial(middle_body, relations=relations, slot=s...  4.32 us
  transfers between devices with their start and end apart: 10, of which 6 were waited for; matrix products, arithmetic and copies ran while one was open for 1% of the time, Pallas kernels for 58%

profile of v3, /device:TPU:0, one launch (start us, length us, event | category | flops | bytes accessed | tf_op | source)
XLA Modules:
  0.0 94.5 jit_solution(5485251926514799607)
XLA Ops:
  0.0 3.4 %pack.1 = bf16[32,80,256]{2,1,0:T(8,128)(2,1)} custom-call(f32[8,30]{1,0:T(8,128)} %refs_0_.1, f32[8,30]{1,0:T(8,128)} %refs_1_.1, bf16[30,8,256]{2,1,0:T(8,128)(2,1)} %refs_2_.1, bf16[30,8,256]{2,1,0:T(8,128)(2,1)} %refs_3_.1, bf16[8,256]{1,0:T(8,128)(2,1)} %refs_4_.1, bf16[8,256]{1,0:T(8,128)(2,1)} %refs_5_.1, bf16[1024,256]{1,0:T(8,128)(2,1)} %own_hbm.3, ...), custom_call_target="tpu_custom_call" | custom-call | flops 536870912 | tf_op jit(solution)/shard_map/pack/pallas_call | solution.py:740
  3.4 7.3 %all-to-all-start = ((bf16[32,80,256]{2,1,0:T(8,128)(2,1)}), bf16[32,80,256]{2,1,0:T(8,128)(2,1)S(1)}, u32[]{:S(2)}, u32[]{:S(2)}) async-start(bf16[32,80,256]{2,1,0:T(8,128)(2,1)} %pack.1), calls=%async_computation | async-start | bytes 2621440 | tf_op jit(solution)/shard_map/all_to_all | solution.py:865
  11.4 0.6 slice_reduce_fusion.tile_ref
  12.0 30.7 %build.1 = (bf16[8192,1024]{1,0:T(8,128)(2,1)}, bf16[8192,1024]{1,0:T(8,128)(2,1)}, f32[8192,256]{1,0:T(8,128)}, f32[8,128,8]{2,1,0:T(8,128)}) custom-call(s32[128]{0:T(128)} %slice_reduce_fusion.tile_ref, s32[1]{0:T(128)S(6)} %copy.15.count_ref, s32[128,128]{1,0:T(8,128)} %bitcast.15, s32[128,128]{1,0:T(8,128)} %bitcast.16, s32[128,128]{1,0:T(8,128)} %bitcast.12, ...), custom_call_target="tpu_custom_call" | custom-call | flops 17179869184 | bytes 33554432 | tf_op jit(solution)/shard_map/build/pallas_call | solution.py:352
  42.8 0.0 all-to-all-done.incoming_ref
  42.9 0.1 collective-permute-start.3
  43.0 0.0 copy-start
  43.0 1.3 %collective-permute-start = (bf16[256,256]{1,0:T(8,128)(2,1)S(1)}, bf16[256,256]{1,0:T(8,128)(2,1)S(1)}, u32[]{:S(2)}, u32[]{:S(2)}) collective-permute-start(bf16[256,256]{1,0:T(8,128)(2,1)S(1)} %slice_bitcast_fusion.refs_0_), channel_id=1, source_target_pairs={{0,4},{1,5},{2,6},{3,7},{4,0},{5,1},{6,2},{7,3},{8,12},{9,13},{10,... | collective-permute-start | bytes 393224 | tf_op jit(solution)/shard_map/ppermute | solution.py:872
  44.3 9.2 %pool.1.mean_ref = bf16[1024,2048]{1,0:T(8,128)(2,1)S(1)} custom-call(bf16[8192,1024]{1,0:T(8,128)(2,1)} %get-tuple-element.24.counts_ref, f32[8192,256]{1,0:T(8,128)} %get-tuple-element.27.pooled_ref, bf16[32,80,256]{2,1,0:T(8,128)(2,1)S(1)} %all-to-all-done.incoming_ref, f32[8,128,8]{2,1,0:T(8,128)} %get-tuple-element.28.degree_hbm), custom_call_target="tpu_custom_call" | custom-call | flops 4294967296 | bytes 16777216 | tf_op jit(solution)/shard_map/pool/pallas_call | solution.py:457
  53.5 0.0 collective-permute-done.refs_4_
  53.5 2.6 %collective-permute-start.1 = (bf16[256,256]{1,0:T(8,128)(2,1)S(1)}, bf16[256,256]{1,0:T(8,128)(2,1)S(1)}, u32[]{:S(2)}, u32[]{:S(2)}) collective-permute-start(bf16[256,256]{1,0:T(8,128)(2,1)S(1)} %slice_bitcast_fusion.refs_0_), channel_id=1, source_target_pairs={{0,2},{1,3},{2,0},{3,1},{4,6},{5,7},{6,4},{7,5},{8,10},{9,11},{10,... | collective-permute-start | bytes 393224 | tf_op jit(solution)/shard_map/ppermute | solution.py:872
  56.1 0.1 collective-permute-start.2
  56.2 0.0 collective-permute-done.3.swapped_ref
  56.2 4.3 %middle.1 = (bf16[1024,256]{1,0:T(8,128)(2,1)}, bf16[32,32,256]{2,1,0:T(8,128)(2,1)}, bf16[256,256]{1,0:T(8,128)(2,1)}) custom-call(bf16[1024,2048]{1,0:T(8,128)(2,1)S(1)} %pool.1.mean_ref, bf16[1024,256]{1,0:T(8,128)(2,1)} %own_hbm.3, bf16[32,80,256]{2,1,0:T(8,128)(2,1)S(1)} %all-to-all-done.incoming_ref, ...), custom_call_target="tpu_custom_call" | custom-call | flops 1073741824 | tf_op jit(solution)/shard_map/middle/pallas_call | solution.py:563
  60.5 0.0 collective-permute-done.1.refs_2_
  60.5 2.1 %collective-permute-done.2.refs_6_ = bf16[256,256]{1,0:T(8,128)(2,1)S(1)} collective-permute-done((bf16[256,256]{1,0:T(8,128)(2,1)S(1)}, bf16[256,256]{1,0:T(8,128)(2,1)S(1)}, u32[]{:S(2)}, u32[]{:S(2)}) %collective-permute-start.2) | collective-permute-done | bytes 131104 | tf_op jit(solution)/shard_map/ppermute | solution.py:872
  62.6 6.0 %all-to-all-start.1 = ((bf16[32,32,256]{2,1,0:T(8,128)(2,1)}), bf16[32,32,256]{2,1,0:T(8,128)(2,1)S(1)}, u32[]{:S(2)}, u32[]{:S(2)}) async-start(bf16[32,32,256]{2,1,0:T(8,128)(2,1)} %get-tuple-element.33), calls=%async_computation.1 | async-start | bytes 1048576 | tf_op jit(solution)/shard_map/all_to_all | solution.py:896
  68.6 0.0 copy-done
  68.6 0.3 collective-permute-start.4
  68.9 0.3 collective-permute-start.5
  69.2 0.3 collective-permute-start.6
  69.4 0.3 collective-permute-start.7
  69.7 0.3 collective-permute-done.4.refs_1_
  70.0 0.2 collective-permute-done.5.refs_3_
  70.3 0.3 collective-permute-done.6.refs_5_
  70.5 0.2 collective-permute-done.7.refs_7_
  70.8 0.1 copy-done.5
  70.9 0.3 copy-done.6
  71.2 0.2 copy-done.7
  71.4 10.5 %first.1.partial_hbm = f32[1024,256]{1,0:T(8,128)} custom-call(bf16[8192,1024]{1,0:T(8,128)(2,1)} %get-tuple-element.34.counts_ref, bf16[1024,256]{1,0:T(8,128)(2,1)} %get-tuple-element.35.own_hbm, f32[8,128,8]{2,1,0:T(8,128)} %get-tuple-element.28.degree_hbm, bf16[256,256]{1,0:T(8,128)(2,1)} %get-tuple-element.36.self_hbm, f32[1,256]{1,0:T(1,128)} %bitcast.13, ...), custom_call_target="tpu_custom_call" | custom-call | flops 5368709120 | bytes 16777216 | tf_op jit(solution)/shard_map/first/pallas_call | solution.py:624
  82.0 2.2 %all-to-all-done.1 = bf16[32,32,256]{2,1,0:T(8,128)(2,1)S(1)} async-done(((bf16[32,32,256]{2,1,0:T(8,128)(2,1)}), bf16[32,32,256]{2,1,0:T(8,128)(2,1)S(1)}, u32[]{:S(2)}, u32[]{:S(2)}) %all-to-all-start.1) | async-done | bytes 524320 | tf_op jit(solution)/shard_map/all_to_all | solution.py:896
  84.2 10.3 %last.1 = bf16[1024,256]{1,0:T(8,128)(2,1)} custom-call(bf16[8192,1024]{1,0:T(8,128)(2,1)} %get-tuple-element.24.counts_ref, bf16[1024,256]{1,0:T(8,128)(2,1)S(1)} %bitcast.9, f32[8,128,8]{2,1,0:T(8,128)} %get-tuple-element.28.degree_hbm, f32[1024,256]{1,0:T(8,128)} %first.1.partial_hbm, bf16[256,256]{1,0:T(8,128)(2,1)} %copy-done, ...), custom_call_target="tpu_custom_call" | custom-call | flops 5368709120 | bytes 16777216 | tf_op jit(solution)/shard_map/last/pallas_call | solution.py:671
  (15 shorter events, 0.1 us)
Async XLA Ops:
  0.0 11.4 %copy-start.8 = (s32[1,128,128]{2,1,0:T(8,128)S(1)}, s32[1,128,128]{2,1,0:T(8,128)}, u32[]{:S(2)}) copy-start(s32[1,128,128]{2,1,0:T(8,128)} %param.17) | copy-start | bytes 196612
  3.4 39.4 %all-to-all-start = ((bf16[32,80,256]{2,1,0:T(8,128)(2,1)}), bf16[32,80,256]{2,1,0:T(8,128)(2,1)S(1)}, u32[]{:S(2)}, u32[]{:S(2)}) async-start(bf16[32,80,256]{2,1,0:T(8,128)(2,1)} %pack.1), calls=%async_computation | async-start | bytes 2621440 | tf_op jit(solution)/shard_map/all_to_all | solution.py:865
  42.9 13.3 %collective-permute-start.3 = (bf16[32,40,256]{2,1,0:T(8,128)(2,1)S(1)}, bf16[32,40,256]{2,1,0:T(8,128)(2,1)S(1)}, u32[]{:S(2)}, u32[]{:S(2)}) collective-permute-start(bf16[32,40,256]{2,1,0:T(8,128)(2,1)S(1)} %slice.11), channel_id=1, source_target_pairs={{0,1},{1,0},{2,3},{3,2},{4,5},{5,4},{6,7},{7,6},{8,9},{9,8},{10,11... | collective-permute-start | bytes 1966088 | tf_op jit(solution)/shard_map/ppermute | solution.py:872
  43.0 25.6 %copy-start = (bf16[256,256]{1,0:T(8,128)(2,1)}, bf16[256,256]{1,0:T(8,128)(2,1)S(1)}, u32[]{:S(2)}) copy-start(bf16[256,256]{1,0:T(8,128)(2,1)S(1)} %slice_bitcast_fusion.refs_0_) | copy-start | bytes 393220
  43.0 10.5 %collective-permute-start = (bf16[256,256]{1,0:T(8,128)(2,1)S(1)}, bf16[256,256]{1,0:T(8,128)(2,1)S(1)}, u32[]{:S(2)}, u32[]{:S(2)}) collective-permute-start(bf16[256,256]{1,0:T(8,128)(2,1)S(1)} %slice_bitcast_fusion.refs_0_), channel_id=1, source_target_pairs={{0,4},{1,5},{2,6},{3,7},{4,0},{5,1},{6,2},{7,3},{8,12},{9,13},{10,... | collective-permute-start | bytes 393224 | tf_op jit(solution)/shard_map/ppermute | solution.py:872
  53.5 17.3 %copy-start.1 = (bf16[256,256]{1,0:T(8,128)(2,1)}, bf16[256,256]{1,0:T(8,128)(2,1)S(1)}, u32[]{:S(2)}) copy-start(bf16[256,256]{1,0:T(8,128)(2,1)S(1)} %collective-permute-done.refs_4_) | copy-start | bytes 393220
  53.5 7.0 %collective-permute-start.1 = (bf16[256,256]{1,0:T(8,128)(2,1)S(1)}, bf16[256,256]{1,0:T(8,128)(2,1)S(1)}, u32[]{:S(2)}, u32[]{:S(2)}) collective-permute-start(bf16[256,256]{1,0:T(8,128)(2,1)S(1)} %slice_bitcast_fusion.refs_0_), channel_id=1, source_target_pairs={{0,2},{1,3},{2,0},{3,1},{4,6},{5,7},{6,4},{7,5},{8,10},{9,11},{10,... | collective-permute-start | bytes 393224 | tf_op jit(solution)/shard_map/ppermute | solution.py:872
  56.1 6.5 %collective-permute-start.2 = (bf16[256,256]{1,0:T(8,128)(2,1)S(1)}, bf16[256,256]{1,0:T(8,128)(2,1)S(1)}, u32[]{:S(2)}, u32[]{:S(2)}) collective-permute-start(bf16[256,256]{1,0:T(8,128)(2,1)S(1)} %collective-permute-done.refs_4_), channel_id=1, source_target_pairs={{0,2},{1,3},{2,0},{3,1},{4,6},{5,7},{6,4},{7,5},{8,10},{9,11},{10,... | collective-permute-start | bytes 393224 | tf_op jit(solution)/shard_map/ppermute | solution.py:872
  60.5 10.3 %copy-start.2 = (bf16[256,256]{1,0:T(8,128)(2,1)}, bf16[256,256]{1,0:T(8,128)(2,1)S(1)}, u32[]{:S(2)}) copy-start(bf16[256,256]{1,0:T(8,128)(2,1)S(1)} %collective-permute-done.1.refs_2_) | copy-start | bytes 393220
  62.6 8.2 %copy-start.3 = (bf16[256,256]{1,0:T(8,128)(2,1)}, bf16[256,256]{1,0:T(8,128)(2,1)S(1)}, u32[]{:S(2)}) copy-start(bf16[256,256]{1,0:T(8,128)(2,1)S(1)} %collective-permute-done.2.refs_6_) | copy-start | bytes 393220
  62.6 21.6 %all-to-all-start.1 = ((bf16[32,32,256]{2,1,0:T(8,128)(2,1)}), bf16[32,32,256]{2,1,0:T(8,128)(2,1)S(1)}, u32[]{:S(2)}, u32[]{:S(2)}) async-start(bf16[32,32,256]{2,1,0:T(8,128)(2,1)} %get-tuple-element.33), calls=%async_computation.1 | async-start | bytes 1048576 | tf_op jit(solution)/shard_map/all_to_all | solution.py:896
  68.6 1.4 %collective-permute-start.4 = (bf16[256,256]{1,0:T(8,128)(2,1)S(1)}, bf16[256,256]{1,0:T(8,128)(2,1)S(1)}, u32[]{:S(2)}, u32[]{:S(2)}) collective-permute-start(bf16[256,256]{1,0:T(8,128)(2,1)S(1)} %slice_bitcast_fusion.refs_0_), channel_id=1, source_target_pairs={{0,1},{1,0},{2,3},{3,2},{4,5},{5,4},{6,7},{7,6},{8,9},{9,8},{10,11... | collective-permute-start | bytes 393224 | tf_op jit(solution)/shard_map/ppermute | solution.py:872
  68.9 1.3 %collective-permute-start.5 = (bf16[256,256]{1,0:T(8,128)(2,1)S(1)}, bf16[256,256]{1,0:T(8,128)(2,1)S(1)}, u32[]{:S(2)}, u32[]{:S(2)}) collective-permute-start(bf16[256,256]{1,0:T(8,128)(2,1)S(1)} %collective-permute-done.1.refs_2_), channel_id=1, source_target_pairs={{0,1},{1,0},{2,3},{3,2},{4,5},{5,4},{6,7},{7,6},{8,9},{9,8},{10,11... | collective-permute-start | bytes 393224 | tf_op jit(solution)/shard_map/ppermute | solution.py:872
  69.2 1.3 %collective-permute-start.6 = (bf16[256,256]{1,0:T(8,128)(2,1)S(1)}, bf16[256,256]{1,0:T(8,128)(2,1)S(1)}, u32[]{:S(2)}, u32[]{:S(2)}) collective-permute-start(bf16[256,256]{1,0:T(8,128)(2,1)S(1)} %collective-permute-done.refs_4_), channel_id=1, source_target_pairs={{0,1},{1,0},{2,3},{3,2},{4,5},{5,4},{6,7},{7,6},{8,9},{9,8},{10,11... | collective-permute-start | bytes 393224 | tf_op jit(solution)/shard_map/ppermute | solution.py:872
  69.4 1.3 %collective-permute-start.7 = (bf16[256,256]{1,0:T(8,128)(2,1)S(1)}, bf16[256,256]{1,0:T(8,128)(2,1)S(1)}, u32[]{:S(2)}, u32[]{:S(2)}) collective-permute-start(bf16[256,256]{1,0:T(8,128)(2,1)S(1)} %collective-permute-done.2.refs_6_), channel_id=1, source_target_pairs={{0,1},{1,0},{2,3},{3,2},{4,5},{5,4},{6,7},{7,6},{8,9},{9,8},{10,11... | collective-permute-start | bytes 393224 | tf_op jit(solution)/shard_map/ppermute | solution.py:872
  70.0 0.8 copy-start.4
  70.3 0.7 copy-start.5
  70.5 0.7 copy-start.6
  70.8 0.7 copy-start.7

commit v4 on v3

--- a/solution.py
+++ b/solution.py
@@ -10,6 +10,7 @@
 WIN = 16
 CHUNK = 512
 GROUP = 8
+EACH = 2
 MIB = 1 << 20
 WHOLE_MAX = 36 * MIB
 CONTRACT_LANES = (((1,), (1,)), ((), ()))
@@ -57,17 +58,17 @@
     return second, after
 
 
-def pair_rows(ref, first, second):
-    one = jnp.where(first >= 0, ref[pl.ds(jnp.maximum(first, 0), 1), :], -1)
-    two = jnp.where(second >= 0, ref[pl.ds(jnp.maximum(second, 0), 1), :], -1)
-    return jnp.concatenate([one, two], axis=1)
-
-
-def pair_counts(first, second, slot_ref, code_ref, low_ref, rows, slots):
-    left = hot(rows, pair_rows(code_ref, first, second)).astype(jnp.bfloat16)
-    right = hot(CHUNK, pair_rows(low_ref, first, second)).astype(jnp.bfloat16)
+def some_rows(ref, blocks):
+    return jnp.concatenate(
+        [jnp.where(b >= 0, ref[pl.ds(jnp.maximum(b, 0), 1), :], -1) for b in blocks], axis=1
+    )
+
+
+def count_blocks(blocks, slot_ref, code_ref, low_ref, rows, slots):
+    left = hot(rows, some_rows(code_ref, blocks)).astype(jnp.bfloat16)
+    right = hot(CHUNK, some_rows(low_ref, blocks)).astype(jnp.bfloat16)
     counts = lax.dot_general(left, right, CONTRACT_LANES, preferred_element_type=jnp.float32)
-    degree = jnp.sum(hot(slots, pair_rows(slot_ref, first, second)), axis=1, keepdims=True)
+    degree = jnp.sum(hot(slots, some_rows(slot_ref, blocks)), axis=1, keepdims=True)
     return counts, degree
 
 
@@ -100,7 +101,7 @@
 
     def step(first):
         second, after = pair_of(first, next_ref)
-        counts, degree = pair_counts(first, second, slot_ref, code_ref, low_ref, rows, slots)
+        counts, degree = count_blocks([first, second], slot_ref, code_ref, low_ref, rows, slots)
         sum_ref[...] += counts
         degree_ref[...] += degree
         return after
@@ -244,8 +245,9 @@
     code_edges(source_ref, relation_ref, target_ref, slot_ref, code_ref, low_ref, relations)
     link_blocks(tile_ref, count_ref, head_ref, next_ref, tiles)
     head_ref[tiles] = -1
+    degree_ref[tiles // GROUP] = jnp.zeros((slots, GROUP), jnp.float32)
     counted = functools.partial(
-        pair_counts, slot_ref=slot_ref, code_ref=code_ref, low_ref=low_ref, rows=rows, slots=slots
+        count_blocks, slot_ref=slot_ref, code_ref=code_ref, low_ref=low_ref, rows=rows, slots=slots
     )
 
     def place(t, piece):
@@ -256,87 +258,136 @@
     def part(counts, piece):
         return counts[piece * slots : (piece + 1) * slots]
 
-    def add_degree(i, u, degree):
+    def add(t, blocks):
+        counts, degree = counted(blocks)
+        for piece in range(pieces):
+            ref, where = place(t, piece)
+            total = ref[where].astype(jnp.float32) + part(counts, piece)
+            ref[where] = total.astype(jnp.bfloat16)
+        add_degree(t, degree)
+
+    def add_degree(t, degree):
         lanes = lax.broadcasted_iota(jnp.int32, (slots, GROUP), 1)
-        degree_ref[i] += jnp.where(lanes == u, degree, 0.0)
-
-    def group(i, carry):
+        degree_ref[t // GROUP] += jnp.where(lanes == t % GROUP, degree, 0.0)
+
+    def copy_tile(t):
+        some = pl.ds(pl.multiple_of(t * slots, slots), slots)
+        pltpu.make_async_copy(local_v.at[some], local_ref.at[some], sems.at[0]).start()
+        pltpu.make_async_copy(remote_v.at[some], remote_ref.at[some], sems.at[1]).start()
+
+    def base(i, carry):
+        afters = []
         for u in range(GROUP):
             t = i * GROUP + u
             first = head_ref[t]
             second, after = pair_of(first, next_ref)
-            counts, degree = counted(first, second)
+            counts, degree = counted([first, second])
             for piece in range(pieces):
                 ref, where = place(t, piece)
                 ref[where] = part(counts, piece).astype(jnp.bfloat16)
             degree_ref[i, :, pl.ds(u, 1)] = degree
             head_ref[t] = after
-
-        short = jnp.int32(0)
-        for u in range(GROUP):
-            t = i * GROUP + u
+            afters.append(after)
+        for u, after in enumerate(afters):
+
+            @pl.when(after < 0)
+            def _():
+                copy_tile(i * GROUP + u)
+
+        return carry
+
+    lax.fori_loop(0, tiles // GROUP, base, 0)
+
+    def sort_tile(t, sizes):
+        short, mid, long = sizes
+        first = head_ref[t]
+        _, third = pair_of(first, next_ref)
+        _, fifth = pair_of(third, next_ref)
+        list_ref[0, short] = t
+        list_ref[1, mid] = t
+        list_ref[2, long] = t
+        more = first >= 0
+        return (
+            short + jnp.where(more & (third < 0), 1, 0),
+            mid + jnp.where(more & (third >= 0) & (fifth < 0), 1, 0),
+            long + jnp.where(more & (fifth >= 0), 1, 0),
+        )
+
+    zero = jnp.int32(0)
+    short, mid, long = lax.fori_loop(0, tiles, sort_tile, (zero, zero, zero))
+    for k in range(4):
+        list_ref[0, short + k] = tiles
+        list_ref[1, mid + k] = tiles
+
+    def add_short(j, carry):
+        for k in range(4):
+            t = list_ref[0, 4 * j + k]
             first = head_ref[t]
-            _, after = pair_of(first, next_ref)
-            list_ref[short] = t
-            short += jnp.where((first >= 0) & (after < 0), 1, 0)
-        list_ref[short] = tiles
-
-        def add_two(j, carry):
-            for k in range(2):
-                t = list_ref[2 * j + k]
-                first = head_ref[t]
-                second, _ = pair_of(first, next_ref)
-                counts, degree = counted(first, second)
-                for piece in range(pieces):
-                    ref, where = place(t, piece)
-                    total = ref[where].astype(jnp.float32) + part(counts, piece)
-                    ref[where] = total.astype(jnp.bfloat16)
-                add_degree(i, t - i * GROUP, degree)
-            return carry
-
-        lax.fori_loop(0, (short + 1) // 2, add_two, 0)
-
-        def long(u, carry):
-            t = i * GROUP + u
+            second, _ = pair_of(first, next_ref)
+            add(t, [first, second])
+        for k in range(4):
+            t = list_ref[0, 4 * j + k]
+
+            @pl.when(t < tiles)
+            def _():
+                copy_tile(t)
+
+        return carry
+
+    def add_mid(j, carry):
+        for k in range(2):
+            t = list_ref[1, 2 * j + k]
             first = head_ref[t]
-            _, after = pair_of(first, next_ref)
-
-            @pl.when(after >= 0)
+            second, third = pair_of(first, next_ref)
+            fourth, _ = pair_of(third, next_ref)
+            add(t, [first, second, third, fourth])
+        for k in range(2):
+            t = list_ref[1, 2 * j + k]
+
+            @pl.when(t < tiles)
             def _():
-                for piece in range(pieces):
-                    ref, where = place(t, piece)
-                    sum_ref[pl.ds(piece * slots, slots), :] = ref[where].astype(jnp.float32)
-
-                def step(first):
-                    second, after = pair_of(first, next_ref)
-                    counts, degree = counted(first, second)
-                    sum_ref[...] += counts
-                    add_degree(i, u, degree)
-                    return after
-
-                lax.while_loop(lambda first: first >= 0, step, first)
-                for piece in range(pieces):
-                    ref, where = place(t, piece)
-                    ref[where] = sum_ref[pl.ds(piece * slots, slots), :].astype(jnp.bfloat16)
-
-            return carry
-
-        lax.fori_loop(0, GROUP, long, 0)
+                copy_tile(t)
+
+        return carry
+
+    def add_long(j, carry):
+        t = list_ref[2, j]
+        for piece in range(pieces):
+            ref, where = place(t, piece)
+            sum_ref[pl.ds(piece * slots, slots), :] = ref[where].astype(jnp.float32)
+
+        def step(first):
+            second, after = pair_of(first, next_ref)
+            counts, degree = counted([first, second])
+            sum_ref[...] += counts
+            add_degree(t, degree)
+            return after
+
+        lax.while_loop(lambda first: first >= 0, step, head_ref[t])
+        for piece in range(pieces):
+            ref, where = place(t, piece)
+            ref[where] = sum_ref[pl.ds(piece * slots, slots), :].astype(jnp.bfloat16)
+        copy_tile(t)
+        return carry
+
+    lax.fori_loop(0, (short + 3) // 4, add_short, 0)
+    lax.fori_loop(0, (mid + 1) // 2, add_mid, 0)
+    lax.fori_loop(0, long, add_long, 0)
+
+    def pool_own(i, carry):
         some = pl.ds(pl.multiple_of(i * GROUP * slots, GROUP * slots), GROUP * slots)
         pooled_v[some, :] = jnp.dot(
             local_v[some, :], own_ref[...], preferred_element_type=jnp.float32
         )
-        pltpu.make_async_copy(local_v.at[some], local_ref.at[some], sems.at[0]).start()
-        pltpu.make_async_copy(remote_v.at[some], remote_ref.at[some], sems.at[1]).start()
         pltpu.make_async_copy(pooled_v.at[some], pooled_ref.at[some], sems.at[2]).start()
         return carry
 
-    lax.fori_loop(0, tiles // GROUP, group, 0)
+    lax.fori_loop(0, tiles // GROUP, pool_own, 0)
     every = pl.ds(0, tiles * slots)
     pltpu.make_async_copy(local_v.at[every], local_ref, sems.at[0]).wait()
     pltpu.make_async_copy(remote_v.at[every], remote_ref, sems.at[1]).wait()
     pltpu.make_async_copy(pooled_v, pooled_ref, sems.at[2]).wait()
-    pltpu.sync_copy(degree_ref, degree_hbm)
+    pltpu.sync_copy(degree_ref.at[pl.ds(0, tiles // GROUP)], degree_hbm)
 
 
 def build(tile_of, count, source, relation, target, own, *, relations, remote_rows):
@@ -366,13 +417,13 @@
             pltpu.VMEM((blocks, block_width), jnp.int32),
             pltpu.VMEM((blocks, block_width), jnp.int32),
             pltpu.VMEM((node_rows, width), jnp.bfloat16),
-            pltpu.VMEM((tiles // GROUP, slots, GROUP), jnp.float32),
+            pltpu.VMEM((tiles // GROUP + 1, slots, GROUP), jnp.float32),
             pltpu.VMEM((rows + slots, node_rows), jnp.bfloat16),
             pltpu.VMEM((rows + slots, remote_rows), jnp.bfloat16),
             pltpu.VMEM((rows, width), jnp.float32),
             pltpu.SMEM((tiles + 1,), jnp.int32),
             pltpu.SMEM((blocks,), jnp.int32),
-            pltpu.SMEM((GROUP + 1,), jnp.int32),
+            pltpu.SMEM((3, tiles + 8), jnp.int32),
             pltpu.VMEM((blocks, block_width), jnp.int32),
             pltpu.VMEM((blocks, block_width), jnp.int32),
             pltpu.VMEM((blocks, block_width), jnp.int32),
@@ -391,7 +442,7 @@
 
 
 def pool_groups(
-    counts_ref, counts_v, sems, table_ref, degree_ref, mean_ref, relations, ready=None, extra=None
+    counts_ref, counts_v, sems, table_ref, degree_ref, mean_ref, relations, begun, extra=None
 ):
     size = GROUP * WIN * relations
     groups = counts_ref.shape[0] // size
@@ -423,8 +474,7 @@
         return carry
 
     lax.fori_loop(0, groups, begin, 0)
-    if ready is not None:
-        ready()
+    begun()
     lax.fori_loop(0, groups, step, 0)
 
 
@@ -439,12 +489,12 @@
 ):
     inputs = start_all(in_sems, (degree_hbm, degree_v))
 
-    def ready():
+    def begun():
         copy_table(incoming_ref, table_v, slot)
         wait_all(inputs)
 
     pool_groups(
-        counts_ref, counts_v, sems, table_v, degree_v, mean_ref, relations, ready,
+        counts_ref, counts_v, sems, table_v, degree_v, mean_ref, relations, begun,
         extra=(pooled_ref, pooled_v),
     )
 
@@ -588,11 +638,14 @@
 
 def weight_copies(pieces, weights_v, relations):
     width = weights_v.shape[1]
-    class_ = lax.axis_index("dom") & (relations - 1)
-    return [
-        (piece, weights_v.at[pl.ds(pl.multiple_of((class_ ^ k) * width, width), width)])
-        for k, piece in enumerate(pieces)
-    ]
+    ways = relations // EACH
+    class_ = lax.axis_index("dom") & (ways - 1)
+
+    def rows(k):
+        relation = (class_ ^ (k // EACH)) + ways * (k % EACH)
+        return weights_v.at[pl.ds(pl.multiple_of(relation * width, width), width)]
+
+    return [(piece, rows(k)) for k, piece in enumerate(pieces)]
 
 
 def first_body(
@@ -600,17 +653,22 @@
 ):
     pieces, refs = refs[:relations], refs[relations:]
     out_hbm, own_v, degree_v, self_v, bias_v, out_v, weights_v, counts_v, mean_v, sems, in_sems = refs
-    inputs = start_all(
-        in_sems,
-        (own_hbm, own_v),
-        (degree_hbm, degree_v),
-        (self_hbm, self_v),
-        (bias_hbm, bias_v),
-        *weight_copies(pieces, weights_v, relations),
-    )
-    pool_groups(
-        counts_ref, counts_v, sems, own_v, degree_v, mean_v, relations, lambda: wait_all(inputs)
-    )
+    inputs = start_all(in_sems, (own_hbm, own_v), (degree_hbm, degree_v))
+    later = []
+
+    def begun():
+        later.extend(
+            start_all(
+                in_sems.at[pl.ds(2, 2 + relations)],
+                (self_hbm, self_v),
+                (bias_hbm, bias_v),
+                *weight_copies(pieces, weights_v, relations),
+            )
+        )
+        wait_all(inputs)
+
+    pool_groups(counts_ref, counts_v, sems, own_v, degree_v, mean_v, relations, begun)
+    wait_all(later)
     total = jnp.dot(mean_v[...], weights_v[...], preferred_element_type=jnp.float32)
     total += jnp.dot(own_v[...], self_v[...], preferred_element_type=jnp.float32)
     out_v[...] = total + bias_v[...]
@@ -649,15 +707,21 @@
 def last_body(counts_ref, table_ref, degree_hbm, partial_hbm, *refs, relations):
     pieces, refs = refs[:relations], refs[relations:]
     out_ref, degree_v, partial_v, weights_v, counts_v, mean_v, sems, in_sems = refs
-    inputs = start_all(
-        in_sems,
-        (degree_hbm, degree_v),
-        (partial_hbm, partial_v),
-        *weight_copies(pieces, weights_v, relations),
-    )
-    pool_groups(
-        counts_ref, counts_v, sems, table_ref, degree_v, mean_v, relations, lambda: wait_all(inputs)
-    )
+    inputs = start_all(in_sems, (degree_hbm, degree_v))
+    later = []
+
+    def begun():
+        later.extend(
+            start_all(
+                in_sems.at[pl.ds(1, 1 + relations)],
+                (partial_hbm, partial_v),
+                *weight_copies(pieces, weights_v, relations),
+            )
+        )
+        wait_all(inputs)
+
+    pool_groups(counts_ref, counts_v, sems, table_ref, degree_v, mean_v, relations, begun)
+    wait_all(later)
     total = jnp.dot(mean_v[...], weights_v[...], preferred_element_type=jnp.float32)
     out_ref[...] = (total + partial_v[...]).astype(out_ref.dtype)
 
@@ -716,7 +780,8 @@
     own = [self_first[...], self_second[...]]
     for device in range(devices):
         side = device % 2
-        rows = first[side * half : (side + 1) * half] + [own[side], second[device % relations]]
+        ways = relations // EACH
+        rows = first[side * half : (side + 1) * half] + [own[side]] + second[device % ways :: ways]
         for k, value in enumerate(rows):
             at = slot + k * piece
             out_v[device, at : at + piece, :] = value
@@ -733,7 +798,7 @@
     relations = coef_first.shape[0]
     piece, width = self_first.shape
     hbm = pl.BlockSpec(memory_space=pltpu.HBM)
-    shape = (devices, slot + (relations // 2 + 2) * piece, width)
+    shape = (devices, slot + (relations // 2 + 1 + EACH) * piece, width)
     args = (
         coef_first, coef_second, bases_first, bases_second, self_first, self_second, features, send,
     )
@@ -873,26 +938,29 @@
 
     next_at = slot + (relations // 2 + 1) * self_first.shape[0]
     swapped = from_peer(incoming[:, slot:next_at], 1)
-    pieces = {0: incoming[:, next_at:].reshape(width, width)}
+    row = self_first.shape[0]
+    pieces = {
+        (0, e): incoming[:, next_at + e * row : next_at + (e + 1) * row].reshape(width, width)
+        for e in range(EACH)
+    }
 
     def widen(mask):
-        pieces.update({k | mask: from_peer(piece, mask) for k, piece in sorted(pieces.items())})
-
-    mask = relations // 2
+        pieces.update(
+            {(k | mask, e): from_peer(piece, mask) for (k, e), piece in sorted(pieces.items())}
+        )
+
+    mask = relations // EACH // 2
     widen(mask)
     mean = pool(remote, pooled, incoming, degree, relations=relations, slot=slot)
     pieces, mean = lax.optimization_barrier((pieces, mean))
-    while mask > 2:
+    while mask > 1:
         mask //= 2
         widen(mask)
     hidden, picked, self_next = middle(
         mean, features, incoming, swapped, bias_first[None], send, relations=relations
     )
     pieces, picked = lax.optimization_barrier((pieces, picked))
-    while mask > 1:
-        mask //= 2
-        widen(mask)
-    pieces = [pieces[k] for k in range(relations)]
+    pieces = [piece for _, piece in sorted(pieces.items())]
     table = lax.all_to_all(picked, "dom", split_axis=0, concat_axis=0, tiled=True)
     partial = first(
         local, hidden, degree, self_next, bias_second[None], pieces, relations=relations

time: 94.4 us -> 92.2 us (0.977)
  waiting for transfers between devices: 5.37 us -> 11.7 us
  Pallas kernels: 68.5 us -> 63.9 us
  starting transfers between devices: 18.5 us -> 14.4 us
    all_to_all x1, waiting for transfers between devices: 0.01 us -> 6.53 us  [shards(): lax.all_to_all(outgoing, 'dom', split_axis=0, concat_axis=0, tiled=True)]
    pallas_call x1, Pallas kernels: 30.7 us -> 27 us  [build(): pl.pallas_call(functools.partial(build_body, tiles=tiles, relations=relat...]
    ppermute x8 -> x7, waiting for transfers between devices: 3.15 us -> 0.02 us  [from_peer(): return lax.ppermute(array, 'dom', [(i, i ^ mask) for i in range(devices)])]
    all_to_all x1, waiting for transfers between devices: 2.22 us -> 5.15 us  [shards(): lax.all_to_all(picked, 'dom', split_axis=0, concat_axis=0, tiled=True)]
    all_to_all x1, starting transfers between devices: 6 us -> 3.86 us  [shards(): lax.all_to_all(picked, 'dom', split_axis=0, concat_axis=0, tiled=True)]
    ppermute x8 -> x7, starting transfers between devices: 5.15 us -> 3.23 us  [from_peer(): return lax.ppermute(array, 'dom', [(i, i ^ mask) for i in range(devices)])]
  transfers between devices with their start and end apart: 10 -> 9, of which waited for: 6 -> 2; matrix products, arithmetic and copies ran while one was open for 1% -> 1% of each run, Pallas kernels for 58% -> 55%
where the time goes in v4:
time: 92.2 us; the launch traced here: 91.8 us
  Pallas kernels  63.9 us (69%)
  starting transfers between devices  14.4 us (16%)
  waiting for transfers between devices  11.7 us (13%)
  between operations  1.08 us (1%)
    pallas_call x1, Pallas kernels, build(): pl.pallas_call(functools.partial(build_body, tiles=tiles, relations=relat...  27 us
    pallas_call x1, Pallas kernels, first(): pl.pallas_call(functools.partial(first_body, relations=relations), out_sh...  10.2 us
    pallas_call x1, Pallas kernels, last(): pl.pallas_call(functools.partial(last_body, relations=relations), out_sha...  9.67 us
    pallas_call x1, Pallas kernels, pool(): pl.pallas_call(functools.partial(pool_body, relations=relations, slot=slo...  9.18 us
    all_to_all x1, starting transfers between devices, shards(): lax.all_to_all(outgoing, 'dom', split_axis=0, concat_axis=0, tiled=True)  7.33 us
    all_to_all x1, waiting for transfers between devices, shards(): lax.all_to_all(outgoing, 'dom', split_axis=0, concat_axis=0, tiled=True)  6.53 us
    all_to_all x1, waiting for transfers between devices, shards(): lax.all_to_all(picked, 'dom', split_axis=0, concat_axis=0, tiled=True)  5.15 us
    pallas_call x1, Pallas kernels, middle(): pl.pallas_call(functools.partial(middle_body, relations=relations, slot=s...  4.32 us
  transfers between devices with their start and end apart: 9, of which 2 were waited for; matrix products, arithmetic and copies ran while one was open for 1% of the time, Pallas kernels for 55%

profile of v4, /device:TPU:0, one launch (start us, length us, event | category | flops | bytes accessed | tf_op | source)
XLA Modules:
  0.0 91.8 jit_solution(7442463308613542686)
XLA Ops:
  0.0 3.5 %pack.1 = bf16[32,88,256]{2,1,0:T(8,128)(2,1)} custom-call(f32[8,30]{1,0:T(8,128)} %refs_0_.1, f32[8,30]{1,0:T(8,128)} %refs_1_.1, bf16[30,8,256]{2,1,0:T(8,128)(2,1)} %refs_2_.1, bf16[30,8,256]{2,1,0:T(8,128)(2,1)} %refs_3_.1, bf16[8,256]{1,0:T(8,128)(2,1)} %refs_4_.1, bf16[8,256]{1,0:T(8,128)(2,1)} %refs_5_.1, bf16[1024,256]{1,0:T(8,128)(2,1)} %own_hbm.3, ...), custom_call_target="tpu_custom_call" | custom-call | flops 536870912 | tf_op jit(solution)/shard_map/pack/pallas_call | solution.py:805
  3.5 7.3 %all-to-all-start = ((bf16[32,88,256]{2,1,0:T(8,128)(2,1)}), bf16[32,88,256]{2,1,0:T(8,128)(2,1)S(1)}, u32[]{:S(2)}, u32[]{:S(2)}) async-start(bf16[32,88,256]{2,1,0:T(8,128)(2,1)} %pack.1), calls=%async_computation | async-start | bytes 2883584 | tf_op jit(solution)/shard_map/all_to_all | solution.py:930
  11.5 0.6 slice_reduce_fusion.tile_ref
  12.1 27.0 %build.1 = (bf16[8192,1024]{1,0:T(8,128)(2,1)}, bf16[8192,1024]{1,0:T(8,128)(2,1)}, f32[8192,256]{1,0:T(8,128)}, f32[8,128,8]{2,1,0:T(8,128)}) custom-call(s32[128]{0:T(128)} %slice_reduce_fusion.tile_ref, s32[1]{0:T(128)S(6)} %copy.15.count_ref, s32[128,128]{1,0:T(8,128)} %bitcast.17, s32[128,128]{1,0:T(8,128)} %bitcast.18, s32[128,128]{1,0:T(8,128)} %bitcast.14, ...), custom_call_target="tpu_custom_call" | custom-call | flops 17179869184 | bytes 33554432 | tf_op jit(solution)/shard_map/build/pallas_call | solution.py:403
  39.1 6.5 %all-to-all-done.incoming_ref = bf16[32,88,256]{2,1,0:T(8,128)(2,1)S(1)} async-done(((bf16[32,88,256]{2,1,0:T(8,128)(2,1)}), bf16[32,88,256]{2,1,0:T(8,128)(2,1)S(1)}, u32[]{:S(2)}, u32[]{:S(2)}) %all-to-all-start) | async-done | bytes 1441824 | tf_op jit(solution)/shard_map/all_to_all | solution.py:930
  45.7 0.1 collective-permute-start.6
  45.8 0.0 copy-start.1
  45.8 0.0 copy-start
  45.8 1.3 %collective-permute-start.1 = (bf16[256,256]{1,0:T(8,128)(2,1)S(1)}, bf16[256,256]{1,0:T(8,128)(2,1)S(1)}, u32[]{:S(2)}, u32[]{:S(2)}) collective-permute-start(bf16[256,256]{1,0:T(8,128)(2,1)S(1)} %get-tuple-element.46.refs_1_), channel_id=1, source_target_pairs={{0,2},{1,3},{2,0},{3,1},{4,6},{5,7},{6,4},{7,5},{8,10},{9,11},{10,... | collective-permute-start | bytes 393224 | tf_op jit(solution)/shard_map/ppermute | solution.py:937
  47.2 0.8 collective-permute-start
  47.9 9.2 %pool.1.mean_ref = bf16[1024,2048]{1,0:T(8,128)(2,1)S(1)} custom-call(bf16[8192,1024]{1,0:T(8,128)(2,1)} %get-tuple-element.30.counts_ref, f32[8192,256]{1,0:T(8,128)} %get-tuple-element.33.pooled_ref, bf16[32,88,256]{2,1,0:T(8,128)(2,1)S(1)} %all-to-all-done.incoming_ref, f32[8,128,8]{2,1,0:T(8,128)} %get-tuple-element.34.degree_hbm), custom_call_target="tpu_custom_call" | custom-call | flops 4294967296 | bytes 16777216 | tf_op jit(solution)/shard_map/pool/pallas_call | solution.py:507
  57.1 0.0 collective-permute-done.1.refs_5_
  57.1 0.0 collective-permute-done.refs_4_
  57.2 0.1 collective-permute-start.2
  57.2 0.0 copy-done
  57.3 0.5 collective-permute-start.3
  57.7 0.1 collective-permute-start.4
  57.8 0.4 collective-permute-start.5
  58.3 0.0 collective-permute-done.6.swapped_ref
  58.3 4.3 %middle.1 = (bf16[1024,256]{1,0:T(8,128)(2,1)}, bf16[32,32,256]{2,1,0:T(8,128)(2,1)}, bf16[256,256]{1,0:T(8,128)(2,1)}) custom-call(bf16[1024,2048]{1,0:T(8,128)(2,1)S(1)} %pool.1.mean_ref, bf16[1024,256]{1,0:T(8,128)(2,1)} %own_hbm.3, bf16[32,88,256]{2,1,0:T(8,128)(2,1)S(1)} %all-to-all-done.incoming_ref, ...), custom_call_target="tpu_custom_call" | custom-call | flops 1073741824 | tf_op jit(solution)/shard_map/middle/pallas_call | solution.py:613
  62.6 0.0 collective-permute-done.2.refs_2_
  62.6 0.0 collective-permute-done.3.refs_3_
  62.6 0.0 collective-permute-done.4.refs_6_
  62.6 0.0 collective-permute-done.5.refs_7_
  62.7 3.9 %all-to-all-start.1 = ((bf16[32,32,256]{2,1,0:T(8,128)(2,1)}), bf16[32,32,256]{2,1,0:T(8,128)(2,1)S(1)}, u32[]{:S(2)}, u32[]{:S(2)}) async-start(bf16[32,32,256]{2,1,0:T(8,128)(2,1)} %get-tuple-element.41), calls=%async_computation.1 | async-start | bytes 1048576 | tf_op jit(solution)/shard_map/all_to_all | solution.py:964
  66.5 0.0 copy-done.2
  66.5 0.0 copy-done.3
  66.6 0.0 copy-done.4
  66.6 0.0 copy-done.5
  66.6 10.2 %first.1.partial_hbm = f32[1024,256]{1,0:T(8,128)} custom-call(bf16[8192,1024]{1,0:T(8,128)(2,1)} %get-tuple-element.42.counts_ref, bf16[1024,256]{1,0:T(8,128)(2,1)} %get-tuple-element.43.own_hbm, f32[8,128,8]{2,1,0:T(8,128)} %get-tuple-element.34.degree_hbm, bf16[256,256]{1,0:T(8,128)(2,1)} %get-tuple-element.44.self_hbm, f32[1,256]{1,0:T(1,128)} %bitcast.16, ...), custom_call_target="tpu_custom_call" | custom-call | flops 5368709120 | bytes 16777216 | tf_op jit(solution)/shard_map/first/pallas_call | solution.py:682
  76.8 5.1 %all-to-all-done.1 = bf16[32,32,256]{2,1,0:T(8,128)(2,1)S(1)} async-done(((bf16[32,32,256]{2,1,0:T(8,128)(2,1)}), bf16[32,32,256]{2,1,0:T(8,128)(2,1)S(1)}, u32[]{:S(2)}, u32[]{:S(2)}) %all-to-all-start.1) | async-done | bytes 524320 | tf_op jit(solution)/shard_map/all_to_all | solution.py:964
  82.0 9.7 %last.1 = bf16[1024,256]{1,0:T(8,128)(2,1)} custom-call(bf16[8192,1024]{1,0:T(8,128)(2,1)} %get-tuple-element.30.counts_ref, bf16[1024,256]{1,0:T(8,128)(2,1)S(1)} %bitcast.11, f32[8,128,8]{2,1,0:T(8,128)} %get-tuple-element.34.degree_hbm, f32[1024,256]{1,0:T(8,128)} %first.1.partial_hbm, bf16[256,256]{1,0:T(8,128)(2,1)} %copy-done.1, ...), custom_call_target="tpu_custom_call" | custom-call | flops 5368709120 | bytes 16777216 | tf_op jit(solution)/shard_map/last/pallas_call | solution.py:735
  (13 shorter events, 0.1 us)
Async XLA Ops:
  0.0 11.5 %copy-start.8 = (s32[1,128,128]{2,1,0:T(8,128)S(1)}, s32[1,128,128]{2,1,0:T(8,128)}, u32[]{:S(2)}) copy-start(s32[1,128,128]{2,1,0:T(8,128)} %param.17) | copy-start | bytes 196612
  3.5 42.2 %all-to-all-start = ((bf16[32,88,256]{2,1,0:T(8,128)(2,1)}), bf16[32,88,256]{2,1,0:T(8,128)(2,1)S(1)}, u32[]{:S(2)}, u32[]{:S(2)}) async-start(bf16[32,88,256]{2,1,0:T(8,128)(2,1)} %pack.1), calls=%async_computation | async-start | bytes 2883584 | tf_op jit(solution)/shard_map/all_to_all | solution.py:930
  45.7 12.6 %collective-permute-start.6 = (bf16[32,40,256]{2,1,0:T(8,128)(2,1)S(1)}, bf16[32,40,256]{2,1,0:T(8,128)(2,1)S(1)}, u32[]{:S(2)}, u32[]{:S(2)}) collective-permute-start(bf16[32,40,256]{2,1,0:T(8,128)(2,1)S(1)} %slice.15), channel_id=1, source_target_pairs={{0,1},{1,0},{2,3},{3,2},{4,5},{5,4},{6,7},{7,6},{8,9},{9,8},{10,11... | collective-permute-start | bytes 1966088 | tf_op jit(solution)/shard_map/ppermute | solution.py:937
  45.8 11.3 %copy-start.1 = (bf16[256,256]{1,0:T(8,128)(2,1)}, bf16[256,256]{1,0:T(8,128)(2,1)S(1)}, u32[]{:S(2)}) copy-start(bf16[256,256]{1,0:T(8,128)(2,1)S(1)} %get-tuple-element.45.refs_0_) | copy-start | bytes 393220
  45.8 11.4 %copy-start = (bf16[256,256]{1,0:T(8,128)(2,1)}, bf16[256,256]{1,0:T(8,128)(2,1)S(1)}, u32[]{:S(2)}) copy-start(bf16[256,256]{1,0:T(8,128)(2,1)S(1)} %get-tuple-element.46.refs_1_) | copy-start | bytes 393220
  45.8 11.3 %collective-permute-start.1 = (bf16[256,256]{1,0:T(8,128)(2,1)S(1)}, bf16[256,256]{1,0:T(8,128)(2,1)S(1)}, u32[]{:S(2)}, u32[]{:S(2)}) collective-permute-start(bf16[256,256]{1,0:T(8,128)(2,1)S(1)} %get-tuple-element.46.refs_1_), channel_id=1, source_target_pairs={{0,2},{1,3},{2,0},{3,1},{4,6},{5,7},{6,4},{7,5},{8,10},{9,11},{10,... | collective-permute-start | bytes 393224 | tf_op jit(solution)/shard_map/ppermute | solution.py:937
  47.2 10.0 %collective-permute-start = (bf16[256,256]{1,0:T(8,128)(2,1)S(1)}, bf16[256,256]{1,0:T(8,128)(2,1)S(1)}, u32[]{:S(2)}, u32[]{:S(2)}) collective-permute-start(bf16[256,256]{1,0:T(8,128)(2,1)S(1)} %get-tuple-element.45.refs_0_), channel_id=1, source_target_pairs={{0,2},{1,3},{2,0},{3,1},{4,6},{5,7},{6,4},{7,5},{8,10},{9,11},{10,... | collective-permute-start | bytes 393224 | tf_op jit(solution)/shard_map/ppermute | solution.py:937
  57.1 9.4 %copy-start.2 = (bf16[256,256]{1,0:T(8,128)(2,1)}, bf16[256,256]{1,0:T(8,128)(2,1)S(1)}, u32[]{:S(2)}) copy-start(bf16[256,256]{1,0:T(8,128)(2,1)S(1)} %collective-permute-done.1.refs_5_) | copy-start | bytes 393220
  57.2 9.4 %copy-start.3 = (bf16[256,256]{1,0:T(8,128)(2,1)}, bf16[256,256]{1,0:T(8,128)(2,1)S(1)}, u32[]{:S(2)}) copy-start(bf16[256,256]{1,0:T(8,128)(2,1)S(1)} %collective-permute-done.refs_4_) | copy-start | bytes 393220
  57.2 5.4 %collective-permute-start.2 = (bf16[256,256]{1,0:T(8,128)(2,1)S(1)}, bf16[256,256]{1,0:T(8,128)(2,1)S(1)}, u32[]{:S(2)}, u32[]{:S(2)}) collective-permute-start(bf16[256,256]{1,0:T(8,128)(2,1)S(1)} %get-tuple-element.45.refs_0_), channel_id=1, source_target_pairs={{0,1},{1,0},{2,3},{3,2},{4,5},{5,4},{6,7},{7,6},{8,9},{9,8},{10,11... | collective-permute-start | bytes 393224 | tf_op jit(solution)/shard_map/ppermute | solution.py:937
  57.3 5.4 %collective-permute-start.3 = (bf16[256,256]{1,0:T(8,128)(2,1)S(1)}, bf16[256,256]{1,0:T(8,128)(2,1)S(1)}, u32[]{:S(2)}, u32[]{:S(2)}) collective-permute-start(bf16[256,256]{1,0:T(8,128)(2,1)S(1)} %get-tuple-element.46.refs_1_), channel_id=1, source_target_pairs={{0,1},{1,0},{2,3},{3,2},{4,5},{5,4},{6,7},{7,6},{8,9},{9,8},{10,11... | collective-permute-start | bytes 393224 | tf_op jit(solution)/shard_map/ppermute | solution.py:937
  57.7 4.9 %collective-permute-start.4 = (bf16[256,256]{1,0:T(8,128)(2,1)S(1)}, bf16[256,256]{1,0:T(8,128)(2,1)S(1)}, u32[]{:S(2)}, u32[]{:S(2)}) collective-permute-start(bf16[256,256]{1,0:T(8,128)(2,1)S(1)} %collective-permute-done.refs_4_), channel_id=1, source_target_pairs={{0,1},{1,0},{2,3},{3,2},{4,5},{5,4},{6,7},{7,6},{8,9},{9,8},{10,11... | collective-permute-start | bytes 393224 | tf_op jit(solution)/shard_map/ppermute | solution.py:937
  57.8 4.8 %collective-permute-start.5 = (bf16[256,256]{1,0:T(8,128)(2,1)S(1)}, bf16[256,256]{1,0:T(8,128)(2,1)S(1)}, u32[]{:S(2)}, u32[]{:S(2)}) collective-permute-start(bf16[256,256]{1,0:T(8,128)(2,1)S(1)} %collective-permute-done.1.refs_5_), channel_id=1, source_target_pairs={{0,1},{1,0},{2,3},{3,2},{4,5},{5,4},{6,7},{7,6},{8,9},{9,8},{10,11... | collective-permute-start | bytes 393224 | tf_op jit(solution)/shard_map/ppermute | solution.py:937
  62.6 4.0 %copy-start.4 = (bf16[256,256]{1,0:T(8,128)(2,1)}, bf16[256,256]{1,0:T(8,128)(2,1)S(1)}, u32[]{:S(2)}) copy-start(bf16[256,256]{1,0:T(8,128)(2,1)S(1)} %collective-permute-done.2.refs_2_) | copy-start | bytes 393220
  62.6 3.9 %copy-start.5 = (bf16[256,256]{1,0:T(8,128)(2,1)}, bf16[256,256]{1,0:T(8,128)(2,1)S(1)}, u32[]{:S(2)}) copy-start(bf16[256,256]{1,0:T(8,128)(2,1)S(1)} %collective-permute-done.3.refs_3_) | copy-start | bytes 393220
  62.6 3.9 %copy-start.6 = (bf16[256,256]{1,0:T(8,128)(2,1)}, bf16[256,256]{1,0:T(8,128)(2,1)S(1)}, u32[]{:S(2)}) copy-start(bf16[256,256]{1,0:T(8,128)(2,1)S(1)} %collective-permute-done.4.refs_6_) | copy-start | bytes 393220
  62.7 3.9 %copy-start.7 = (bf16[256,256]{1,0:T(8,128)(2,1)}, bf16[256,256]{1,0:T(8,128)(2,1)S(1)}, u32[]{:S(2)}) copy-start(bf16[256,256]{1,0:T(8,128)(2,1)S(1)} %collective-permute-done.5.refs_7_) | copy-start | bytes 393220
  62.7 19.3 %all-to-all-start.1 = ((bf16[32,32,256]{2,1,0:T(8,128)(2,1)}), bf16[32,32,256]{2,1,0:T(8,128)(2,1)S(1)}, u32[]{:S(2)}, u32[]{:S(2)}) async-start(bf16[32,32,256]{2,1,0:T(8,128)(2,1)} %get-tuple-element.41), calls=%async_computation.1 | async-start | bytes 1048576 | tf_op jit(solution)/shard_map/all_to_all | solution.py:964

commit v5 on v4

--- a/solution.py
+++ b/solution.py
@@ -10,7 +10,7 @@
 WIN = 16
 CHUNK = 512
 GROUP = 8
-EACH = 2
+EACH = 1
 MIB = 1 << 20
 WHOLE_MAX = 36 * MIB
 CONTRACT_LANES = (((1,), (1,)), ((), ()))
@@ -378,7 +378,7 @@
         some = pl.ds(pl.multiple_of(i * GROUP * slots, GROUP * slots), GROUP * slots)
         pooled_v[some, :] = jnp.dot(
             local_v[some, :], own_ref[...], preferred_element_type=jnp.float32
-        )
+        ).astype(jnp.bfloat16)
         pltpu.make_async_copy(pooled_v.at[some], pooled_ref.at[some], sems.at[2]).start()
         return carry
 
@@ -407,7 +407,7 @@
         out_shape=[
             pltpu.HBM((rows, node_rows), jnp.bfloat16),
             pltpu.HBM((rows, remote_rows), jnp.bfloat16),
-            pltpu.HBM((rows, width), jnp.float32),
+            pltpu.HBM((rows, width), jnp.bfloat16),
             pltpu.HBM((tiles // GROUP, slots, GROUP), jnp.float32),
         ],
         in_specs=[smem, smem] + [hbm] * 4,
@@ -420,7 +420,7 @@
             pltpu.VMEM((tiles // GROUP + 1, slots, GROUP), jnp.float32),
             pltpu.VMEM((rows + slots, node_rows), jnp.bfloat16),
             pltpu.VMEM((rows + slots, remote_rows), jnp.bfloat16),
-            pltpu.VMEM((rows, width), jnp.float32),
+            pltpu.VMEM((rows, width), jnp.bfloat16),
             pltpu.SMEM((tiles + 1,), jnp.int32),
             pltpu.SMEM((blocks,), jnp.int32),
             pltpu.SMEM((3, tiles + 8), jnp.int32),
@@ -465,7 +465,7 @@
         some = pl.ds(pl.multiple_of(i * size, size), size)
         total = jnp.dot(counts_v[some, :], table_ref[...], preferred_element_type=jnp.float32)
         if extra is not None:
-            total += extra[1][some, :]
+            total += extra[1][some, :].astype(jnp.float32)
         share = 1.0 / jnp.maximum(degree_ref[i], 1.0)
         slots = WIN * relations
         for u in range(GROUP):
@@ -945,23 +945,23 @@
     }
 
     def widen(mask):
-        pieces.update(
-            {(k | mask, e): from_peer(piece, mask) for (k, e), piece in sorted(pieces.items())}
-        )
+        for (k, e), piece in sorted(pieces.items()):
+            pieces[k | mask, e] = from_peer(piece, mask)
 
     mask = relations // EACH // 2
     widen(mask)
     mean = pool(remote, pooled, incoming, degree, relations=relations, slot=slot)
     pieces, mean = lax.optimization_barrier((pieces, mean))
+    mask //= 2
+    widen(mask)
+    hidden, picked, self_next = middle(
+        mean, features, incoming, swapped, bias_first[None], send, relations=relations
+    )
+    table = lax.all_to_all(picked, "dom", split_axis=0, concat_axis=0, tiled=True)
     while mask > 1:
         mask //= 2
         widen(mask)
-    hidden, picked, self_next = middle(
-        mean, features, incoming, swapped, bias_first[None], send, relations=relations
-    )
-    pieces, picked = lax.optimization_barrier((pieces, picked))
     pieces = [piece for _, piece in sorted(pieces.items())]
-    table = lax.all_to_all(picked, "dom", split_axis=0, concat_axis=0, tiled=True)
     partial = first(
         local, hidden, degree, self_next, bias_second[None], pieces, relations=relations
     )

time: 92.2 us -> 98.5 us (1.068)
  waiting for transfers between devices: 11.7 us -> 15.9 us
  starting transfers between devices: 14.4 us -> 17.5 us
  Pallas kernels: 63.9 us -> 62.4 us
    ppermute x7 -> x8, waiting for transfers between devices: 0.02 us -> 12.1 us  [from_peer(): return lax.ppermute(array, 'dom', [(i, i ^ mask) for i in range(devices)])]
    all_to_all x1, waiting for transfers between devices: 5.15 us -> 0.01 us  [shards(): lax.all_to_all(picked, 'dom', split_axis=0, concat_axis=0, tiled=True)]
    all_to_all x1, waiting for transfers between devices: 6.53 us -> 3.78 us  [shards(): lax.all_to_all(outgoing, 'dom', split_axis=0, concat_axis=0, tiled=True)]
    all_to_all x1, starting transfers between devices: 3.86 us -> 6.07 us  [shards(): lax.all_to_all(picked, 'dom', split_axis=0, concat_axis=0, tiled=True)]
    pallas_call x1, Pallas kernels: 9.18 us -> 7.95 us  [pool(): pl.pallas_call(functools.partial(pool_body, relations=relations, slot=slo...]
    ppermute x7 -> x8, starting transfers between devices: 3.23 us -> 4.11 us  [from_peer(): return lax.ppermute(array, 'dom', [(i, i ^ mask) for i in range(devices)])]
  transfers between devices with their start and end apart: 9 -> 10, of which waited for: 2 -> 4; matrix products, arithmetic and copies ran while one was open for 1% -> 1% of each run, Pallas kernels for 55% -> 46%
where the time goes in v5:
time: 98.5 us; the launch traced here: 98.2 us
  Pallas kernels  62.4 us (63%)
  starting transfers between devices  17.5 us (18%)
  waiting for transfers between devices  15.9 us (16%)
  local copies, waits for them, and re-layouts  1.32 us (1%)
  between operations  1.01 us (1%)
    pallas_call x1, Pallas kernels, build(): pl.pallas_call(functools.partial(build_body, tiles=tiles, relations=relat...  26.9 us
    ppermute x8, waiting for transfers between devices, from_peer(): return lax.ppermute(array, 'dom', [(i, i ^ mask) for i in range(devices)])  12.1 us
    pallas_call x1, Pallas kernels, first(): pl.pallas_call(functools.partial(first_body, relations=relations), out_sh...  10.2 us
    pallas_call x1, Pallas kernels, last(): pl.pallas_call(functools.partial(last_body, relations=relations), out_sha...  9.68 us
    pallas_call x1, Pallas kernels, pool(): pl.pallas_call(functools.partial(pool_body, relations=relations, slot=slo...  7.95 us
    all_to_all x1, starting transfers between devices, shards(): lax.all_to_all(outgoing, 'dom', split_axis=0, concat_axis=0, tiled=True)  7.33 us
    all_to_all x1, starting transfers between devices, shards(): lax.all_to_all(picked, 'dom', split_axis=0, concat_axis=0, tiled=True)  6.07 us
    pallas_call x1, Pallas kernels, middle(): pl.pallas_call(functools.partial(middle_body, relations=relations, slot=s...  4.33 us
  transfers between devices with their start and end apart: 10, of which 4 were waited for; matrix products, arithmetic and copies ran while one was open for 1% of the time, Pallas kernels for 46%

profile of v5, /device:TPU:0, one launch (start us, length us, event | category | flops | bytes accessed | tf_op | source)
XLA Modules:
  0.0 98.2 jit_solution(2015747211047390561)
XLA Ops:
  0.0 3.4 %pack.1 = bf16[32,80,256]{2,1,0:T(8,128)(2,1)} custom-call(f32[8,30]{1,0:T(8,128)} %refs_0_.1, f32[8,30]{1,0:T(8,128)} %refs_1_.1, bf16[30,8,256]{2,1,0:T(8,128)(2,1)} %refs_2_.1, bf16[30,8,256]{2,1,0:T(8,128)(2,1)} %refs_3_.1, bf16[8,256]{1,0:T(8,128)(2,1)} %refs_4_.1, bf16[8,256]{1,0:T(8,128)(2,1)} %refs_5_.1, bf16[1024,256]{1,0:T(8,128)(2,1)} %own_hbm.3, ...), custom_call_target="tpu_custom_call" | custom-call | flops 536870912 | tf_op jit(solution)/shard_map/pack/pallas_call | solution.py:805
  3.4 7.3 %all-to-all-start = ((bf16[32,80,256]{2,1,0:T(8,128)(2,1)}), bf16[32,80,256]{2,1,0:T(8,128)(2,1)S(1)}, u32[]{:S(2)}, u32[]{:S(2)}) async-start(bf16[32,80,256]{2,1,0:T(8,128)(2,1)} %pack.1), calls=%async_computation | async-start | bytes 2621440 | tf_op jit(solution)/shard_map/all_to_all | solution.py:930
  11.4 0.6 slice_reduce_fusion.tile_ref
  12.0 26.9 %build.1 = (bf16[8192,1024]{1,0:T(8,128)(2,1)}, bf16[8192,1024]{1,0:T(8,128)(2,1)}, bf16[8192,256]{1,0:T(8,128)(2,1)}, f32[8,128,8]{2,1,0:T(8,128)}) custom-call(s32[128]{0:T(128)} %slice_reduce_fusion.tile_ref, s32[1]{0:T(128)S(6)} %copy.15.count_ref, s32[128,128]{1,0:T(8,128)} %bitcast.15, s32[128,128]{1,0:T(8,128)} %bitcast.16, s32[128,128]{1,0:T(8,128)} %bitcast.12, ...), custom_call_target="tpu_custom_call" | custom-call | flops 17179869184 | bytes 33554432 | tf_op jit(solution)/shard_map/build/pallas_call | solution.py:403
  38.9 3.8 %all-to-all-done.incoming_ref = bf16[32,80,256]{2,1,0:T(8,128)(2,1)S(1)} async-done(((bf16[32,80,256]{2,1,0:T(8,128)(2,1)}), bf16[32,80,256]{2,1,0:T(8,128)(2,1)S(1)}, u32[]{:S(2)}, u32[]{:S(2)}) %all-to-all-start) | async-done | bytes 1310752 | tf_op jit(solution)/shard_map/all_to_all | solution.py:930
  42.7 0.1 collective-permute-start.1
  42.8 1.4 %collective-permute-start = (bf16[256,256]{1,0:T(8,128)(2,1)S(1)}, bf16[256,256]{1,0:T(8,128)(2,1)S(1)}, u32[]{:S(2)}, u32[]{:S(2)}) collective-permute-start(bf16[256,256]{1,0:T(8,128)(2,1)S(1)} %slice_bitcast_fusion.refs_0_), channel_id=1, source_target_pairs={{0,4},{1,5},{2,6},{3,7},{4,0},{5,1},{6,2},{7,3},{8,12},{9,13},{10,... | collective-permute-start | bytes 393224 | tf_op jit(solution)/shard_map/ppermute | solution.py:937
  44.3 8.0 %pool.1.mean_ref = bf16[1024,2048]{1,0:T(8,128)(2,1)S(1)} custom-call(bf16[8192,1024]{1,0:T(8,128)(2,1)} %get-tuple-element.19.counts_ref, bf16[8192,256]{1,0:T(8,128)(2,1)} %get-tuple-element.22.pooled_ref, bf16[32,80,256]{2,1,0:T(8,128)(2,1)S(1)} %all-to-all-done.incoming_ref, f32[8,128,8]{2,1,0:T(8,128)} %get-tuple-element.23.degree_hbm), custom_call_target="tpu_custom_call" | custom-call | flops 4294967296 | bytes 16777216 | tf_op jit(solution)/shard_map/pool/pallas_call | solution.py:507
  52.2 0.0 collective-permute-done.refs_4_
  52.2 0.0 collective-permute-done.1.swapped_ref
  52.3 4.3 %middle.1 = (bf16[1024,256]{1,0:T(8,128)(2,1)}, bf16[32,32,256]{2,1,0:T(8,128)(2,1)}, bf16[256,256]{1,0:T(8,128)(2,1)}) custom-call(bf16[1024,2048]{1,0:T(8,128)(2,1)S(1)} %pool.1.mean_ref, bf16[1024,256]{1,0:T(8,128)(2,1)} %own_hbm.3, bf16[32,80,256]{2,1,0:T(8,128)(2,1)S(1)} %all-to-all-done.incoming_ref, ...), custom_call_target="tpu_custom_call" | custom-call | flops 1073741824 | tf_op jit(solution)/shard_map/middle/pallas_call | solution.py:613
  56.6 6.1 %all-to-all-start.1 = ((bf16[32,32,256]{2,1,0:T(8,128)(2,1)}), bf16[32,32,256]{2,1,0:T(8,128)(2,1)S(1)}, u32[]{:S(2)}, u32[]{:S(2)}) async-start(bf16[32,32,256]{2,1,0:T(8,128)(2,1)} %get-tuple-element.25), calls=%async_computation.1 | async-start | bytes 1048576 | tf_op jit(solution)/shard_map/all_to_all | solution.py:960
  62.7 1.7 %collective-permute-start.3 = (bf16[256,256]{1,0:T(8,128)(2,1)S(1)}, bf16[256,256]{1,0:T(8,128)(2,1)S(1)}, u32[]{:S(2)}, u32[]{:S(2)}) collective-permute-start(bf16[256,256]{1,0:T(8,128)(2,1)S(1)} %slice_bitcast_fusion.refs_0_), channel_id=1, source_target_pairs={{0,2},{1,3},{2,0},{3,1},{4,6},{5,7},{6,4},{7,5},{8,10},{9,11},{10,... | collective-permute-start | bytes 393224 | tf_op jit(solution)/shard_map/ppermute | solution.py:937
  64.3 0.4 collective-permute-start.6
  64.8 0.0 collective-permute-start.2
  64.8 0.5 collective-permute-start.5
  65.3 7.7 %collective-permute-done.3.refs_2_ = bf16[256,256]{1,0:T(8,128)(2,1)S(1)} collective-permute-done((bf16[256,256]{1,0:T(8,128)(2,1)S(1)}, bf16[256,256]{1,0:T(8,128)(2,1)S(1)}, u32[]{:S(2)}, u32[]{:S(2)}) %collective-permute-start.3) | collective-permute-done | bytes 131104 | tf_op jit(solution)/shard_map/ppermute | solution.py:937
  73.0 0.0 collective-permute-start.4
  73.0 3.1 %collective-permute-done.6.refs_6_ = bf16[256,256]{1,0:T(8,128)(2,1)S(1)} collective-permute-done((bf16[256,256]{1,0:T(8,128)(2,1)S(1)}, bf16[256,256]{1,0:T(8,128)(2,1)S(1)}, u32[]{:S(2)}, u32[]{:S(2)}) %collective-permute-start.6) | collective-permute-done | bytes 131104 | tf_op jit(solution)/shard_map/ppermute | solution.py:937
  76.1 0.0 collective-permute-start.7
  76.1 0.0 collective-permute-done.2.refs_1_
  76.1 0.0 copy-start.4
  76.1 0.0 collective-permute-done.5.refs_5_
  76.2 0.0 collective-permute-done.4.refs_3_
  76.2 1.3 %collective-permute-done.7.refs_7_ = bf16[256,256]{1,0:T(8,128)(2,1)S(1)} collective-permute-done((bf16[256,256]{1,0:T(8,128)(2,1)S(1)}, bf16[256,256]{1,0:T(8,128)(2,1)S(1)}, u32[]{:S(2)}, u32[]{:S(2)}) %collective-permute-start.7) | collective-permute-done | bytes 131104 | tf_op jit(solution)/shard_map/ppermute | solution.py:937
  77.5 0.0 copy-done.2
  77.5 0.0 copy-done.4
  77.5 0.0 copy-done.5
  77.5 0.6 copy-done.7
  78.1 10.2 %first.1.partial_hbm = f32[1024,256]{1,0:T(8,128)} custom-call(bf16[8192,1024]{1,0:T(8,128)(2,1)} %get-tuple-element.26.counts_ref, bf16[1024,256]{1,0:T(8,128)(2,1)} %get-tuple-element.27.own_hbm, f32[8,128,8]{2,1,0:T(8,128)} %get-tuple-element.23.degree_hbm, bf16[256,256]{1,0:T(8,128)(2,1)} %get-tuple-element.28.self_hbm, f32[1,256]{1,0:T(1,128)} %bitcast.13, ...), custom_call_target="tpu_custom_call" | custom-call | flops 5368709120 | bytes 16777216 | tf_op jit(solution)/shard_map/first/pallas_call | solution.py:682
  88.3 0.0 all-to-all-done.1
  88.3 9.7 %last.1 = bf16[1024,256]{1,0:T(8,128)(2,1)} custom-call(bf16[8192,1024]{1,0:T(8,128)(2,1)} %get-tuple-element.19.counts_ref, bf16[1024,256]{1,0:T(8,128)(2,1)S(1)} %bitcast.9, f32[8,128,8]{2,1,0:T(8,128)} %get-tuple-element.23.degree_hbm, f32[1024,256]{1,0:T(8,128)} %first.1.partial_hbm, bf16[256,256]{1,0:T(8,128)(2,1)} %copy-done, ...), custom_call_target="tpu_custom_call" | custom-call | flops 5368709120 | bytes 16777216 | tf_op jit(solution)/shard_map/last/pallas_call | solution.py:735
  (15 shorter events, 0.1 us)
Async XLA Ops:
  0.0 11.4 %copy-start.8 = (s32[1,128,128]{2,1,0:T(8,128)S(1)}, s32[1,128,128]{2,1,0:T(8,128)}, u32[]{:S(2)}) copy-start(s32[1,128,128]{2,1,0:T(8,128)} %param.17) | copy-start | bytes 196612
  3.4 39.3 %all-to-all-start = ((bf16[32,80,256]{2,1,0:T(8,128)(2,1)}), bf16[32,80,256]{2,1,0:T(8,128)(2,1)S(1)}, u32[]{:S(2)}, u32[]{:S(2)}) async-start(bf16[32,80,256]{2,1,0:T(8,128)(2,1)} %pack.1), calls=%async_computation | async-start | bytes 2621440 | tf_op jit(solution)/shard_map/all_to_all | solution.py:930
  42.7 9.5 %collective-permute-start.1 = (bf16[32,40,256]{2,1,0:T(8,128)(2,1)S(1)}, bf16[32,40,256]{2,1,0:T(8,128)(2,1)S(1)}, u32[]{:S(2)}, u32[]{:S(2)}) collective-permute-start(bf16[32,40,256]{2,1,0:T(8,128)(2,1)S(1)} %slice.11), channel_id=1, source_target_pairs={{0,1},{1,0},{2,3},{3,2},{4,5},{5,4},{6,7},{7,6},{8,9},{9,8},{10,11... | collective-permute-start | bytes 1966088 | tf_op jit(solution)/shard_map/ppermute | solution.py:937
  42.8 21.9 %copy-start = (bf16[256,256]{1,0:T(8,128)(2,1)}, bf16[256,256]{1,0:T(8,128)(2,1)S(1)}, u32[]{:S(2)}) copy-start(bf16[256,256]{1,0:T(8,128)(2,1)S(1)} %slice_bitcast_fusion.refs_0_) | copy-start | bytes 393220
  42.8 9.4 %collective-permute-start = (bf16[256,256]{1,0:T(8,128)(2,1)S(1)}, bf16[256,256]{1,0:T(8,128)(2,1)S(1)}, u32[]{:S(2)}, u32[]{:S(2)}) collective-permute-start(bf16[256,256]{1,0:T(8,128)(2,1)S(1)} %slice_bitcast_fusion.refs_0_), channel_id=1, source_target_pairs={{0,4},{1,5},{2,6},{3,7},{4,0},{5,1},{6,2},{7,3},{8,12},{9,13},{10,... | collective-permute-start | bytes 393224 | tf_op jit(solution)/shard_map/ppermute | solution.py:937
  52.2 25.2 %copy-start.1 = (bf16[256,256]{1,0:T(8,128)(2,1)}, bf16[256,256]{1,0:T(8,128)(2,1)S(1)}, u32[]{:S(2)}) copy-start(bf16[256,256]{1,0:T(8,128)(2,1)S(1)} %collective-permute-done.refs_4_) | copy-start | bytes 393220
  56.6 31.7 %all-to-all-start.1 = ((bf16[32,32,256]{2,1,0:T(8,128)(2,1)}), bf16[32,32,256]{2,1,0:T(8,128)(2,1)S(1)}, u32[]{:S(2)}, u32[]{:S(2)}) async-start(bf16[32,32,256]{2,1,0:T(8,128)(2,1)} %get-tuple-element.25), calls=%async_computation.1 | async-start | bytes 1048576 | tf_op jit(solution)/shard_map/all_to_all | solution.py:960
  62.7 10.3 %collective-permute-start.3 = (bf16[256,256]{1,0:T(8,128)(2,1)S(1)}, bf16[256,256]{1,0:T(8,128)(2,1)S(1)}, u32[]{:S(2)}, u32[]{:S(2)}) collective-permute-start(bf16[256,256]{1,0:T(8,128)(2,1)S(1)} %slice_bitcast_fusion.refs_0_), channel_id=1, source_target_pairs={{0,2},{1,3},{2,0},{3,1},{4,6},{5,7},{6,4},{7,5},{8,10},{9,11},{10,... | collective-permute-start | bytes 393224 | tf_op jit(solution)/shard_map/ppermute | solution.py:937
  64.3 11.8 %collective-permute-start.6 = (bf16[256,256]{1,0:T(8,128)(2,1)S(1)}, bf16[256,256]{1,0:T(8,128)(2,1)S(1)}, u32[]{:S(2)}, u32[]{:S(2)}) collective-permute-start(bf16[256,256]{1,0:T(8,128)(2,1)S(1)} %collective-permute-done.refs_4_), channel_id=1, source_target_pairs={{0,2},{1,3},{2,0},{3,1},{4,6},{5,7},{6,4},{7,5},{8,10},{9,11},{10,... | collective-permute-start | bytes 393224 | tf_op jit(solution)/shard_map/ppermute | solution.py:937
  64.8 11.4 %collective-permute-start.2 = (bf16[256,256]{1,0:T(8,128)(2,1)S(1)}, bf16[256,256]{1,0:T(8,128)(2,1)S(1)}, u32[]{:S(2)}, u32[]{:S(2)}) collective-permute-start(bf16[256,256]{1,0:T(8,128)(2,1)S(1)} %slice_bitcast_fusion.refs_0_), channel_id=1, source_target_pairs={{0,1},{1,0},{2,3},{3,2},{4,5},{5,4},{6,7},{7,6},{8,9},{9,8},{10,11... | collective-permute-start | bytes 393224 | tf_op jit(solution)/shard_map/ppermute | solution.py:937
  64.8 11.4 %collective-permute-start.5 = (bf16[256,256]{1,0:T(8,128)(2,1)S(1)}, bf16[256,256]{1,0:T(8,128)(2,1)S(1)}, u32[]{:S(2)}, u32[]{:S(2)}) collective-permute-start(bf16[256,256]{1,0:T(8,128)(2,1)S(1)} %collective-permute-done.refs_4_), channel_id=1, source_target_pairs={{0,1},{1,0},{2,3},{3,2},{4,5},{5,4},{6,7},{7,6},{8,9},{9,8},{10,11... | collective-permute-start | bytes 393224 | tf_op jit(solution)/shard_map/ppermute | solution.py:937
  73.0 4.5 %copy-start.2 = (bf16[256,256]{1,0:T(8,128)(2,1)}, bf16[256,256]{1,0:T(8,128)(2,1)S(1)}, u32[]{:S(2)}) copy-start(bf16[256,256]{1,0:T(8,128)(2,1)S(1)} %collective-permute-done.3.refs_2_) | copy-start | bytes 393220
  73.0 3.2 %collective-permute-start.4 = (bf16[256,256]{1,0:T(8,128)(2,1)S(1)}, bf16[256,256]{1,0:T(8,128)(2,1)S(1)}, u32[]{:S(2)}, u32[]{:S(2)}) collective-permute-start(bf16[256,256]{1,0:T(8,128)(2,1)S(1)} %collective-permute-done.3.refs_2_), channel_id=1, source_target_pairs={{0,1},{1,0},{2,3},{3,2},{4,5},{5,4},{6,7},{7,6},{8,9},{9,8},{10,11... | collective-permute-start | bytes 393224 | tf_op jit(solution)/shard_map/ppermute | solution.py:937
  76.1 1.4 %copy-start.3 = (bf16[256,256]{1,0:T(8,128)(2,1)}, bf16[256,256]{1,0:T(8,128)(2,1)S(1)}, u32[]{:S(2)}) copy-start(bf16[256,256]{1,0:T(8,128)(2,1)S(1)} %collective-permute-done.6.refs_6_) | copy-start | bytes 393220
  76.1 1.3 %collective-permute-start.7 = (bf16[256,256]{1,0:T(8,128)(2,1)S(1)}, bf16[256,256]{1,0:T(8,128)(2,1)S(1)}, u32[]{:S(2)}, u32[]{:S(2)}) collective-permute-start(bf16[256,256]{1,0:T(8,128)(2,1)S(1)} %collective-permute-done.6.refs_6_), channel_id=1, source_target_pairs={{0,1},{1,0},{2,3},{3,2},{4,5},{5,4},{6,7},{7,6},{8,9},{9,8},{10,11... | collective-permute-start | bytes 393224 | tf_op jit(solution)/shard_map/ppermute | solution.py:937
  76.1 1.4 %copy-start.4 = (bf16[256,256]{1,0:T(8,128)(2,1)}, bf16[256,256]{1,0:T(8,128)(2,1)S(1)}, u32[]{:S(2)}) copy-start(bf16[256,256]{1,0:T(8,128)(2,1)S(1)} %collective-permute-done.2.refs_1_) | copy-start | bytes 393220
  76.1 1.3 %copy-start.5 = (bf16[256,256]{1,0:T(8,128)(2,1)}, bf16[256,256]{1,0:T(8,128)(2,1)S(1)}, u32[]{:S(2)}) copy-start(bf16[256,256]{1,0:T(8,128)(2,1)S(1)} %collective-permute-done.5.refs_5_) | copy-start | bytes 393220
  76.2 1.3 %copy-start.6 = (bf16[256,256]{1,0:T(8,128)(2,1)}, bf16[256,256]{1,0:T(8,128)(2,1)S(1)}, u32[]{:S(2)}) copy-start(bf16[256,256]{1,0:T(8,128)(2,1)S(1)} %collective-permute-done.4.refs_3_) | copy-start | bytes 393220
  77.5 0.7 copy-start.7

commit v6 on v5

--- a/solution.py
+++ b/solution.py
@@ -209,6 +209,10 @@
     )(counts, table, pooled, degree)
 
 
+def in_vmem(array):
+    return pltpu.with_memory_space_constraint(array, pltpu.VMEM)
+
+
 def in_hbm(*arrays):
     return [pltpu.with_memory_space_constraint(array, pltpu.HBM) for array in arrays]
 
@@ -227,7 +231,7 @@
 
 def build_body(
     tile_ref, count_ref, source_hbm, relation_hbm, target_hbm, own_hbm,
-    local_ref, remote_ref, pooled_ref, degree_hbm,
+    local_ref, remote_ref, pooled_ref, degree_hbm, ahead_ref,
     source_ref, relation_ref, target_ref, own_ref, degree_ref,
     local_v, remote_v, pooled_v, head_ref, next_ref, list_ref, slot_ref, code_ref, low_ref, sum_ref,
     sems, in_sems, *, tiles, relations, locals_, pieces,
@@ -383,6 +387,7 @@
         return carry
 
     lax.fori_loop(0, tiles // GROUP, pool_own, 0)
+    ahead_ref[...] = remote_v[: GROUP * slots, :]
     every = pl.ds(0, tiles * slots)
     pltpu.make_async_copy(local_v.at[every], local_ref, sems.at[0]).wait()
     pltpu.make_async_copy(remote_v.at[every], remote_ref, sems.at[1]).wait()
@@ -409,9 +414,10 @@
             pltpu.HBM((rows, remote_rows), jnp.bfloat16),
             pltpu.HBM((rows, width), jnp.bfloat16),
             pltpu.HBM((tiles // GROUP, slots, GROUP), jnp.float32),
+            pltpu.VMEM((GROUP * slots, remote_rows), jnp.bfloat16),
         ],
         in_specs=[smem, smem] + [hbm] * 4,
-        out_specs=[hbm] * 4,
+        out_specs=[hbm] * 4 + [pl.BlockSpec(memory_space=pltpu.VMEM)],
         scratch_shapes=[
             pltpu.VMEM((blocks, block_width), jnp.int32),
             pltpu.VMEM((blocks, block_width), jnp.int32),
@@ -442,40 +448,51 @@
 
 
 def pool_groups(
-    counts_ref, counts_v, sems, table_ref, degree_ref, mean_ref, relations, begun, extra=None
+    counts_ref, counts_v, sems, table_ref, degree_ref, mean_ref, relations, begun, extra=None, ahead=None
 ):
-    size = GROUP * WIN * relations
+    slots = WIN * relations
+    size = GROUP * slots
     groups = counts_ref.shape[0] // size
-
-    def copies(i):
-        some = pl.ds(pl.multiple_of(i * size, size), size)
-        found = [pltpu.make_async_copy(counts_ref.at[some], counts_v.at[some], sems.at[0, i])]
+    held = 0 if ahead is None else 1
+
+    def rows(i):
+        return pl.ds(pl.multiple_of(i * size, size), size)
+
+    def count_copy(i):
+        return pltpu.make_async_copy(counts_ref.at[rows(i)], counts_v.at[rows(i)], sems.at[0, i])
+
+    def extra_copy(i):
+        return pltpu.make_async_copy(extra[0].at[rows(i)], extra[1].at[rows(i)], sems.at[1, i])
+
+    def begin(i, carry):
+        count_copy(i).start()
         if extra is not None:
-            found.append(pltpu.make_async_copy(extra[0].at[some], extra[1].at[some], sems.at[1, i]))
-        return found
-
-    def begin(i, carry):
-        for copy in copies(i):
-            copy.start()
+            extra_copy(i).start()
         return carry
 
-    def step(i, carry):
-        for copy in copies(i):
-            copy.wait()
-        some = pl.ds(pl.multiple_of(i * size, size), size)
-        total = jnp.dot(counts_v[some, :], table_ref[...], preferred_element_type=jnp.float32)
+    def finish(i, total):
         if extra is not None:
-            total += extra[1][some, :].astype(jnp.float32)
+            extra_copy(i).wait()
+            total += extra[1][rows(i), :].astype(jnp.float32)
         share = 1.0 / jnp.maximum(degree_ref[i], 1.0)
-        slots = WIN * relations
         for u in range(GROUP):
             mean = total[u * slots : (u + 1) * slots] * share[:, u : u + 1]
             put_means(mean.astype(jnp.bfloat16), mean_ref, i * GROUP + u, relations)
+
+    def step(i, carry):
+        count_copy(i).wait()
+        finish(
+            i, jnp.dot(counts_v[rows(i), :], table_ref[...], preferred_element_type=jnp.float32)
+        )
         return carry
 
-    lax.fori_loop(0, groups, begin, 0)
+    if held and extra is not None:
+        extra_copy(0).start()
+    lax.fori_loop(held, groups, begin, 0)
     begun()
-    lax.fori_loop(0, groups, step, 0)
+    if held:
+        finish(0, jnp.dot(ahead[...], table_ref[...], preferred_element_type=jnp.float32))
+    lax.fori_loop(held, groups, step, 0)
 
 
 def copy_table(incoming_ref, table_ref, slot):
@@ -484,7 +501,7 @@
 
 
 def pool_body(
-    counts_ref, pooled_ref, incoming_ref, degree_hbm, mean_ref,
+    counts_ref, pooled_ref, incoming_ref, degree_hbm, ahead_ref, mean_ref,
     counts_v, pooled_v, table_v, degree_v, sems, in_sems, *, relations, slot,
 ):
     inputs = start_all(in_sems, (degree_hbm, degree_v))
@@ -495,11 +512,11 @@
 
     pool_groups(
         counts_ref, counts_v, sems, table_v, degree_v, mean_ref, relations, begun,
-        extra=(pooled_ref, pooled_v),
-    )
-
-
-def pool(counts, pooled, incoming, degree, *, relations, slot):
+        extra=(pooled_ref, pooled_v), ahead=ahead_ref,
+    )
+
+
+def pool(counts, pooled, incoming, degree, ahead, *, relations, slot):
     rows, depth = counts.shape
     width = incoming.shape[2]
     vmem = pl.BlockSpec(memory_space=pltpu.VMEM)
@@ -507,7 +524,7 @@
     return pl.pallas_call(
         functools.partial(pool_body, relations=relations, slot=slot),
         out_shape=jax.ShapeDtypeStruct((rows // relations, relations * width), jnp.bfloat16),
-        in_specs=[hbm, hbm, vmem, hbm],
+        in_specs=[hbm, hbm, vmem, hbm, vmem],
         out_specs=vmem,
         scratch_shapes=[
             pltpu.VMEM(counts.shape, counts.dtype),
@@ -520,7 +537,7 @@
         compiler_params=params(44),
         cost_estimate=estimate(2 * rows * depth * width, 2 * rows * depth),
         name="pool",
-    )(*in_hbm(counts, pooled), incoming, *in_hbm(degree))
+    )(*in_hbm(counts, pooled), incoming, *in_hbm(degree), in_vmem(ahead))
 
 
 def pick_rows(send_ref, rows_ref, emit, done):
@@ -649,17 +666,19 @@
 
 
 def first_body(
-    counts_ref, own_hbm, degree_hbm, self_hbm, bias_hbm, *refs, relations
+    counts_ref, remote_ref, own_hbm, degree_hbm, self_hbm, bias_hbm, *refs, relations
 ):
     pieces, refs = refs[:relations], refs[relations:]
-    out_hbm, own_v, degree_v, self_v, bias_v, out_v, weights_v, counts_v, mean_v, sems, in_sems = refs
+    out_hbm, ahead_ref, *refs = refs
+    own_v, degree_v, self_v, bias_v, out_v, weights_v, counts_v, mean_v, sems, in_sems = refs
     inputs = start_all(in_sems, (own_hbm, own_v), (degree_hbm, degree_v))
     later = []
 
     def begun():
         later.extend(
             start_all(
-                in_sems.at[pl.ds(2, 2 + relations)],
+                in_sems.at[pl.ds(2, 3 + relations)],
+                (remote_ref.at[pl.ds(0, ahead_ref.shape[0])], ahead_ref),
                 (self_hbm, self_v),
                 (bias_hbm, bias_v),
                 *weight_copies(pieces, weights_v, relations),
@@ -675,15 +694,18 @@
     pltpu.sync_copy(out_v, out_hbm)
 
 
-def first(counts, own, degree, self_weight, bias, pieces, *, relations):
+def first(counts, remote, own, degree, self_weight, bias, pieces, *, relations):
     rows, depth = counts.shape
     nodes, width = own.shape
     hbm = pl.BlockSpec(memory_space=pltpu.HBM)
     return pl.pallas_call(
         functools.partial(first_body, relations=relations),
-        out_shape=pltpu.HBM((nodes, width), jnp.float32),
-        in_specs=[hbm] * (5 + relations),
-        out_specs=hbm,
+        out_shape=[
+            pltpu.HBM((nodes, width), jnp.float32),
+            pltpu.VMEM((GROUP * WIN * relations, remote.shape[1]), jnp.bfloat16),
+        ],
+        in_specs=[hbm] * (6 + relations),
+        out_specs=[hbm, pl.BlockSpec(memory_space=pltpu.VMEM)],
         scratch_shapes=[
             pltpu.VMEM(own.shape, own.dtype),
             pltpu.VMEM(degree.shape, degree.dtype),
@@ -694,17 +716,17 @@
             pltpu.VMEM(counts.shape, counts.dtype),
             pltpu.VMEM((nodes, relations * width), jnp.bfloat16),
             pltpu.SemaphoreType.DMA((1, degree.shape[0])),
-            pltpu.SemaphoreType.DMA((4 + relations,)),
+            pltpu.SemaphoreType.DMA((5 + relations,)),
         ],
         compiler_params=params(44),
         cost_estimate=estimate(
             2 * rows * depth * width + 2 * nodes * relations * width * width, 2 * rows * depth
         ),
         name="first",
-    )(*in_hbm(counts, own, degree, self_weight, bias, *pieces))
-
-
-def last_body(counts_ref, table_ref, degree_hbm, partial_hbm, *refs, relations):
+    )(*in_hbm(counts, remote, own, degree, self_weight, bias, *pieces))
+
+
+def last_body(counts_ref, table_ref, ahead_ref, degree_hbm, partial_hbm, *refs, relations):
     pieces, refs = refs[:relations], refs[relations:]
     out_ref, degree_v, partial_v, weights_v, counts_v, mean_v, sems, in_sems = refs
     inputs = start_all(in_sems, (degree_hbm, degree_v))
@@ -720,13 +742,15 @@
         )
         wait_all(inputs)
 
-    pool_groups(counts_ref, counts_v, sems, table_ref, degree_v, mean_v, relations, begun)
+    pool_groups(
+        counts_ref, counts_v, sems, table_ref, degree_v, mean_v, relations, begun, ahead=ahead_ref
+    )
     wait_all(later)
     total = jnp.dot(mean_v[...], weights_v[...], preferred_element_type=jnp.float32)
     out_ref[...] = (total + partial_v[...]).astype(out_ref.dtype)
 
 
-def last(counts, table, degree, partial, pieces, *, relations):
+def last(counts, table, ahead, degree, partial, pieces, *, relations):
     rows, depth = counts.shape
     width = table.shape[1]
     nodes = rows // relations
@@ -735,7 +759,7 @@
     return pl.pallas_call(
         functools.partial(last_body, relations=relations),
         out_shape=jax.ShapeDtypeStruct((nodes, width), jnp.bfloat16),
-        in_specs=[hbm, vmem] + [hbm] * (2 + relations),
+        in_specs=[hbm, vmem, vmem] + [hbm] * (2 + relations),
         out_specs=vmem,
         scratch_shapes=[
             pltpu.VMEM(degree.shape, degree.dtype),
@@ -751,7 +775,7 @@
             2 * rows * depth * width + 2 * nodes * relations * width * width, 2 * rows * depth
         ),
         name="last",
-    )(*in_hbm(counts), table, *in_hbm(degree, partial, *pieces))
+    )(*in_hbm(counts), table, in_vmem(ahead), *in_hbm(degree, partial, *pieces))
 
 
 def pack_body(*refs):
@@ -928,7 +952,7 @@
         features, send, bases_first, self_first, coef_first, bases_second, self_second, coef_second
     )
     incoming = lax.all_to_all(outgoing, "dom", split_axis=0, concat_axis=0, tiled=True)
-    local, remote, pooled, degree = build(
+    local, remote, pooled, degree, ahead = build(
         *edges, features, relations=relations, remote_rows=remote_rows
     )
     incoming, degree = lax.optimization_barrier((incoming, degree))
@@ -950,7 +974,7 @@
 
     mask = relations // EACH // 2
     widen(mask)
-    mean = pool(remote, pooled, incoming, degree, relations=relations, slot=slot)
+    mean = pool(remote, pooled, incoming, degree, ahead, relations=relations, slot=slot)
     pieces, mean = lax.optimization_barrier((pieces, mean))
     mask //= 2
     widen(mask)
@@ -962,11 +986,13 @@
         mask //= 2
         widen(mask)
     pieces = [piece for _, piece in sorted(pieces.items())]
-    partial = first(
-        local, hidden, degree, self_next, bias_second[None], pieces, relations=relations
+    partial, ahead = first(
+        local, remote, hidden, degree, self_next, bias_second[None], pieces, relations=relations
     )
     table, partial = lax.optimization_barrier((table, partial))
-    return last(remote, table.reshape(-1, width), degree, partial, pieces, relations=relations)
+    return last(
+        remote, table.reshape(-1, width), ahead, degree, partial, pieces, relations=relations
+    )
 
 
 def solution(mesh):

time: 98.5 us -> 98.1 us (level)
  no operation moved by 1% of the time
where the time goes in v6:
time: 98.1 us; the launch traced here: 97.7 us
  Pallas kernels  62 us (63%)
  starting transfers between devices  17.5 us (18%)
  waiting for transfers between devices  15.9 us (16%)
  local copies, waits for them, and re-layouts  1.33 us (1%)
  between operations  1.01 us (1%)
    pallas_call x1, Pallas kernels, build(): pl.pallas_call(functools.partial(build_body, tiles=tiles, relations=relat...  26.9 us
    ppermute x8, waiting for transfers between devices, from_peer(): return lax.ppermute(array, 'dom', [(i, i ^ mask) for i in range(devices)])  12.1 us
    pallas_call x1, Pallas kernels, first(): pl.pallas_call(functools.partial(first_body, relations=relations), out_sh...  10.2 us
    pallas_call x1, Pallas kernels, last(): pl.pallas_call(functools.partial(last_body, relations=relations), out_sha...  8.97 us
    pallas_call x1, Pallas kernels, pool(): pl.pallas_call(functools.partial(pool_body, relations=relations, slot=slo...  8.2 us
    all_to_all x1, starting transfers between devices, shards(): lax.all_to_all(outgoing, 'dom', split_axis=0, concat_axis=0, tiled=True)  7.33 us
    all_to_all x1, starting transfers between devices, shards(): lax.all_to_all(picked, 'dom', split_axis=0, concat_axis=0, tiled=True)  6.06 us
    pallas_call x1, Pallas kernels, middle(): pl.pallas_call(functools.partial(middle_body, relations=relations, slot=s...  4.32 us
  transfers between devices with their start and end apart: 10, of which 4 were waited for; matrix products, arithmetic and copies ran while one was open for 1% of the time, Pallas kernels for 46%

profile of v6, /device:TPU:0, one launch (start us, length us, event | category | flops | bytes accessed | tf_op | source)
XLA Modules:
  0.0 97.7 jit_solution(9257465587310444682)
XLA Ops:
  0.0 3.4 %pack.1 = bf16[32,80,256]{2,1,0:T(8,128)(2,1)} custom-call(f32[8,30]{1,0:T(8,128)} %refs_0_.1, f32[8,30]{1,0:T(8,128)} %refs_1_.1, bf16[30,8,256]{2,1,0:T(8,128)(2,1)} %refs_2_.1, bf16[30,8,256]{2,1,0:T(8,128)(2,1)} %refs_3_.1, bf16[8,256]{1,0:T(8,128)(2,1)} %refs_4_.1, bf16[8,256]{1,0:T(8,128)(2,1)} %refs_5_.1, bf16[1024,256]{1,0:T(8,128)(2,1)} %own_hbm.3, ...), custom_call_target="tpu_custom_call" | custom-call | flops 536870912 | tf_op jit(solution)/shard_map/pack/pallas_call | solution.py:829
  3.4 7.3 %all-to-all-start = ((bf16[32,80,256]{2,1,0:T(8,128)(2,1)}), bf16[32,80,256]{2,1,0:T(8,128)(2,1)S(1)}, u32[]{:S(2)}, u32[]{:S(2)}) async-start(bf16[32,80,256]{2,1,0:T(8,128)(2,1)} %pack.1), calls=%async_computation | async-start | bytes 2621440 | tf_op jit(solution)/shard_map/all_to_all | solution.py:954
  11.4 0.0 copy-done.8
  11.4 0.6 slice_reduce_fusion.tile_ref
  12.0 26.9 %build.1 = (bf16[8192,1024]{1,0:T(8,128)(2,1)}, bf16[8192,1024]{1,0:T(8,128)(2,1)}, bf16[8192,256]{1,0:T(8,128)(2,1)}, f32[8,128,8]{2,1,0:T(8,128)}, bf16[1024,1024]{1,0:T(8,128)(2,1)S(1)}) custom-call(s32[128]{0:T(128)} %slice_reduce_fusion.tile_ref, s32[1]{0:T(128)S(6)} %copy.15.count_ref, s32[128,128]{1,0:T(8,128)} %bitcast.15, s32[128,128]{1,0:T(8,128)} %bitcast.16, ...), custom_call_target="tpu_custom_call" | custom-call | flops 17179869184 | bytes 33554432 | tf_op jit(solution)/shard_map/build/pallas_call | solution.py:408
  38.9 3.8 %all-to-all-done.incoming_ref = bf16[32,80,256]{2,1,0:T(8,128)(2,1)S(1)} async-done(((bf16[32,80,256]{2,1,0:T(8,128)(2,1)}), bf16[32,80,256]{2,1,0:T(8,128)(2,1)S(1)}, u32[]{:S(2)}, u32[]{:S(2)}) %all-to-all-start) | async-done | bytes 1310752 | tf_op jit(solution)/shard_map/all_to_all | solution.py:954
  42.7 0.1 collective-permute-start.1
  42.8 1.4 %collective-permute-start = (bf16[256,256]{1,0:T(8,128)(2,1)S(1)}, bf16[256,256]{1,0:T(8,128)(2,1)S(1)}, u32[]{:S(2)}, u32[]{:S(2)}) collective-permute-start(bf16[256,256]{1,0:T(8,128)(2,1)S(1)} %slice_bitcast_fusion.refs_0_), channel_id=1, source_target_pairs={{0,4},{1,5},{2,6},{3,7},{4,0},{5,1},{6,2},{7,3},{8,12},{9,13},{10,... | collective-permute-start | bytes 393224 | tf_op jit(solution)/shard_map/ppermute | solution.py:961
  44.3 8.2 %pool.1.mean_ref = bf16[1024,2048]{1,0:T(8,128)(2,1)S(1)} custom-call(bf16[8192,1024]{1,0:T(8,128)(2,1)} %get-tuple-element.22.counts_ref.remote_ref, bf16[8192,256]{1,0:T(8,128)(2,1)} %get-tuple-element.25.pooled_ref, bf16[32,80,256]{2,1,0:T(8,128)(2,1)S(1)} %all-to-all-done.incoming_ref, f32[8,128,8]{2,1,0:T(8,128)} %get-tuple-element.26.degree_hbm, ...), custom_call_target="tpu_custom_call" | custom-call | flops 4294967296 | bytes 16777216 | tf_op jit(solution)/shard_map/pool/pallas_call | solution.py:524
  52.5 0.0 collective-permute-done.refs_4_
  52.5 0.0 collective-permute-done.1.swapped_ref
  52.5 4.3 %middle.1 = (bf16[1024,256]{1,0:T(8,128)(2,1)}, bf16[32,32,256]{2,1,0:T(8,128)(2,1)}, bf16[256,256]{1,0:T(8,128)(2,1)}) custom-call(bf16[1024,2048]{1,0:T(8,128)(2,1)S(1)} %pool.1.mean_ref, bf16[1024,256]{1,0:T(8,128)(2,1)} %own_hbm.3, bf16[32,80,256]{2,1,0:T(8,128)(2,1)S(1)} %all-to-all-done.incoming_ref, ...), custom_call_target="tpu_custom_call" | custom-call | flops 1073741824 | tf_op jit(solution)/shard_map/middle/pallas_call | solution.py:630
  56.9 6.1 %all-to-all-start.1 = ((bf16[32,32,256]{2,1,0:T(8,128)(2,1)}), bf16[32,32,256]{2,1,0:T(8,128)(2,1)S(1)}, u32[]{:S(2)}, u32[]{:S(2)}) async-start(bf16[32,32,256]{2,1,0:T(8,128)(2,1)} %get-tuple-element.29), calls=%async_computation.1 | async-start | bytes 1048576 | tf_op jit(solution)/shard_map/all_to_all | solution.py:984
  62.9 1.7 %collective-permute-start.3 = (bf16[256,256]{1,0:T(8,128)(2,1)S(1)}, bf16[256,256]{1,0:T(8,128)(2,1)S(1)}, u32[]{:S(2)}, u32[]{:S(2)}) collective-permute-start(bf16[256,256]{1,0:T(8,128)(2,1)S(1)} %slice_bitcast_fusion.refs_0_), channel_id=1, source_target_pairs={{0,2},{1,3},{2,0},{3,1},{4,6},{5,7},{6,4},{7,5},{8,10},{9,11},{10,... | collective-permute-start | bytes 393224 | tf_op jit(solution)/shard_map/ppermute | solution.py:961
  64.6 0.4 collective-permute-start.6
  65.0 0.0 collective-permute-start.2
  65.0 0.5 collective-permute-start.5
  65.5 7.7 %collective-permute-done.3.refs_2_ = bf16[256,256]{1,0:T(8,128)(2,1)S(1)} collective-permute-done((bf16[256,256]{1,0:T(8,128)(2,1)S(1)}, bf16[256,256]{1,0:T(8,128)(2,1)S(1)}, u32[]{:S(2)}, u32[]{:S(2)}) %collective-permute-start.3) | collective-permute-done | bytes 131104 | tf_op jit(solution)/shard_map/ppermute | solution.py:961
  73.2 0.0 collective-permute-start.4
  73.2 3.1 %collective-permute-done.6.refs_6_ = bf16[256,256]{1,0:T(8,128)(2,1)S(1)} collective-permute-done((bf16[256,256]{1,0:T(8,128)(2,1)}, bf16[256,256]{1,0:T(8,128)(2,1)S(1)}, u32[]{:S(2)}, u32[]{:S(2)}) %collective-permute-start.6) | collective-permute-done | bytes 131104 | tf_op jit(solution)/shard_map/ppermute | solution.py:961
  76.4 0.0 collective-permute-start.7
  76.4 0.0 collective-permute-done.2.refs_1_
  76.4 0.0 collective-permute-done.5.refs_5_
  76.4 0.0 collective-permute-done.4.refs_3_
  76.4 1.3 %collective-permute-done.7.refs_7_ = bf16[256,256]{1,0:T(8,128)(2,1)S(1)} collective-permute-done((bf16[256,256]{1,0:T(8,128)(2,1)S(1)}, bf16[256,256]{1,0:T(8,128)(2,1)S(1)}, u32[]{:S(2)}, u32[]{:S(2)}) %collective-permute-start.7) | collective-permute-done | bytes 131104 | tf_op jit(solution)/shard_map/ppermute | solution.py:961
  77.7 0.0 copy-done.3
  77.7 0.0 copy-done.5
  77.7 0.0 copy-done.6
  77.8 0.6 copy-done.7
  78.4 10.2 %first.1 = (f32[1024,256]{1,0:T(8,128)}, bf16[1024,1024]{1,0:T(8,128)(2,1)S(1)}) custom-call(bf16[8192,1024]{1,0:T(8,128)(2,1)} %get-tuple-element.30.counts_ref, bf16[8192,1024]{1,0:T(8,128)(2,1)} %get-tuple-element.22.counts_ref.remote_ref, bf16[1024,256]{1,0:T(8,128)(2,1)} %get-tuple-element.31.own_hbm, f32[8,128,8]{2,1,0:T(8,128)} %get-tuple-element.26.degree_hbm, ...), custom_call_target="tpu_custom_call" | custom-call | flops 5368709120 | bytes 16777216 | tf_op jit(solution)/shard_map/first/pallas_call | solution.py:701
  88.6 0.0 all-to-all-done.1
  88.6 9.0 %last.1 = bf16[1024,256]{1,0:T(8,128)(2,1)} custom-call(bf16[8192,1024]{1,0:T(8,128)(2,1)} %get-tuple-element.22.counts_ref.remote_ref, bf16[1024,256]{1,0:T(8,128)(2,1)S(1)} %bitcast.9, bf16[1024,1024]{1,0:T(8,128)(2,1)S(1)} %get-tuple-element.37.ahead_ref, f32[8,128,8]{2,1,0:T(8,128)} %get-tuple-element.26.degree_hbm, ...), custom_call_target="tpu_custom_call" | custom-call | flops 5368709120 | bytes 16777216 | tf_op jit(solution)/shard_map/last/pallas_call | solution.py:759
  (15 shorter events, 0.1 us)
Async XLA Ops:
  0.0 11.4 %copy-start.8 = (s32[1,128,128]{2,1,0:T(8,128)S(1)}, s32[1,128,128]{2,1,0:T(8,128)}, u32[]{:S(2)}) copy-start(s32[1,128,128]{2,1,0:T(8,128)} %param.17) | copy-start | bytes 196612
  3.4 39.3 %all-to-all-start = ((bf16[32,80,256]{2,1,0:T(8,128)(2,1)}), bf16[32,80,256]{2,1,0:T(8,128)(2,1)S(1)}, u32[]{:S(2)}, u32[]{:S(2)}) async-start(bf16[32,80,256]{2,1,0:T(8,128)(2,1)} %pack.1), calls=%async_computation | async-start | bytes 2621440 | tf_op jit(solution)/shard_map/all_to_all | solution.py:954
  42.7 9.8 %collective-permute-start.1 = (bf16[32,40,256]{2,1,0:T(8,128)(2,1)S(1)}, bf16[32,40,256]{2,1,0:T(8,128)(2,1)S(1)}, u32[]{:S(2)}, u32[]{:S(2)}) collective-permute-start(bf16[32,40,256]{2,1,0:T(8,128)(2,1)S(1)} %slice.11), channel_id=1, source_target_pairs={{0,1},{1,0},{2,3},{3,2},{4,5},{5,4},{6,7},{7,6},{8,9},{9,8},{10,11... | collective-permute-start | bytes 1966088 | tf_op jit(solution)/shard_map/ppermute | solution.py:961
  42.8 22.2 %copy-start = (bf16[256,256]{1,0:T(8,128)(2,1)}, bf16[256,256]{1,0:T(8,128)(2,1)S(1)}, u32[]{:S(2)}) copy-start(bf16[256,256]{1,0:T(8,128)(2,1)S(1)} %slice_bitcast_fusion.refs_0_) | copy-start | bytes 393220
  42.8 9.6 %collective-permute-start = (bf16[256,256]{1,0:T(8,128)(2,1)S(1)}, bf16[256,256]{1,0:T(8,128)(2,1)S(1)}, u32[]{:S(2)}, u32[]{:S(2)}) collective-permute-start(bf16[256,256]{1,0:T(8,128)(2,1)S(1)} %slice_bitcast_fusion.refs_0_), channel_id=1, source_target_pairs={{0,4},{1,5},{2,6},{3,7},{4,0},{5,1},{6,2},{7,3},{8,12},{9,13},{10,... | collective-permute-start | bytes 393224 | tf_op jit(solution)/shard_map/ppermute | solution.py:961
  52.5 4.4 %copy-start.1 = (bf16[256,256]{1,0:T(8,128)(2,1)}, bf16[256,256]{1,0:T(8,128)(2,1)S(1)}, u32[]{:S(2)}) copy-start(bf16[256,256]{1,0:T(8,128)(2,1)S(1)} %collective-permute-done.refs_4_) | copy-start | bytes 393220
  56.9 31.7 %all-to-all-start.1 = ((bf16[32,32,256]{2,1,0:T(8,128)(2,1)}), bf16[32,32,256]{2,1,0:T(8,128)(2,1)S(1)}, u32[]{:S(2)}, u32[]{:S(2)}) async-start(bf16[32,32,256]{2,1,0:T(8,128)(2,1)} %get-tuple-element.29), calls=%async_computation.1 | async-start | bytes 1048576 | tf_op jit(solution)/shard_map/all_to_all | solution.py:984
  62.9 10.3 %collective-permute-start.3 = (bf16[256,256]{1,0:T(8,128)(2,1)S(1)}, bf16[256,256]{1,0:T(8,128)(2,1)S(1)}, u32[]{:S(2)}, u32[]{:S(2)}) collective-permute-start(bf16[256,256]{1,0:T(8,128)(2,1)S(1)} %slice_bitcast_fusion.refs_0_), channel_id=1, source_target_pairs={{0,2},{1,3},{2,0},{3,1},{4,6},{5,7},{6,4},{7,5},{8,10},{9,11},{10,... | collective-permute-start | bytes 393224 | tf_op jit(solution)/shard_map/ppermute | solution.py:961
  64.6 11.8 %collective-permute-start.6 = (bf16[256,256]{1,0:T(8,128)(2,1)}, bf16[256,256]{1,0:T(8,128)(2,1)S(1)}, u32[]{:S(2)}, u32[]{:S(2)}) collective-permute-start(bf16[256,256]{1,0:T(8,128)(2,1)} %copy-done.1), channel_id=1, source_target_pairs={{0,2},{1,3},{2,0},{3,1},{4,6},{5,7},{6,4},{7,5},{8,10},{9,11},{10,... | collective-permute-start | bytes 393224 | tf_op jit(solution)/shard_map/ppermute | solution.py:961
  65.0 11.4 %collective-permute-start.2 = (bf16[256,256]{1,0:T(8,128)(2,1)S(1)}, bf16[256,256]{1,0:T(8,128)(2,1)S(1)}, u32[]{:S(2)}, u32[]{:S(2)}) collective-permute-start(bf16[256,256]{1,0:T(8,128)(2,1)S(1)} %slice_bitcast_fusion.refs_0_), channel_id=1, source_target_pairs={{0,1},{1,0},{2,3},{3,2},{4,5},{5,4},{6,7},{7,6},{8,9},{9,8},{10,11... | collective-permute-start | bytes 393224 | tf_op jit(solution)/shard_map/ppermute | solution.py:961
  65.0 11.4 %collective-permute-start.5 = (bf16[256,256]{1,0:T(8,128)(2,1)}, bf16[256,256]{1,0:T(8,128)(2,1)S(1)}, u32[]{:S(2)}, u32[]{:S(2)}) collective-permute-start(bf16[256,256]{1,0:T(8,128)(2,1)} %copy-done.1), channel_id=1, source_target_pairs={{0,1},{1,0},{2,3},{3,2},{4,5},{5,4},{6,7},{7,6},{8,9},{9,8},{10,11... | collective-permute-start | bytes 393224 | tf_op jit(solution)/shard_map/ppermute | solution.py:961
  73.2 4.5 %copy-start.2 = (bf16[256,256]{1,0:T(8,128)(2,1)}, bf16[256,256]{1,0:T(8,128)(2,1)S(1)}, u32[]{:S(2)}) copy-start(bf16[256,256]{1,0:T(8,128)(2,1)S(1)} %collective-permute-done.3.refs_2_) | copy-start | bytes 393220
  73.2 3.2 %collective-permute-start.4 = (bf16[256,256]{1,0:T(8,128)(2,1)S(1)}, bf16[256,256]{1,0:T(8,128)(2,1)S(1)}, u32[]{:S(2)}, u32[]{:S(2)}) collective-permute-start(bf16[256,256]{1,0:T(8,128)(2,1)S(1)} %collective-permute-done.3.refs_2_), channel_id=1, source_target_pairs={{0,1},{1,0},{2,3},{3,2},{4,5},{5,4},{6,7},{7,6},{8,9},{9,8},{10,11... | collective-permute-start | bytes 393224 | tf_op jit(solution)/shard_map/ppermute | solution.py:961
  76.4 1.4 %copy-start.3 = (bf16[256,256]{1,0:T(8,128)(2,1)}, bf16[256,256]{1,0:T(8,128)(2,1)S(1)}, u32[]{:S(2)}) copy-start(bf16[256,256]{1,0:T(8,128)(2,1)S(1)} %collective-permute-done.6.refs_6_) | copy-start | bytes 393220
  76.4 1.3 %collective-permute-start.7 = (bf16[256,256]{1,0:T(8,128)(2,1)S(1)}, bf16[256,256]{1,0:T(8,128)(2,1)S(1)}, u32[]{:S(2)}, u32[]{:S(2)}) collective-permute-start(bf16[256,256]{1,0:T(8,128)(2,1)S(1)} %collective-permute-done.6.refs_6_), channel_id=1, source_target_pairs={{0,1},{1,0},{2,3},{3,2},{4,5},{5,4},{6,7},{7,6},{8,9},{9,8},{10,11... | collective-permute-start | bytes 393224 | tf_op jit(solution)/shard_map/ppermute | solution.py:961
  76.4 1.3 %copy-start.4 = (bf16[256,256]{1,0:T(8,128)(2,1)}, bf16[256,256]{1,0:T(8,128)(2,1)S(1)}, u32[]{:S(2)}) copy-start(bf16[256,256]{1,0:T(8,128)(2,1)S(1)} %collective-permute-done.2.refs_1_) | copy-start | bytes 393220
  76.4 1.3 %copy-start.5 = (bf16[256,256]{1,0:T(8,128)(2,1)}, bf16[256,256]{1,0:T(8,128)(2,1)S(1)}, u32[]{:S(2)}) copy-start(bf16[256,256]{1,0:T(8,128)(2,1)S(1)} %collective-permute-done.5.refs_5_) | copy-start | bytes 393220
  76.4 1.3 %copy-start.6 = (bf16[256,256]{1,0:T(8,128)(2,1)}, bf16[256,256]{1,0:T(8,128)(2,1)S(1)}, u32[]{:S(2)}) copy-start(bf16[256,256]{1,0:T(8,128)(2,1)S(1)} %collective-permute-done.4.refs_3_) | copy-start | bytes 393220
  77.7 0.6 copy-start.7

commit v7 on v6

--- a/solution.py
+++ b/solution.py
@@ -231,7 +231,7 @@
 
 def build_body(
     tile_ref, count_ref, source_hbm, relation_hbm, target_hbm, own_hbm,
-    local_ref, remote_ref, pooled_ref, degree_hbm, ahead_ref,
+    local_ref, remote_ref, pooled_ref, degree_hbm,
     source_ref, relation_ref, target_ref, own_ref, degree_ref,
     local_v, remote_v, pooled_v, head_ref, next_ref, list_ref, slot_ref, code_ref, low_ref, sum_ref,
     sems, in_sems, *, tiles, relations, locals_, pieces,
@@ -387,7 +387,6 @@
         return carry
 
     lax.fori_loop(0, tiles // GROUP, pool_own, 0)
-    ahead_ref[...] = remote_v[: GROUP * slots, :]
     every = pl.ds(0, tiles * slots)
     pltpu.make_async_copy(local_v.at[every], local_ref, sems.at[0]).wait()
     pltpu.make_async_copy(remote_v.at[every], remote_ref, sems.at[1]).wait()
@@ -414,10 +413,9 @@
             pltpu.HBM((rows, remote_rows), jnp.bfloat16),
             pltpu.HBM((rows, width), jnp.bfloat16),
             pltpu.HBM((tiles // GROUP, slots, GROUP), jnp.float32),
-            pltpu.VMEM((GROUP * slots, remote_rows), jnp.bfloat16),
         ],
         in_specs=[smem, smem] + [hbm] * 4,
-        out_specs=[hbm] * 4 + [pl.BlockSpec(memory_space=pltpu.VMEM)],
+        out_specs=[hbm] * 4,
         scratch_shapes=[
             pltpu.VMEM((blocks, block_width), jnp.int32),
             pltpu.VMEM((blocks, block_width), jnp.int32),
@@ -501,7 +499,7 @@
 
 
 def pool_body(
-    counts_ref, pooled_ref, incoming_ref, degree_hbm, ahead_ref, mean_ref,
+    counts_ref, pooled_ref, incoming_ref, degree_hbm, mean_ref,
     counts_v, pooled_v, table_v, degree_v, sems, in_sems, *, relations, slot,
 ):
     inputs = start_all(in_sems, (degree_hbm, degree_v))
@@ -512,11 +510,11 @@
 
     pool_groups(
         counts_ref, counts_v, sems, table_v, degree_v, mean_ref, relations, begun,
-        extra=(pooled_ref, pooled_v), ahead=ahead_ref,
-    )
-
-
-def pool(counts, pooled, incoming, degree, ahead, *, relations, slot):
+        extra=(pooled_ref, pooled_v),
+    )
+
+
+def pool(counts, pooled, incoming, degree, *, relations, slot):
     rows, depth = counts.shape
     width = incoming.shape[2]
     vmem = pl.BlockSpec(memory_space=pltpu.VMEM)
@@ -524,7 +522,7 @@
     return pl.pallas_call(
         functools.partial(pool_body, relations=relations, slot=slot),
         out_shape=jax.ShapeDtypeStruct((rows // relations, relations * width), jnp.bfloat16),
-        in_specs=[hbm, hbm, vmem, hbm, vmem],
+        in_specs=[hbm, hbm, vmem, hbm],
         out_specs=vmem,
         scratch_shapes=[
             pltpu.VMEM(counts.shape, counts.dtype),
@@ -537,7 +535,7 @@
         compiler_params=params(44),
         cost_estimate=estimate(2 * rows * depth * width, 2 * rows * depth),
         name="pool",
-    )(*in_hbm(counts, pooled), incoming, *in_hbm(degree), in_vmem(ahead))
+    )(*in_hbm(counts, pooled), incoming, *in_hbm(degree))
 
 
 def pick_rows(send_ref, rows_ref, emit, done):
@@ -577,15 +575,11 @@
     devices = incoming_ref.shape[0]
     piece = width // devices
     block = (half + 1) * width
-    for device in range(devices):
-        for m in range(half + 1):
-            at = m * width + device * piece
-            weights_v[at : at + piece, :] = incoming_ref[
-                device, slot + m * piece : slot + (m + 1) * piece, :
-            ]
-            weights_v[block + at : block + at + piece, :] = swapped_ref[
-                device, m * piece : (m + 1) * piece, :
-            ]
+    for m in range(half + 1):
+        mine = incoming_ref[:, slot + m * piece : slot + (m + 1) * piece, :]
+        weights_v[m * width : (m + 1) * width, :] = mine.reshape(width, width)
+        other = swapped_ref[:, m * piece : (m + 1) * piece, :]
+        weights_v[block + m * width : block + (m + 1) * width, :] = other.reshape(width, width)
     side = lax.axis_index("dom") & 1
     mine_at = pl.multiple_of(side * (half * width), width)
     other_at = pl.multiple_of((1 - side) * (half * width), width)
@@ -952,7 +946,7 @@
         features, send, bases_first, self_first, coef_first, bases_second, self_second, coef_second
     )
     incoming = lax.all_to_all(outgoing, "dom", split_axis=0, concat_axis=0, tiled=True)
-    local, remote, pooled, degree, ahead = build(
+    local, remote, pooled, degree = build(
         *edges, features, relations=relations, remote_rows=remote_rows
     )
     incoming, degree = lax.optimization_barrier((incoming, degree))
@@ -968,23 +962,17 @@
         for e in range(EACH)
     }
 
-    def widen(mask):
-        for (k, e), piece in sorted(pieces.items()):
-            pieces[k | mask, e] = from_peer(piece, mask)
-
-    mask = relations // EACH // 2
-    widen(mask)
-    mean = pool(remote, pooled, incoming, degree, ahead, relations=relations, slot=slot)
+    ways = relations // EACH
+    for k in range(2, ways, 2):
+        for e in range(EACH):
+            pieces[k, e] = from_peer(pieces[0, e], k)
+    mean = pool(remote, pooled, incoming, degree, relations=relations, slot=slot)
     pieces, mean = lax.optimization_barrier((pieces, mean))
-    mask //= 2
-    widen(mask)
     hidden, picked, self_next = middle(
         mean, features, incoming, swapped, bias_first[None], send, relations=relations
     )
     table = lax.all_to_all(picked, "dom", split_axis=0, concat_axis=0, tiled=True)
-    while mask > 1:
-        mask //= 2
-        widen(mask)
+    pieces.update({(k | 1, e): from_peer(piece, 1) for (k, e), piece in sorted(pieces.items())})
     pieces = [piece for _, piece in sorted(pieces.items())]
     partial, ahead = first(
         local, remote, hidden, degree, self_next, bias_second[None], pieces, relations=relations

time: 98.1 us -> 89.4 us (0.911)
  waiting for transfers between devices: 15.9 us -> 4.44 us
  Pallas kernels: 62 us -> 65.5 us
    ppermute x8, waiting for transfers between devices: 12.1 us -> 1.03 us  [from_peer(): return lax.ppermute(array, 'dom', [(i, i ^ mask) for i in range(devices)])]
    pallas_call x1, Pallas kernels: 26.9 us -> 29.7 us  [build(): pl.pallas_call(functools.partial(build_body, tiles=tiles, relations=relat...]
    all_to_all x1, waiting for transfers between devices: 3.78 us -> 0.97 us  [shards(): lax.all_to_all(outgoing, 'dom', split_axis=0, concat_axis=0, tiled=True)]
    all_to_all x1, waiting for transfers between devices: 0.01 us -> 2.44 us  [shards(): lax.all_to_all(picked, 'dom', split_axis=0, concat_axis=0, tiled=True)]
    all_to_all x1, starting transfers between devices: 6.06 us -> 4.65 us  [shards(): lax.all_to_all(picked, 'dom', split_axis=0, concat_axis=0, tiled=True)]
  transfers between devices with their start and end apart: 10 -> 10, of which waited for: 4 -> 6; matrix products, arithmetic and copies ran while one was open for 1% -> 1% of each run, Pallas kernels for 46% -> 55%
where the time goes in v7:
time: 89.4 us; the launch traced here: 89 us
  Pallas kernels  65.5 us (73%)
  starting transfers between devices  16.7 us (19%)
  waiting for transfers between devices  4.44 us (5%)
  local copies, waits for them, and re-layouts  1.33 us (1%)
  between operations  0.99 us (1%)
    pallas_call x1, Pallas kernels, build(): pl.pallas_call(functools.partial(build_body, tiles=tiles, relations=relat...  29.7 us
    pallas_call x1, Pallas kernels, first(): pl.pallas_call(functools.partial(first_body, relations=relations), out_sh...  10.2 us
    pallas_call x1, Pallas kernels, last(): pl.pallas_call(functools.partial(last_body, relations=relations), out_sha...  8.96 us
    pallas_call x1, Pallas kernels, pool(): pl.pallas_call(functools.partial(pool_body, relations=relations, slot=slo...  8.92 us
    all_to_all x1, starting transfers between devices, shards(): lax.all_to_all(outgoing, 'dom', split_axis=0, concat_axis=0, tiled=True)  7.33 us
    ppermute x8, starting transfers between devices, from_peer(): return lax.ppermute(array, 'dom', [(i, i ^ mask) for i in range(devices)])  4.71 us
    all_to_all x1, starting transfers between devices, shards(): lax.all_to_all(picked, 'dom', split_axis=0, concat_axis=0, tiled=True)  4.65 us
    pallas_call x1, Pallas kernels, middle(): pl.pallas_call(functools.partial(middle_body, relations=relations, slot=s...  4.32 us
  transfers between devices with their start and end apart: 10, of which 6 were waited for; matrix products, arithmetic and copies ran while one was open for 1% of the time, Pallas kernels for 55%

profile of v7, /device:TPU:0, one launch (start us, length us, event | category | flops | bytes accessed | tf_op | source)
XLA Modules:
  0.0 89.0 jit_solution(3065035771281147762)
XLA Ops:
  0.0 3.4 %pack.1 = bf16[32,80,256]{2,1,0:T(8,128)(2,1)} custom-call(f32[8,30]{1,0:T(8,128)} %refs_0_.1, f32[8,30]{1,0:T(8,128)} %refs_1_.1, bf16[30,8,256]{2,1,0:T(8,128)(2,1)} %refs_2_.1, bf16[30,8,256]{2,1,0:T(8,128)(2,1)} %refs_3_.1, bf16[8,256]{1,0:T(8,128)(2,1)} %refs_4_.1, bf16[8,256]{1,0:T(8,128)(2,1)} %refs_5_.1, bf16[1024,256]{1,0:T(8,128)(2,1)} %own_hbm.3, ...), custom_call_target="tpu_custom_call" | custom-call | flops 536870912 | tf_op jit(solution)/shard_map/pack/pallas_call | solution.py:823
  3.4 7.3 %all-to-all-start = ((bf16[32,80,256]{2,1,0:T(8,128)(2,1)}), bf16[32,80,256]{2,1,0:T(8,128)(2,1)S(1)}, u32[]{:S(2)}, u32[]{:S(2)}) async-start(bf16[32,80,256]{2,1,0:T(8,128)(2,1)} %pack.1), calls=%async_computation | async-start | bytes 2621440 | tf_op jit(solution)/shard_map/all_to_all | solution.py:948
  11.4 0.6 slice_reduce_fusion.tile_ref
  12.0 29.7 %build.1 = (bf16[8192,1024]{1,0:T(8,128)(2,1)}, bf16[8192,1024]{1,0:T(8,128)(2,1)}, bf16[8192,256]{1,0:T(8,128)(2,1)}, f32[8,128,8]{2,1,0:T(8,128)}) custom-call(s32[128]{0:T(128)} %slice_reduce_fusion.tile_ref, s32[1]{0:T(128)S(6)} %copy.15.count_ref, s32[128,128]{1,0:T(8,128)} %bitcast.15, s32[128,128]{1,0:T(8,128)} %bitcast.16, s32[128,128]{1,0:T(8,128)} %bitcast.12, ...), custom_call_target="tpu_custom_call" | custom-call | flops 17179869184 | bytes 33554432 | tf_op jit(solution)/shard_map/build/pallas_call | solution.py:407
  41.7 1.0 %all-to-all-done.incoming_ref = bf16[32,80,256]{2,1,0:T(8,128)(2,1)S(1)} async-done(((bf16[32,80,256]{2,1,0:T(8,128)(2,1)}), bf16[32,80,256]{2,1,0:T(8,128)(2,1)S(1)}, u32[]{:S(2)}, u32[]{:S(2)}) %all-to-all-start) | async-done | bytes 1310752 | tf_op jit(solution)/shard_map/all_to_all | solution.py:948
  42.7 0.1 collective-permute-start.3
  42.8 2.3 %collective-permute-start.2 = (bf16[256,256]{1,0:T(8,128)(2,1)S(1)}, bf16[256,256]{1,0:T(8,128)(2,1)S(1)}, u32[]{:S(2)}, u32[]{:S(2)}) collective-permute-start(bf16[256,256]{1,0:T(8,128)(2,1)S(1)} %slice_bitcast_fusion.refs_0_), channel_id=1, source_target_pairs={{0,6},{1,7},{2,4},{3,5},{4,2},{5,3},{6,0},{7,1},{8,14},{9,15},{10,... | collective-permute-start | bytes 393224 | tf_op jit(solution)/shard_map/ppermute | solution.py:955
  45.2 0.5 collective-permute-start.1
  45.7 0.7 collective-permute-start
  46.4 8.9 %pool.1.mean_ref = bf16[1024,2048]{1,0:T(8,128)(2,1)S(1)} custom-call(bf16[8192,1024]{1,0:T(8,128)(2,1)} %get-tuple-element.23.counts_ref.remote_ref, bf16[8192,256]{1,0:T(8,128)(2,1)} %get-tuple-element.26.pooled_ref, bf16[32,80,256]{2,1,0:T(8,128)(2,1)S(1)} %all-to-all-done.incoming_ref, f32[8,128,8]{2,1,0:T(8,128)} %get-tuple-element.27.degree_hbm), custom_call_target="tpu_custom_call" | custom-call | flops 4294967296 | bytes 16777216 | tf_op jit(solution)/shard_map/pool/pallas_call | solution.py:522
  55.3 0.0 collective-permute-done.2.refs_6_
  55.4 0.0 collective-permute-done.1.refs_4_
  55.4 0.0 collective-permute-done.refs_2_
  55.4 0.0 collective-permute-done.3.swapped_ref
  55.4 4.3 %middle.1 = (bf16[1024,256]{1,0:T(8,128)(2,1)}, bf16[32,32,256]{2,1,0:T(8,128)(2,1)}, bf16[256,256]{1,0:T(8,128)(2,1)}) custom-call(bf16[1024,2048]{1,0:T(8,128)(2,1)S(1)} %pool.1.mean_ref, bf16[1024,256]{1,0:T(8,128)(2,1)} %own_hbm.3, bf16[32,80,256]{2,1,0:T(8,128)(2,1)S(1)} %all-to-all-done.incoming_ref, ...), custom_call_target="tpu_custom_call" | custom-call | flops 1073741824 | tf_op jit(solution)/shard_map/middle/pallas_call | solution.py:624
  59.7 4.7 %all-to-all-start.1 = ((bf16[32,32,256]{2,1,0:T(8,128)(2,1)}), bf16[32,32,256]{2,1,0:T(8,128)(2,1)S(1)}, u32[]{:S(2)}, u32[]{:S(2)}) async-start(bf16[32,32,256]{2,1,0:T(8,128)(2,1)} %get-tuple-element.29), calls=%async_computation.1 | async-start | bytes 1048576 | tf_op jit(solution)/shard_map/all_to_all | solution.py:974
  64.4 0.0 copy-done
  64.4 0.1 collective-permute-start.4
  64.5 0.4 collective-permute-start.5
  65.0 0.1 collective-permute-start.6
  65.1 0.4 collective-permute-start.7
  65.5 0.3 collective-permute-done.4.refs_1_
  65.8 0.2 collective-permute-done.5.refs_3_
  66.0 0.3 collective-permute-done.6.refs_5_
  66.3 0.2 collective-permute-done.7.refs_7_
  66.5 0.0 copy-done.1
  66.5 0.1 copy-done.5
  66.7 0.3 copy-done.6
  67.0 0.2 copy-done.7
  67.2 10.2 %first.1 = (f32[1024,256]{1,0:T(8,128)}, bf16[1024,1024]{1,0:T(8,128)(2,1)S(1)}) custom-call(bf16[8192,1024]{1,0:T(8,128)(2,1)} %get-tuple-element.30.counts_ref, bf16[8192,1024]{1,0:T(8,128)(2,1)} %get-tuple-element.23.counts_ref.remote_ref, bf16[1024,256]{1,0:T(8,128)(2,1)} %get-tuple-element.31.own_hbm, f32[8,128,8]{2,1,0:T(8,128)} %get-tuple-element.27.degree_hbm, ...), custom_call_target="tpu_custom_call" | custom-call | flops 5368709120 | bytes 16777216 | tf_op jit(solution)/shard_map/first/pallas_call | solution.py:695
  77.4 2.4 %all-to-all-done.1 = bf16[32,32,256]{2,1,0:T(8,128)(2,1)S(1)} async-done(((bf16[32,32,256]{2,1,0:T(8,128)(2,1)}), bf16[32,32,256]{2,1,0:T(8,128)(2,1)S(1)}, u32[]{:S(2)}, u32[]{:S(2)}) %all-to-all-start.1) | async-done | bytes 524320 | tf_op jit(solution)/shard_map/all_to_all | solution.py:974
  79.8 9.0 %last.1 = bf16[1024,256]{1,0:T(8,128)(2,1)} custom-call(bf16[8192,1024]{1,0:T(8,128)(2,1)} %get-tuple-element.23.counts_ref.remote_ref, bf16[1024,256]{1,0:T(8,128)(2,1)S(1)} %bitcast.9, bf16[1024,1024]{1,0:T(8,128)(2,1)S(1)} %get-tuple-element.39.ahead_ref, f32[8,128,8]{2,1,0:T(8,128)} %get-tuple-element.27.degree_hbm, ...), custom_call_target="tpu_custom_call" | custom-call | flops 5368709120 | bytes 16777216 | tf_op jit(solution)/shard_map/last/pallas_call | solution.py:753
  (15 shorter events, 0.1 us)
Async XLA Ops:
  0.0 11.4 %copy-start.8 = (s32[1,128,128]{2,1,0:T(8,128)S(1)}, s32[1,128,128]{2,1,0:T(8,128)}, u32[]{:S(2)}) copy-start(s32[1,128,128]{2,1,0:T(8,128)} %param.17) | copy-start | bytes 196612
  3.4 39.3 %all-to-all-start = ((bf16[32,80,256]{2,1,0:T(8,128)(2,1)}), bf16[32,80,256]{2,1,0:T(8,128)(2,1)S(1)}, u32[]{:S(2)}, u32[]{:S(2)}) async-start(bf16[32,80,256]{2,1,0:T(8,128)(2,1)} %pack.1), calls=%async_computation | async-start | bytes 2621440 | tf_op jit(solution)/shard_map/all_to_all | solution.py:948
  42.7 12.7 %collective-permute-start.3 = (bf16[32,40,256]{2,1,0:T(8,128)(2,1)S(1)}, bf16[32,40,256]{2,1,0:T(8,128)(2,1)S(1)}, u32[]{:S(2)}, u32[]{:S(2)}) collective-permute-start(bf16[32,40,256]{2,1,0:T(8,128)(2,1)S(1)} %slice.11), channel_id=1, source_target_pairs={{0,1},{1,0},{2,3},{3,2},{4,5},{5,4},{6,7},{7,6},{8,9},{9,8},{10,11... | collective-permute-start | bytes 1966088 | tf_op jit(solution)/shard_map/ppermute | solution.py:955
  42.8 21.6 %copy-start = (bf16[256,256]{1,0:T(8,128)(2,1)}, bf16[256,256]{1,0:T(8,128)(2,1)S(1)}, u32[]{:S(2)}) copy-start(bf16[256,256]{1,0:T(8,128)(2,1)S(1)} %slice_bitcast_fusion.refs_0_) | copy-start | bytes 393220
  42.8 12.5 %collective-permute-start.2 = (bf16[256,256]{1,0:T(8,128)(2,1)S(1)}, bf16[256,256]{1,0:T(8,128)(2,1)S(1)}, u32[]{:S(2)}, u32[]{:S(2)}) collective-permute-start(bf16[256,256]{1,0:T(8,128)(2,1)S(1)} %slice_bitcast_fusion.refs_0_), channel_id=1, source_target_pairs={{0,6},{1,7},{2,4},{3,5},{4,2},{5,3},{6,0},{7,1},{8,14},{9,15},{10,... | collective-permute-start | bytes 393224 | tf_op jit(solution)/shard_map/ppermute | solution.py:955
  45.2 10.2 %collective-permute-start.1 = (bf16[256,256]{1,0:T(8,128)(2,1)S(1)}, bf16[256,256]{1,0:T(8,128)(2,1)S(1)}, u32[]{:S(2)}, u32[]{:S(2)}) collective-permute-start(bf16[256,256]{1,0:T(8,128)(2,1)S(1)} %slice_bitcast_fusion.refs_0_), channel_id=1, source_target_pairs={{0,4},{1,5},{2,6},{3,7},{4,0},{5,1},{6,2},{7,3},{8,12},{9,13},{10,... | collective-permute-start | bytes 393224 | tf_op jit(solution)/shard_map/ppermute | solution.py:955
  45.7 9.7 %collective-permute-start = (bf16[256,256]{1,0:T(8,128)(2,1)S(1)}, bf16[256,256]{1,0:T(8,128)(2,1)S(1)}, u32[]{:S(2)}, u32[]{:S(2)}) collective-permute-start(bf16[256,256]{1,0:T(8,128)(2,1)S(1)} %slice_bitcast_fusion.refs_0_), channel_id=1, source_target_pairs={{0,2},{1,3},{2,0},{3,1},{4,6},{5,7},{6,4},{7,5},{8,10},{9,11},{10,... | collective-permute-start | bytes 393224 | tf_op jit(solution)/shard_map/ppermute | solution.py:955
  55.3 11.2 %copy-start.1 = (bf16[256,256]{1,0:T(8,128)(2,1)}, bf16[256,256]{1,0:T(8,128)(2,1)S(1)}, u32[]{:S(2)}) copy-start(bf16[256,256]{1,0:T(8,128)(2,1)S(1)} %collective-permute-done.2.refs_6_) | copy-start | bytes 393220
  55.4 11.2 %copy-start.2 = (bf16[256,256]{1,0:T(8,128)(2,1)}, bf16[256,256]{1,0:T(8,128)(2,1)S(1)}, u32[]{:S(2)}) copy-start(bf16[256,256]{1,0:T(8,128)(2,1)S(1)} %collective-permute-done.1.refs_4_) | copy-start | bytes 393220
  55.4 11.1 %copy-start.3 = (bf16[256,256]{1,0:T(8,128)(2,1)}, bf16[256,256]{1,0:T(8,128)(2,1)S(1)}, u32[]{:S(2)}) copy-start(bf16[256,256]{1,0:T(8,128)(2,1)S(1)} %collective-permute-done.refs_2_) | copy-start | bytes 393220
  59.7 20.1 %all-to-all-start.1 = ((bf16[32,32,256]{2,1,0:T(8,128)(2,1)}), bf16[32,32,256]{2,1,0:T(8,128)(2,1)S(1)}, u32[]{:S(2)}, u32[]{:S(2)}) async-start(bf16[32,32,256]{2,1,0:T(8,128)(2,1)} %get-tuple-element.29), calls=%async_computation.1 | async-start | bytes 1048576 | tf_op jit(solution)/shard_map/all_to_all | solution.py:974
  64.4 1.4 %collective-permute-start.4 = (bf16[256,256]{1,0:T(8,128)(2,1)S(1)}, bf16[256,256]{1,0:T(8,128)(2,1)S(1)}, u32[]{:S(2)}, u32[]{:S(2)}) collective-permute-start(bf16[256,256]{1,0:T(8,128)(2,1)S(1)} %slice_bitcast_fusion.refs_0_), channel_id=1, source_target_pairs={{0,1},{1,0},{2,3},{3,2},{4,5},{5,4},{6,7},{7,6},{8,9},{9,8},{10,11... | collective-permute-start | bytes 393224 | tf_op jit(solution)/shard_map/ppermute | solution.py:955
  64.5 1.5 %collective-permute-start.5 = (bf16[256,256]{1,0:T(8,128)(2,1)S(1)}, bf16[256,256]{1,0:T(8,128)(2,1)S(1)}, u32[]{:S(2)}, u32[]{:S(2)}) collective-permute-start(bf16[256,256]{1,0:T(8,128)(2,1)S(1)} %collective-permute-done.refs_2_), channel_id=1, source_target_pairs={{0,1},{1,0},{2,3},{3,2},{4,5},{5,4},{6,7},{7,6},{8,9},{9,8},{10,11... | collective-permute-start | bytes 393224 | tf_op jit(solution)/shard_map/ppermute | solution.py:955
  65.0 1.3 %collective-permute-start.6 = (bf16[256,256]{1,0:T(8,128)(2,1)S(1)}, bf16[256,256]{1,0:T(8,128)(2,1)S(1)}, u32[]{:S(2)}, u32[]{:S(2)}) collective-permute-start(bf16[256,256]{1,0:T(8,128)(2,1)S(1)} %collective-permute-done.1.refs_4_), channel_id=1, source_target_pairs={{0,1},{1,0},{2,3},{3,2},{4,5},{5,4},{6,7},{7,6},{8,9},{9,8},{10,11... | collective-permute-start | bytes 393224 | tf_op jit(solution)/shard_map/ppermute | solution.py:955
  65.1 1.5 %collective-permute-start.7 = (bf16[256,256]{1,0:T(8,128)(2,1)S(1)}, bf16[256,256]{1,0:T(8,128)(2,1)S(1)}, u32[]{:S(2)}, u32[]{:S(2)}) collective-permute-start(bf16[256,256]{1,0:T(8,128)(2,1)S(1)} %collective-permute-done.2.refs_6_), channel_id=1, source_target_pairs={{0,1},{1,0},{2,3},{3,2},{4,5},{5,4},{6,7},{7,6},{8,9},{9,8},{10,11... | collective-permute-start | bytes 393224 | tf_op jit(solution)/shard_map/ppermute | solution.py:955
  65.8 0.7 copy-start.4
  66.0 0.6 copy-start.5
  66.3 0.7 copy-start.6
  66.5 0.6 copy-start.7
